TPU v7x, 32 devices: a whole 2x2x4 slice. The times are simulated.
32 devices in a mesh: parts: 2 (over y), seq: 4 (over z), head: 4 (over x, core).
Axes of the slice: x: 2, y: 2, z: 4, core: 2. Of those that a mesh axis runs over, the one named last changes fastest.
Arguments:
- queries: bfloat16 [256, 8192], P(('parts', 'seq'), 'head'), parts along dimension 0, may hold values from -110 to 110
- root_keys: bfloat16 [16384, 1024], P(('parts', 'seq'), 'head'), parts along dimension 0, may hold values from -6 to 6
- root_values: bfloat16 [16384, 1024], P(('parts', 'seq'), 'head'), parts along dimension 0, may hold values from -6 to 6
- branch_keys: bfloat16 [16, 2048, 1024], P(('parts', 'seq'), None, 'head'), parts along dimension 0, may hold values from -6 to 6
- branch_values: bfloat16 [16, 2048, 1024], P(('parts', 'seq'), None, 'head'), parts along dimension 0, may hold values from -6 to 6
- branch_id: int32 [256, 1], P('parts'), parts along dimension 0, may hold values from 0 to 7; in each aligned block of 128 rows (0 to 127, 128 to 255, ...) at most 32 rows name the same one
- doc_len: int32 [16], P('parts'), parts along dimension 0, may hold values from 1 to 2048, 10240 in all
Outputs:
- attended: bfloat16 [256, 8192], P(('parts', 'seq'), 'head'), parts along dimension 0
There are 2 independent parts, one for each index of `parts`. A program takes and returns all parts, laid end to end along the dimension named above; each array names one. Nothing has to cross between parts.
Inputs may be any that keep to these rules, and one draw needn't show every extreme that they name: `branch_id`: each of the 8 branches is named by at most 32 rows, a bound that some block reaches. `doc_len`: the 8 lengths of ONE part sum to 10240 and the largest of them is exactly 2048; the printed array holds all parts end to end, so its whole sum is that total times the number of parts.
All inputs are finite; a program needn't handle non-finite values.
Results may differ from a plain program's by a relative error of at most 0.008.
Values may be sent and summed in bfloat16 or wider, within the bound.
No kernel may reach another device: no remote copies, remote signals or barrier semaphores. Data moves between devices by JAX's collectives and lax.ppermute only.
A program may use at most 64 MiB of HBM per device.

v0:
```python
import jax
import jax.numpy as jnp
from jax import lax
from jax.sharding import PartitionSpec as P

QHEADS = 64
KVHEADS = 8
HEAD_DIM = 128


masked_score = -1e30


def attend(query_head_rows, key_tile_rows, value_tile_rows, usable):
    logit_scale = HEAD_DIM ** (-0.5)
    logit_scores = (
        jnp.einsum(
            "mfsa,nfa->mfsn", query_head_rows, key_tile_rows, preferred_element_type=jnp.float32
        )
        * logit_scale
    )
    keep = usable[:, None, None, :]
    logit_scores = jnp.where(keep, logit_scores, masked_score)
    row_max = jnp.max(logit_scores, axis=-1)
    softmax_weights = jnp.where(keep, jnp.exp(logit_scores - row_max[..., None]), 0.0)
    row_sum = jnp.sum(softmax_weights, axis=-1)
    weighted_values = jnp.einsum(
        "taoz,zah->taoh",
        softmax_weights.astype(jnp.bfloat16),
        value_tile_rows,
        preferred_element_type=jnp.float32,
    )
    return (row_max, row_sum, weighted_values)


def combine(first, second):
    row_max = jnp.maximum(first[0], second[0])
    factor_a = jnp.exp(first[0] - row_max)
    factor_b = jnp.exp(second[0] - row_max)
    return (
        row_max,
        first[1] * factor_a + second[1] * factor_b,
        first[2] * factor_a[..., None] + second[2] * factor_b[..., None],
    )


def body(queries, root_keys, root_values, branch_keys, branch_values, branch_id, doc_len):
    gathered = lax.all_gather(queries, "seq", axis=0, tiled=True)
    row_count = gathered.shape[0]
    kv_local = root_keys.shape[1] // HEAD_DIM
    group = QHEADS // KVHEADS
    query_head_rows = gathered.reshape(row_count, kv_local, group, HEAD_DIM)
    block_len = min(1024, root_keys.shape[0])
    block_count = root_keys.shape[0] // block_len
    key_blocks = root_keys.reshape(block_count, block_len, kv_local, HEAD_DIM)
    value_blocks = root_values.reshape(block_count, block_len, kv_local, HEAD_DIM)
    starts = (
        jnp.full((row_count, kv_local, group), masked_score, jnp.float32),
        jnp.zeros((row_count, kv_local, group), jnp.float32),
        jnp.zeros((row_count, kv_local, group, HEAD_DIM), jnp.float32),
    )

    def root_step(carry, pair):
        usable = jnp.ones((1, block_len), bool)
        return (combine(carry, attend(query_head_rows, pair[0], pair[1], usable)), None)

    root_part, _ = lax.scan(root_step, starts, (key_blocks, value_blocks))
    seq_count = lax.axis_size("seq")
    row_dev = row_count // seq_count
    branch_dev = branch_keys.shape[0]
    most_rows = 2 * row_dev // branch_dev
    branch_len = branch_keys.shape[1]
    branch_part = starts
    for local_branch in range(branch_dev):
        branch = lax.axis_index("seq") * branch_dev + local_branch
        chosen = jnp.argsort((branch_id[:, 0] != branch).astype(jnp.int32), stable=True)[:most_rows]
        row_live = branch_id[chosen, 0] == branch
        key_live = jnp.arange(branch_len) < doc_len[branch]
        usable = row_live[:, None] & key_live[None, :]
        key_tile_rows = branch_keys[local_branch].reshape(branch_len, kv_local, HEAD_DIM)
        value_tile_rows = branch_values[local_branch].reshape(branch_len, kv_local, HEAD_DIM)
        result = attend(query_head_rows[chosen], key_tile_rows, value_tile_rows, usable)
        target = jnp.where(row_live, chosen, row_count)
        branch_part = (
            branch_part[0].at[target].set(result[0], mode="drop"),
            branch_part[1].at[target].set(result[1], mode="drop"),
            branch_part[2].at[target].set(result[2], mode="drop"),
        )
    local_part = combine(root_part, branch_part)
    shares = (
        lax.all_to_all(local_part[0][None], "seq", split_axis=1, concat_axis=0, tiled=True),
        lax.all_to_all(local_part[1][None], "seq", split_axis=1, concat_axis=0, tiled=True),
        lax.all_to_all(local_part[2][None], "seq", split_axis=1, concat_axis=0, tiled=True),
    )
    row_max = jnp.max(shares[0], axis=0)
    factor = jnp.exp(shares[0] - row_max[None])
    row_sum = jnp.sum(shares[1] * factor, axis=0)
    weighted_values = jnp.sum(shares[2] * factor[..., None], axis=0)
    attended = weighted_values / row_sum[..., None]
    return attended.astype(jnp.bfloat16).reshape(row_dev, kv_local * group * HEAD_DIM)


def solution(mesh):
    in_specs = (
        P(("parts", "seq"), "head"),
        P(("parts", "seq"), "head"),
        P(("parts", "seq"), "head"),
        P(("parts", "seq"), None, "head"),
        P(("parts", "seq"), None, "head"),
        P("parts", None),
        P("parts"),
    )
    out_specs = P(("parts", "seq"), "head")
    return jax.shard_map(body, mesh=mesh, in_specs=in_specs, out_specs=out_specs, check_vma=False)
```

profile of v0, /device:TPU:0, one launch (start us, length us, event | category | flops | bytes accessed | tf_op | source)
XLA Modules:
  0.0 124.0 jit_solution(15404459378698408892)
XLA Ops:
  0.0 17.7 %all_gather.3 = bf16[128,2048]{1,0:T(8,128)(2,1)S(1)} all-gather(bf16[32,2048]{1,0:T(8,128)(2,1)} %param.9), channel_id=1, replica_groups=mesh['parts'=2,'seq'=4,'head'=4] {'seq'}, dimensions={0}, use_global_device_ids=true | all-gather | bytes 655360 | tf_op jit(solution)/shard_map/all_gather | solution.py:48
  19.4 2.5 %sort.31 = (s32[128]{0:T(128)}, s32[128]{0:T(128)S(1)}) sort(s32[128]{0:T(128)S(1)} %get-tuple-element.139, s32[128]{0:T(128)S(1)} %iota.17), dimensions={0}, to_apply=%region_4.5 | sort | flops 896 | bytes 2048 | tf_op jit(solution)/shard_map/jit(argsort)/sort | solution.py:76
  23.3 2.5 %sort.32 = (s32[128]{0:T(128)}, s32[128]{0:T(128)S(1)}) sort(s32[128]{0:T(128)S(1)} %get-tuple-element.138, s32[128]{0:T(128)S(1)} %iota.19), dimensions={0}, to_apply=%region_7.8 | sort | flops 896 | bytes 2048 | tf_op jit(solution)/shard_map/jit(argsort)/sort | solution.py:76
  31.9 2.2 %reshape.114 = bf16[2,1024,2,128]{3,2,1,0:T(2,128)(2,1)} reshape(bf16[2048,256]{1,0:T(8,128)(2,1)} %param.11) | data formatting | bytes 2097152 | tf_op jit(solution)/shard_map/reshape | solution.py:56
  34.1 13.9 %while.15 = (s32[]{:T(128)}, f32[128,2,8]{0,2,1:T(8,128)S(1)}, f32[128,2,8]{0,2,1:T(8,128)S(1)}, f32[128,2,8,128]{0,3,2,1:T(8,128)S(1)}, bf16[2,1024,2,128]{3,2,...) while((s32[]{:T(128)}, f32[128,2,8]{0,2,1:T(8,128)S(1)}, ...), condition=%wide.region_3.4_spmd.clone, body=%wide.region_0.3_spmd.clone.sunk | while | flops 1091579904 | bytes 32096368 | solution.py:67
  34.1 1.9 %constant_dynamic-slice_fusion.3 = (bf16[1,1024,2,128]{3,2,1,0:T(2,128)(2,1)S(1)}, bf16[1,1024,2,128]{3,2,1,0:T(2,128)(2,1)S(1)}) fusion(bf16[2,1024,2,128]{3,2,1,0:T(2,128)(2,1)} %get-tuple-element.227, s32[]{:T(128)S(6)} %copy.152, bf16[2,1024,2,128]{3,2,1,0:T(2,128)(2,1)} %get-tuple-element.225), kind=kLoop, calls=%fused_computation.30.clone.1 | loop fusion | bytes 2097156 | tf_op jit(solution)/shard_map/while/body/jit(dynamic_index_in_dim)/dynamic_slice | solution.py:67
  39.1 1.9 %fusion.73 = f32[128,2,8,128]{0,3,2,1:T(8,128)S(1)} fusion(f32[2,1024,128,8]{2,1,3,0:T(8,128)S(1)} %get-tuple-element.196, f32[128,2,8]{0,2,1:T(8,128)S(1)} %get-tuple-element.197, f32[128,2,8,128]{0,3,2,1:T(8,128)S(1)} %get-tuple-element.215, bf16[1,1024,2,128]{1,3,2,0:T(8,128)(2,1)S(1)} %copy.145, f32[128,2,8]{0,2,1:T(8,128)S(1)} %get-tuple-element.201, ...), kind=kOutput, calls=%fused_computation.20.clone.1 | convolution fusion | flops 544210944 | bytes 11034625 | tf_op jit(solution)/shard_map/while/body/eval_jaxpr/taoz,zah->taoh/dot_general | solution.py:27
  41.0 1.9 %constant_dynamic-slice_fusion.3 = (bf16[1,1024,2,128]{3,2,1,0:T(2,128)(2,1)S(1)}, bf16[1,1024,2,128]{3,2,1,0:T(2,128)(2,1)S(1)}) fusion(bf16[2,1024,2,128]{3,2,1,0:T(2,128)(2,1)} %get-tuple-element.227, s32[]{:T(128)S(6)} %copy.152, bf16[2,1024,2,128]{3,2,1,0:T(2,128)(2,1)} %get-tuple-element.225), kind=kLoop, calls=%fused_computation.30.clone.1 | loop fusion | bytes 2097156 | tf_op jit(solution)/shard_map/while/body/jit(dynamic_index_in_dim)/dynamic_slice | solution.py:67
  46.1 1.9 %fusion.73 = f32[128,2,8,128]{0,3,2,1:T(8,128)S(1)} fusion(f32[2,1024,128,8]{2,1,3,0:T(8,128)S(1)} %get-tuple-element.196, f32[128,2,8]{0,2,1:T(8,128)S(1)} %get-tuple-element.197, f32[128,2,8,128]{0,3,2,1:T(8,128)S(1)} %get-tuple-element.215, bf16[1,1024,2,128]{1,3,2,0:T(8,128)(2,1)S(1)} %copy.145, f32[128,2,8]{0,2,1:T(8,128)S(1)} %get-tuple-element.201, ...), kind=kOutput, calls=%fused_computation.20.clone.1 | convolution fusion | flops 544210944 | bytes 11034625 | tf_op jit(solution)/shard_map/while/body/eval_jaxpr/taoz,zah->taoh/dot_general | solution.py:27
  48.0 2.7 %fusion.54 = (bf16[1,2048,256]{2,1,0:T(8,128)(2,1)S(1)}, bf16[1,2048,256]{2,1,0:T(8,128)(2,1)}) fusion(bf16[2,2048,256]{2,1,0:T(8,128)(2,1)} %param.12), kind=kLoop, calls=%fused_computation.93 | loop fusion | bytes 4194304 | tf_op jit(solution)/shard_map/slice | solution.py:80
  57.1 1.9 %copy-done.2 = f32[2,32,8,2048]{3,2,1,0:T(8,128)} copy-done((f32[2,32,8,2048]{3,2,1,0:T(8,128)}, f32[2,32,8,2048]{3,2,1,0:T(8,128)S(1)}, u32[]{:S(2)}) %copy-start.2) | copy-done | bytes 4194328
  60.6 1.5 %scatter_fusion = f32[128,2,8]{2,1,0:T(2,128)S(1)} fusion(f32[128,2,8]{2,1,0:T(2,128)S(1)} %broadcast_in_dim.99, s32[32]{0:T(128)S(1)} %copy-done.10, f32[32,2,8]{2,1,0:T(2,128)S(1)} %copy.83), kind=kCustom, calls=%fused_computation.4 | custom fusion | bytes 6272 | tf_op jit(solution)/shard_map/scatter | solution.py:85
  62.2 1.7 %scatter_fusion.1 = f32[128,2,8]{2,1,0:T(2,128)S(1)} fusion(f32[128,2,8]{2,1,0:T(2,128)S(1)} %scatter_fusion, s32[32]{0:T(128)S(1)} %copy-done.12, f32[32,2,8]{2,1,0:T(2,128)S(1)} %copy.88), kind=kCustom, calls=%fused_computation.5 | custom fusion | bytes 6272 | tf_op jit(solution)/shard_map/scatter | solution.py:85
  65.6 1.6 %scatter_fusion.5 = f32[128,2,8]{2,1,0:T(2,128)S(1)} fusion(f32[128,2,8]{2,1,0:T(2,128)S(1)} %scatter_fusion.4, s32[32]{0:T(128)S(1)} %copy-done.12, f32[32,2,8]{2,1,0:T(2,128)S(1)} %copy.103), kind=kCustom, calls=%fused_computation.9 | custom fusion | bytes 6272 | tf_op jit(solution)/shard_map/scatter | solution.py:86
  68.2 5.4 %all-to-all-start.2 = ((f32[4,1,512]{2,1,0:T(1,128)}), f32[4,1,512]{2,1,0:T(1,128)S(1)}, u32[]{:S(2)}, u32[]{:S(2)}) async-start(f32[4,1,512]{2,1,0:T(1,128)} %reshape.221), calls=%async_computation.2 | async-start | bytes 16384 | tf_op jit(solution)/shard_map/all_to_all | solution.py:92
  73.6 1.7 %fusion.55 = (bf16[1,2048,256]{2,1,0:T(8,128)(2,1)S(1)}, bf16[1,2048,256]{2,1,0:T(8,128)(2,1)S(1)}) fusion(bf16[2,2048,256]{2,1,0:T(8,128)(2,1)} %param.13), kind=kLoop, calls=%fused_computation.94 | loop fusion | bytes 4194304 | tf_op jit(solution)/shard_map/slice | solution.py:81
  77.5 4.1 %fusion.36 = f32[32,2,8,128]{3,2,0,1:T(8,128)} fusion(bf16[2048,2,128,1]{0,2,3,1:T(8,128)(2,1)S(1)} %bitcast.148, f32[2,32,8,2048]{3,2,1,0:T(8,128)} %copy-done.1, f32[32,2,8]{2,0,1:T(8,128)S(1)} %copy-done.7, pred[32,2048]{1,0:T(8,128)(4,1)S(1)} %broadcast_and_fusion.1), kind=kOutput, calls=%fused_computation.53 | convolution fusion | flops 273678336 | bytes 5572608 | tf_op jit(solution)/shard_map/taoz,zah->taoh/dot_general | solution.py:27
  84.8 1.5 %scatter_fusion.2 = f32[128,2,8,128]{3,2,1,0:T(8,128)S(1)} fusion(f32[128,2,8,128]{3,2,1,0:T(8,128)S(1)} %broadcast_in_dim.101, s32[32]{0:T(128)S(1)} %copy-done.11, f32[32,2,8,128]{3,2,1,0:T(8,128)S(1)} %copy.94), kind=kCustom, calls=%fused_computation.6 | custom fusion | bytes 786560 | tf_op jit(solution)/shard_map/scatter | solution.py:87
  86.3 1.6 %scatter_fusion.3 = f32[128,2,8,128]{3,2,1,0:T(8,128)S(1)} fusion(f32[128,2,8,128]{3,2,1,0:T(8,128)S(1)} %scatter_fusion.2, s32[32]{0:T(128)S(1)} %copy-done.13, f32[32,2,8,128]{3,2,1,0:T(8,128)S(1)} %copy.97), kind=kCustom, calls=%fused_computation.7 | custom fusion | bytes 786560 | tf_op jit(solution)/shard_map/scatter | solution.py:87
  87.9 5.1 %all-to-all-start.1 = ((f32[4,1,512]{2,1,0:T(1,128)}), f32[4,1,512]{2,1,0:T(1,128)S(1)}, u32[]{:S(2)}, u32[]{:S(2)}) async-start(f32[4,1,512]{2,1,0:T(1,128)} %reshape.219), calls=%async_computation.1 | async-start | bytes 16384 | tf_op jit(solution)/shard_map/all_to_all | solution.py:91
  93.0 1.6 %add_bitcast_fusion = f32[1,128,2,8,128]{4,3,2,0,1:T(8,128)} fusion(f32[128,2,8,128]{3,2,1,0:T(8,128)S(1)} %scatter_fusion.3, f32[128,2,8,128]{3,2,1,0:T(8,128)S(1)} %copy.91, f32[128,2,8]{2,1,0:T(2,128)S(1)} %copy.99, f32[128,2,8]{2,1,0:T(2,128)S(1)} %copy.90), kind=kLoop, calls=%fused_computation.56 | loop fusion | flops 786432 | bytes 3162112 | tf_op jit(solution)/shard_map/broadcast_in_dim | solution.py:93
  94.6 4.0 %all-to-all-done.1 = f32[4,1,512]{2,1,0:T(1,128)S(1)} async-done(((f32[4,1,512]{2,1,0:T(1,128)}), f32[4,1,512]{2,1,0:T(1,128)S(1)}, u32[]{:S(2)}, u32[]{:S(2)}) %all-to-all-start.1) | async-done | bytes 8224 | tf_op jit(solution)/shard_map/all_to_all | solution.py:91
  98.6 3.5 %all-to-all-start = ((f32[1,128,2,8,128]{4,3,2,0,1:T(8,128)}), f32[1,128,2,8,128]{4,3,2,0,1:T(8,128)S(1)}, u32[]{:S(2)}, u32[]{:S(2)}) async-start(f32[1,128,2,8,128]{4,3,2,0,1:T(8,128)} %add_bitcast_fusion), calls=%async_computation | async-start | bytes 2097152 | tf_op jit(solution)/shard_map/all_to_all | solution.py:93
  104.7 18.1 %all-to-all-done = f32[1,128,2,8,128]{4,3,2,0,1:T(8,128)S(1)} async-done(((f32[1,128,2,8,128]{4,3,2,0,1:T(8,128)}), f32[1,128,2,8,128]{4,3,2,0,1:T(8,128)S(1)}, u32[]{:S(2)}, u32[]{:S(2)}) %all-to-all-start) | async-done | bytes 1048608 | tf_op jit(solution)/shard_map/all_to_all | solution.py:93
  (104 shorter events, 34.6 us)
Async XLA Ops:
  0.0 22.0 %copy-start = (s32[128,1]{0,1:T(1,128)S(1)}, s32[128,1]{0,1:T(1,128)}, u32[]{:S(2)}) copy-start(s32[128,1]{0,1:T(1,128)} %param.14) | copy-start | bytes 1540
  0.0 27.1 %copy-start.15 = (s32[8]{0:T(128)S(1)}, s32[8]{0:T(128)}, u32[]{:S(2)}) copy-start(s32[8]{0:T(128)} %param.15) | copy-start | bytes 100
  0.0 30.7 %copy-start.4 = (bf16[2048,256]{1,0:T(8,128)(2,1)S(1)}, bf16[2048,256]{1,0:T(8,128)(2,1)}, u32[]{:S(2)}) copy-start(bf16[2048,256]{1,0:T(8,128)(2,1)} %param.10) | copy-start | bytes 3145732
  52.9 2.8 %copy-start.9 = (pred[2048]{0:T(1024)(128)(4,1)S(1)}, pred[2048]{0:T(1024)(128)(4,1)}, u32[]{:S(2)}) copy-start(pred[2048]{0:T(1024)(128)(4,1)} %iota_compare_fusion) | copy-start | bytes 6148
  52.9 2.8 %copy-start.14 = (pred[32]{0:T(512)(128)(4,1)S(1)}, pred[32]{0:T(512)(128)(4,1)}, u32[]{:S(2)}) copy-start(pred[32]{0:T(512)(128)(4,1)} %get-tuple-element.120) | copy-start | bytes 100
  54.1 1.6 %copy-start.6 = (f32[32,2,8]{2,0,1:T(8,128)}, f32[32,2,8]{2,0,1:T(8,128)S(1)}, u32[]{:S(2)}) copy-start(f32[32,2,8]{2,0,1:T(8,128)S(1)} %get-tuple-element.140) | copy-start | bytes 6148
  54.1 3.0 %copy-start.1 = (f32[2,32,8,2048]{3,2,1,0:T(8,128)}, f32[2,32,8,2048]{3,2,1,0:T(8,128)S(1)}, u32[]{:S(2)}) copy-start(f32[2,32,8,2048]{3,2,1,0:T(8,128)S(1)} %get-tuple-element.141) | copy-start | bytes 12582916
  55.9 4.8 %copy-start.10 = (s32[32]{0:T(128)S(1)}, s32[32]{0:T(128)}, u32[]{:S(2)}) copy-start(s32[32]{0:T(128)} %get-tuple-element.123) | copy-start | bytes 388
  55.9 6.3 %copy-start.12 = (s32[32]{0:T(128)S(1)}, s32[32]{0:T(128)}, u32[]{:S(2)}) copy-start(s32[32]{0:T(128)} %get-tuple-element.119) | copy-start | bytes 388
  57.1 2.0 %copy-start.2 = (f32[2,32,8,2048]{3,2,1,0:T(8,128)}, f32[2,32,8,2048]{3,2,1,0:T(8,128)S(1)}, u32[]{:S(2)}) copy-start(f32[2,32,8,2048]{3,2,1,0:T(8,128)S(1)} %get-tuple-element.143) | copy-start | bytes 12582916
  68.2 19.6 %all-to-all-start.2 = ((f32[4,1,512]{2,1,0:T(1,128)}), f32[4,1,512]{2,1,0:T(1,128)S(1)}, u32[]{:S(2)}, u32[]{:S(2)}) async-start(f32[4,1,512]{2,1,0:T(1,128)} %reshape.221), calls=%async_computation.2 | async-start | bytes 16384 | tf_op jit(solution)/shard_map/all_to_all | solution.py:92
  73.6 3.8 %copy-start.7 = (f32[32,2,8]{2,0,1:T(8,128)S(1)}, f32[32,2,8]{2,0,1:T(8,128)}, u32[]{:S(2)}) copy-start(f32[32,2,8]{2,0,1:T(8,128)} %copy-done.6) | copy-start | bytes 6148
  77.5 4.2 %copy-start.3 = (f32[2,32,8,2048]{3,2,1,0:T(8,128)S(1)}, f32[2,32,8,2048]{3,2,1,0:T(8,128)}, u32[]{:S(2)}) copy-start(f32[2,32,8,2048]{3,2,1,0:T(8,128)} %copy-done.2) | copy-start | bytes 12582916
  77.5 4.2 %copy-start.5 = (bf16[1,2048,256]{1,2,0:T(8,128)(2,1)S(1)}, bf16[1,2048,256]{1,2,0:T(8,128)(2,1)}, u32[]{:S(2)}) copy-start(bf16[1,2048,256]{1,2,0:T(8,128)(2,1)} %copy.126) | copy-start | bytes 3145732
  81.6 1.7 %copy-start.8 = (f32[32,2,8,128]{3,2,0,1:T(8,128)S(1)}, f32[32,2,8,128]{3,2,0,1:T(8,128)}, u32[]{:S(2)}) copy-start(f32[32,2,8,128]{3,2,0,1:T(8,128)} %fusion.36) | copy-start | bytes 786436
  82.8 1.9 %copy-start.11 = (s32[32]{0:T(128)S(1)}, s32[32]{0:T(128)}, u32[]{:S(2)}) copy-start(s32[32]{0:T(128)} %get-tuple-element.123) | copy-start | bytes 388
  82.8 3.5 %copy-start.13 = (s32[32]{0:T(128)S(1)}, s32[32]{0:T(128)}, u32[]{:S(2)}) copy-start(s32[32]{0:T(128)} %get-tuple-element.119) | copy-start | bytes 388
  87.9 10.7 %all-to-all-start.1 = ((f32[4,1,512]{2,1,0:T(1,128)}), f32[4,1,512]{2,1,0:T(1,128)S(1)}, u32[]{:S(2)}, u32[]{:S(2)}) async-start(f32[4,1,512]{2,1,0:T(1,128)} %reshape.219), calls=%async_computation.1 | async-start | bytes 16384 | tf_op jit(solution)/shard_map/all_to_all | solution.py:91
  98.6 24.2 %all-to-all-start = ((f32[1,128,2,8,128]{4,3,2,0,1:T(8,128)}), f32[1,128,2,8,128]{4,3,2,0,1:T(8,128)S(1)}, u32[]{:S(2)}, u32[]{:S(2)}) async-start(f32[1,128,2,8,128]{4,3,2,0,1:T(8,128)} %add_bitcast_fusion), calls=%async_computation | async-start | bytes 2097152 | tf_op jit(solution)/shard_map/all_to_all | solution.py:93
where the time goes:
time: 125 us; the launch traced here: 124 us
  local copies, waits for them, and re-layouts  37 us (30%)
  waiting for transfers between devices  22.1 us (18%)
  other arithmetic  18.4 us (15%)
  blocking collectives  17.7 us (14%)
  matrix products  14 us (11%)
  starting transfers between devices  14 us (11%)
    all_to_all x1, waiting for transfers between devices, body(): lax.all_to_all(local_part[2][None], 'seq', split_axis=1, concat_axis=0, t...  18.1 us
    all_gather x1, blocking collectives, body(): gathered = lax.all_gather(queries, 'seq', axis=0, tiled=True)  17.7 us
    unnamed x42, local copies, waits for them, and re-layouts  9.32 us
    dot_general x4, matrix products, attend(): jnp.einsum('taoz,zah->taoh', softmax_weights.astype(jnp.bfloat16), value_...  9.15 us
    reduce_sum x4, other arithmetic, attend(): row_sum = jnp.sum(softmax_weights, axis=-1)  5.79 us
    all_to_all x1, starting transfers between devices, body(): lax.all_to_all(local_part[1][None], 'seq', split_axis=1, concat_axis=0, t...  5.38 us
    all_to_all x1, starting transfers between devices, body(): lax.all_to_all(local_part[0][None], 'seq', split_axis=1, concat_axis=0, t...  5.1 us
    sort x2, other arithmetic, body(): jnp.argsort((branch_id[:, 0] != branch).astype(jnp.int32), stable=True)  5.07 us
  transfers between devices with their start and end apart: 3, of which 2 were waited for; matrix products, arithmetic and copies ran while one was open for 15% of the time, Pallas kernels for 0%

commit v1 on v0

v1 whole, which is shorter than its diff:
```python
import functools
import math

import jax
import jax.numpy as jnp
from jax import lax
from jax.experimental import pallas as pl
from jax.experimental.pallas import tpu as pltpu
from jax.sharding import PartitionSpec as P

QHEADS = 64
KVHEADS = 8
HEAD_DIM = 128
GROUP = QHEADS // KVHEADS
LOW = -1.0e30
SCALE = HEAD_DIM ** -0.5 * math.log2(math.e)
STAT = 16


def dot(a, b, dims=(((1,), (0,)), ((), ()))):
    return lax.dot_general(a, b, dims, preferred_element_type=jnp.float32)


def pieces(x):
    hi = x.astype(jnp.bfloat16)
    rest = x - hi.astype(jnp.float32)
    mid = rest.astype(jnp.bfloat16)
    low = (rest - mid.astype(jnp.float32)).astype(jnp.bfloat16)
    return hi, mid, low


def attend(query, keys, values, score_ref, weight_ref, bias=None):
    rows = query.shape[0]
    total = score_ref.shape[1]
    tile = 256
    best = None
    for j in range(total // tile):
        s = dot(query, keys(j, tile), (((1,), (1,)), ((), ())))
        if bias is not None:
            s = s + bias(j, tile)
        score_ref[:, j * tile:(j + 1) * tile] = s
        for part in range(tile // HEAD_DIM):
            t = s[:, part * HEAD_DIM:(part + 1) * HEAD_DIM]
            best = t if best is None else jnp.maximum(best, t)
    peak = jnp.broadcast_to(jnp.max(best, axis=1, keepdims=True) * SCALE, (rows, HEAD_DIM))
    peak2 = jnp.concatenate([peak, peak], axis=1)
    for j in range(total // tile):
        w = jnp.exp2(score_ref[:, j * tile:(j + 1) * tile] * SCALE - peak2)
        weight_ref[:, j * tile:(j + 1) * tile] = w.astype(jnp.bfloat16)
    tiles = [jnp.concatenate([values(j, tile), jnp.ones((tile, HEAD_DIM), jnp.bfloat16)], axis=1) for j in range(total // tile)]
    out = dot(weight_ref[...], jnp.concatenate(tiles, axis=0))
    denominator = out[:, HEAD_DIM:]
    return out[:, :HEAD_DIM] / denominator, peak + jnp.log2(denominator)


def stack_heads(chunk, f):
    at = f * GROUP
    return jnp.concatenate([chunk[:, (at + h) * HEAD_DIM:(at + h + 1) * HEAD_DIM] for h in range(GROUP)], axis=0)


def write_share(out_ref, first, f, output, level, row_dev, heads):
    out_ref[first + f * GROUP * row_dev:first + (f + 1) * GROUP * row_dev, :] = output.astype(jnp.bfloat16)
    lane = lax.broadcasted_iota(jnp.int32, (row_dev, HEAD_DIM), 1)
    stat = jnp.zeros((row_dev, HEAD_DIM), jnp.float32)
    for h in range(GROUP):
        stat = jnp.where(lane % heads == f * GROUP + h, level[h * row_dev:(h + 1) * row_dev, :], stat)
    return stat


def write_stats(out_ref, first, stat, row_dev, heads):
    lane = lax.broadcasted_iota(jnp.int32, (row_dev, HEAD_DIM), 1)
    hi, mid, low = pieces(stat)
    zero = jnp.zeros_like(stat)
    packed = jnp.where(lane < heads, hi.astype(jnp.float32), jnp.where(lane < 2 * heads, mid.astype(jnp.float32), jnp.where(lane < 3 * heads, low.astype(jnp.float32), zero)))
    half = row_dev // 2
    both = packed[:half] + pltpu.roll(packed[half:], HEAD_DIM // 2, 1)
    out_ref[first + heads * row_dev:first + heads * row_dev + half, :] = both.astype(jnp.bfloat16)


def work(me_ref, doc_ref, id_ref, rk_ref, rv_ref, bk_ref, bv_ref, *rest, shares, kv_local, most_rows):
    q_refs = rest[:shares]
    out_refs = rest[shares:2 * shares]
    score_ref, weight_ref, pick_ref, level_ref, branch_ref = rest[2 * shares:]
    row_dev = q_refs[0].shape[0]
    rows = id_ref.shape[0]
    branch_dev = bk_ref.shape[0]
    heads = kv_local * GROUP
    me = me_ref[0]

    ids = id_ref[...]
    before = (lax.broadcasted_iota(jnp.int32, (rows, rows), 0) > lax.broadcasted_iota(jnp.int32, (rows, rows), 1)).astype(jnp.bfloat16)
    for b in range(branch_dev):
        named = ids == me * branch_dev + b
        named_wide = jnp.broadcast_to(named.astype(jnp.float32), (rows, HEAD_DIM))
        rank = dot(before, named_wide.astype(jnp.bfloat16))[:, :most_rows]
        slot = lax.broadcasted_iota(jnp.int32, (rows, most_rows), 1).astype(jnp.float32)
        chosen = jnp.where((rank == slot) & (named_wide[:, :most_rows] > 0.0), 1.0, 0.0)
        pick_ref[b] = chosen.astype(jnp.bfloat16)

    for f in range(kv_local):
        cut = slice(f * HEAD_DIM, (f + 1) * HEAD_DIM)
        wide = slice(f * GROUP * HEAD_DIM, (f + 1) * GROUP * HEAD_DIM)
        for b in range(branch_dev):
            picked = None
            for k in range(shares):
                source = lax.rem(me - k + shares, shares)
                sel = pick_ref[b, pl.ds(pl.multiple_of(source * row_dev, row_dev), row_dev), :]
                part = dot(sel, q_refs[k][:, wide], (((0,), (0,)), ((), ())))
                picked = part if picked is None else picked + part
            query = stack_heads(picked.astype(jnp.bfloat16), 0)
            length = doc_ref[me * branch_dev + b]

            def bias(j, tile):
                slot = lax.broadcasted_iota(jnp.int32, (1, tile), 1) + j * tile
                return jnp.where(slot < length, 0.0, LOW)

            output, level = attend(query, lambda j, t: bk_ref[b, j * t:(j + 1) * t, cut], lambda j, t: bv_ref[b, j * t:(j + 1) * t, cut], score_ref, weight_ref, bias)
            for h in range(GROUP):
                at = slice(h * most_rows, (h + 1) * most_rows)
                to = slice((f * GROUP + h) * HEAD_DIM, (f * GROUP + h + 1) * HEAD_DIM)
                branch_ref[b * most_rows:(b + 1) * most_rows, to] = output[at]
                level_ref[b * most_rows:(b + 1) * most_rows, to] = level[at]

    for k in range(shares):
        source = lax.rem(me - k + shares, shares)
        at = pl.ds(pl.multiple_of(source * row_dev, row_dev), row_dev)
        pick = jnp.concatenate([pick_ref[b, at, :] for b in range(branch_dev)], axis=1)
        has = jnp.sum(pick.astype(jnp.float32), axis=1, keepdims=True) > 0.0
        stat = None
        for f in range(kv_local):
            cut = slice(f * HEAD_DIM, (f + 1) * HEAD_DIM)
            wide = slice(f * GROUP * HEAD_DIM, (f + 1) * GROUP * HEAD_DIM)
            query = stack_heads(q_refs[k], f)
            output, level = attend(query, lambda j, t: rk_ref[j * t:(j + 1) * t, cut], lambda j, t: rv_ref[j * t:(j + 1) * t, cut], score_ref, weight_ref)
            b_out = sum(dot(pick, p) for p in pieces(branch_ref[:, wide])[:2])
            b_level = sum(dot(pick, p) for p in pieces(level_ref[:, wide]))
            b_level = jnp.where(has, b_level, LOW)
            b_out, b_level = stack_heads(b_out, 0), stack_heads(b_level, 0)
            top = jnp.maximum(level, b_level)
            ours, theirs = jnp.exp2(level - top), jnp.exp2(b_level - top)
            both = ours + theirs
            merged = (output * ours + b_out * theirs) / both
            here = write_share(out_refs[k], 0, f, merged, top + jnp.log2(both), row_dev, heads)
            stat = here if stat is None else stat + here
        write_stats(out_refs[k], 0, stat, row_dev, heads)


def join(*refs, heads):
    share_refs, out_ref = refs[:-1], refs[-1]
    row_dev = out_ref.shape[0]
    half = row_dev // 2
    levels = []
    for ref in share_refs:
        s = ref[heads * row_dev:heads * row_dev + half, :].astype(jnp.float32)
        levels.append(s + pltpu.roll(s, HEAD_DIM - heads, 1) + pltpu.roll(s, HEAD_DIM - 2 * heads, 1))
    top = functools.reduce(jnp.maximum, levels)
    parts = [jnp.exp2(x - top) for x in levels]
    whole = functools.reduce(jnp.add, parts)
    parts = [x / whole for x in parts]
    for h in range(heads):
        result = None
        for ref, part in zip(share_refs, parts):
            factor = jnp.concatenate([jnp.broadcast_to(part[:, at:at + 1], (half, HEAD_DIM)) for at in (h, HEAD_DIM // 2 + h)], axis=0)
            term = ref[h * row_dev:(h + 1) * row_dev, :].astype(jnp.float32) * factor
            result = term if result is None else result + term
        out_ref[:, h * HEAD_DIM:(h + 1) * HEAD_DIM] = result.astype(jnp.bfloat16)


VMEM = pl.BlockSpec(memory_space=pltpu.VMEM)
SMEM = pl.BlockSpec(memory_space=pltpu.SMEM)


def body(queries, root_keys, root_values, branch_keys, branch_values, branch_id, doc_len):
    shares = lax.axis_size("seq")
    me = lax.axis_index("seq").astype(jnp.int32)
    row_dev, width = queries.shape
    heads = width // HEAD_DIM
    kv_local = root_keys.shape[1] // HEAD_DIM
    branch_dev, branch_len, _ = branch_keys.shape
    most_rows = 2 * row_dev // branch_dev

    def shift(x, k):
        return lax.ppermute(x, "seq", [(i, (i + k) % shares) for i in range(shares)])

    gathered = [queries] + [shift(queries, k) for k in range(1, shares)]
    share_shape = jax.ShapeDtypeStruct((heads * row_dev + row_dev // 2, HEAD_DIM), jnp.bfloat16)
    block = GROUP * row_dev
    sent = pl.pallas_call(
        functools.partial(work, shares=shares, kv_local=kv_local, most_rows=most_rows),
        out_shape=[share_shape] * shares,
        in_specs=[SMEM, SMEM] + [VMEM] * (5 + shares),
        out_specs=[VMEM] * shares,
        scratch_shapes=[
            pltpu.VMEM((block, root_keys.shape[0]), jnp.float32),
            pltpu.VMEM((block, root_keys.shape[0]), jnp.bfloat16),
            pltpu.VMEM((branch_dev, branch_id.shape[0], most_rows), jnp.bfloat16),
            pltpu.VMEM((branch_dev * most_rows, width), jnp.float32),
            pltpu.VMEM((branch_dev * most_rows, width), jnp.float32),
        ],
        name="work",
    )(me[None], doc_len, branch_id, root_keys, root_values, branch_keys, branch_values, *gathered)
    received = [sent[0]] + [shift(sent[k], shares - k) for k in range(1, shares)]
    return pl.pallas_call(
        functools.partial(join, heads=heads),
        out_shape=jax.ShapeDtypeStruct((row_dev, width), jnp.bfloat16),
        in_specs=[VMEM] * shares,
        out_specs=VMEM,
        name="join",
    )(*received)


def solution(mesh):
    rows = P(("parts", "seq"), "head")
    in_specs = (
        rows,
        rows,
        rows,
        P(("parts", "seq"), None, "head"),
        P(("parts", "seq"), None, "head"),
        P("parts", None),
        P("parts"),
    )
    return jax.shard_map(body, mesh=mesh, in_specs=in_specs, out_specs=rows, check_vma=False)
```

time: 125 us -> 50.7 us (0.41)
  local copies, waits for them, and re-layouts: 37 us -> 2.75 us
  other arithmetic: 18.4 us -> 0 us
  blocking collectives: 17.7 us -> 0 us
  Pallas kernels: 0 us -> 17.6 us
  matrix products: 14 us -> 0 us
  waiting for transfers between devices: 22.1 us -> 16.3 us
    all_to_all x3 -> x0, waiting for transfers between devices: 22.1 us -> none  [the longest x1 18.1 us: body(): lax.all_to_all(local_part[2][None], 'seq', split_axis=1, concat_axis=0, t...]
    all_gather x1 -> x0, blocking collectives: 17.7 us -> none  [body(): gathered = lax.all_gather(queries, 'seq', axis=0, tiled=True)]
    pallas_call x0 -> x2, Pallas kernels: none -> 17.6 us  [the longest x1 15.3 us: body(): pl.pallas_call(functools.partial(work, shares=shares, kv_local=kv_local,...]
    ppermute x0 -> x6, waiting for transfers between devices: none -> 16.3 us  [shift(): lax.ppermute(x, 'seq', [(i, (i + k) % shares) for i in range(shares)])]
    dot_general x8 -> x0, matrix products: 14 us -> none  [the longest x4 9.15 us: attend(): jnp.einsum('taoz,zah->taoh', softmax_weights.astype(jnp.bfloat16), value_...]
    all_to_all x3 -> x0, starting transfers between devices: 14 us -> none  [the longest x1 5.38 us: body(): lax.all_to_all(local_part[1][None], 'seq', split_axis=1, concat_axis=0, t...]
    ppermute x0 -> x6, starting transfers between devices: none -> 13.8 us  [shift(): lax.ppermute(x, 'seq', [(i, (i + k) % shares) for i in range(shares)])]
    scatter x8 -> x0, local copies, waits for them, and re-layouts: 9.56 us -> none  [the longest x3 3.32 us: body(): branch_part[0].at[target].set(result[0], mode='drop')]
  transfers between devices with their start and end apart: 3 -> 6, of which waited for: 2 -> 4; matrix products, arithmetic and copies ran while one was open for 15% -> 3% of each run, Pallas kernels for 0% -> 0%
where the time goes in v1:
time: 50.7 us; the launch traced here: 50.5 us
  Pallas kernels  17.6 us (35%)
  waiting for transfers between devices  16.3 us (32%)
  starting transfers between devices  13.8 us (27%)
  local copies, waits for them, and re-layouts  2.75 us (5%)
    ppermute x6, waiting for transfers between devices, shift(): lax.ppermute(x, 'seq', [(i, (i + k) % shares) for i in range(shares)])  16.3 us
    pallas_call x1, Pallas kernels, body(): pl.pallas_call(functools.partial(work, shares=shares, kv_local=kv_local,...  15.3 us
    ppermute x6, starting transfers between devices, shift(): lax.ppermute(x, 'seq', [(i, (i + k) % shares) for i in range(shares)])  13.8 us
    unnamed x13, local copies, waits for them, and re-layouts  2.75 us
    pallas_call x1, Pallas kernels, body(): pl.pallas_call(functools.partial(join, heads=heads), out_shape=jax.ShapeD...  2.32 us
  transfers between devices with their start and end apart: 6, of which 4 were waited for; matrix products, arithmetic and copies ran while one was open for 3% of the time, Pallas kernels for 0%

profile of v1, /device:TPU:0, one launch (start us, length us, event | category | flops | bytes accessed | tf_op | source)
XLA Modules:
  0.0 50.5 jit_solution(9513572134209604260)
XLA Ops:
  0.0 4.1 %collective-permute-start.1 = (bf16[32,2048]{1,0:T(8,128)(2,1)}, bf16[32,2048]{1,0:T(8,128)(2,1)S(1)}, u32[]{:S(2)}, u32[]{:S(2)}) collective-permute-start(bf16[32,2048]{1,0:T(8,128)(2,1)} %rest_0_.1), channel_id=1, source_target_pairs={{0,8},{4,12},{8,0},{12,4},{1,9},{5,13},{9,1},{13,5},{2,10},{6,14},... | collective-permute-start | bytes 393224 | tf_op jit(solution)/shard_map/ppermute | solution.py:183
  4.1 1.6 %collective-permute-start = (bf16[32,2048]{1,0:T(8,128)(2,1)}, bf16[32,2048]{1,0:T(8,128)(2,1)S(1)}, u32[]{:S(2)}, u32[]{:S(2)}) collective-permute-start(bf16[32,2048]{1,0:T(8,128)(2,1)} %rest_0_.1), channel_id=1, source_target_pairs={{0,4},{4,8},{8,12},{12,0},{1,5},{5,9},{9,13},{13,1},{2,6},{6,10},{... | collective-permute-start | bytes 393224 | tf_op jit(solution)/shard_map/ppermute | solution.py:183
  5.6 2.2 %collective-permute-start.2 = (bf16[32,2048]{1,0:T(8,128)(2,1)}, bf16[32,2048]{1,0:T(8,128)(2,1)S(1)}, u32[]{:S(2)}, u32[]{:S(2)}) collective-permute-start(bf16[32,2048]{1,0:T(8,128)(2,1)} %rest_0_.1), channel_id=1, source_target_pairs={{0,12},{4,0},{8,4},{12,8},{1,13},{5,1},{9,5},{13,9},{2,14},{6,2},{... | collective-permute-start | bytes 393224 | tf_op jit(solution)/shard_map/ppermute | solution.py:183
  7.9 1.4 %copy.8.id_ref = s32[128,1]{1,0:T(8,128)} copy(s32[128,1]{0,1:T(1,128)} %param.12) | data formatting | bytes 1024 | tf_op args[5]
  9.3 5.0 %collective-permute-done.1.rest_2_ = bf16[32,2048]{1,0:T(8,128)(2,1)S(1)} collective-permute-done((bf16[32,2048]{1,0:T(8,128)(2,1)}, bf16[32,2048]{1,0:T(8,128)(2,1)S(1)}, u32[]{:S(2)}, u32[]{:S(2)}) %collective-permute-start.1) | collective-permute-done | bytes 131104 | tf_op jit(solution)/shard_map/ppermute | solution.py:183
  14.3 0.0 copy-start.3
  14.3 0.0 collective-permute-done.rest_1_
  14.3 0.0 copy-start.4
  14.3 0.7 %collective-permute-done.2.rest_3_ = bf16[32,2048]{1,0:T(8,128)(2,1)S(1)} collective-permute-done((bf16[32,2048]{1,0:T(8,128)(2,1)}, bf16[32,2048]{1,0:T(8,128)(2,1)S(1)}, u32[]{:S(2)}, u32[]{:S(2)}) %collective-permute-start.2) | collective-permute-done | bytes 131104 | tf_op jit(solution)/shard_map/ppermute | solution.py:183
  15.0 0.0 copy-start.5
  15.0 0.0 copy-done.3
  15.0 0.0 copy-done.4
  15.0 0.7 %copy-done.5 = bf16[32,2048]{1,0:T(8,128)(2,1)} copy-done((bf16[32,2048]{1,0:T(8,128)(2,1)}, bf16[32,2048]{1,0:T(8,128)(2,1)S(1)}, u32[]{:S(2)}) %copy-start.5) | copy-done | bytes 131096
  15.6 15.3 %work.1 = (bf16[528,128]{1,0:T(8,128)(2,1)}, bf16[528,128]{1,0:T(8,128)(2,1)}, bf16[528,128]{1,0:T(8,128)(2,1)}, bf16[528,128]{1,0:T(8,128)(2,1)}) custom-call(s32[1]{0:T(128)} %bitcast.me_ref, s32[8]{0:T(128)} %doc_ref.1, s32[128,1]{1,0:T(8,128)} %copy.8.id_ref, bf16[2048,256]{1,0:T(8,128)(2,1)} %rk_ref.1, bf16[2048,256]{1,0:T(8,128)(2,1)} %rv_ref.1, ...), custom_call_target="tpu_custom_call" | custom-call | tf_op jit(solution)/shard_map/work/pallas_call | solution.py:188
  30.9 2.1 %collective-permute-start.3 = (bf16[528,128]{1,0:T(8,128)(2,1)}, bf16[528,128]{1,0:T(8,128)(2,1)S(1)}, u32[]{:S(2)}, u32[]{:S(2)}) collective-permute-start(bf16[528,128]{1,0:T(8,128)(2,1)} %get-tuple-element.10), channel_id=1, source_target_pairs={{0,12},{4,0},{8,4},{12,8},{1,13},{5,1},{9,5},{13,9},{2,14},{6,2},{... | collective-permute-start | bytes 405512 | tf_op jit(solution)/shard_map/ppermute | solution.py:183
  33.0 1.8 %collective-permute-start.4 = (bf16[528,128]{1,0:T(8,128)(2,1)}, bf16[528,128]{1,0:T(8,128)(2,1)S(1)}, u32[]{:S(2)}, u32[]{:S(2)}) collective-permute-start(bf16[528,128]{1,0:T(8,128)(2,1)} %get-tuple-element.11), channel_id=1, source_target_pairs={{0,8},{4,12},{8,0},{12,4},{1,9},{5,13},{9,1},{13,5},{2,10},{6,14},... | collective-permute-start | bytes 405512 | tf_op jit(solution)/shard_map/ppermute | solution.py:183
  34.8 2.0 %collective-permute-start.5 = (bf16[528,128]{1,0:T(8,128)(2,1)}, bf16[528,128]{1,0:T(8,128)(2,1)S(1)}, u32[]{:S(2)}, u32[]{:S(2)}) collective-permute-start(bf16[528,128]{1,0:T(8,128)(2,1)} %get-tuple-element.12), channel_id=1, source_target_pairs={{0,4},{4,8},{8,12},{12,0},{1,5},{5,9},{9,13},{13,1},{2,6},{6,10},{... | collective-permute-start | bytes 405512 | tf_op jit(solution)/shard_map/ppermute | solution.py:183
  36.9 0.1 collective-permute-done.3.refs_1_
  37.0 10.5 %collective-permute-done.4.refs_2_ = bf16[528,128]{1,0:T(8,128)(2,1)S(1)} collective-permute-done((bf16[528,128]{1,0:T(8,128)(2,1)}, bf16[528,128]{1,0:T(8,128)(2,1)S(1)}, u32[]{:S(2)}, u32[]{:S(2)}) %collective-permute-start.4) | collective-permute-done | bytes 135200 | tf_op jit(solution)/shard_map/ppermute | solution.py:183
  47.5 0.0 collective-permute-done.5.refs_3_
  47.5 0.0 copy-done
  47.5 0.6 %copy-done.1 = bf16[528,128]{1,0:T(8,128)(2,1)} copy-done((bf16[528,128]{1,0:T(8,128)(2,1)}, bf16[528,128]{1,0:T(8,128)(2,1)S(1)}, u32[]{:S(2)}) %copy-start.1) | copy-done | bytes 135192
  48.2 0.1 copy-done.2
  48.2 2.3 %join.1 = bf16[32,2048]{1,0:T(8,128)(2,1)} custom-call(bf16[528,128]{1,0:T(8,128)(2,1)} %get-tuple-element.9.refs_0_, bf16[528,128]{1,0:T(8,128)(2,1)} %copy-done, bf16[528,128]{1,0:T(8,128)(2,1)} %copy-done.1, bf16[528,128]{1,0:T(8,128)(2,1)} %copy-done.2), custom_call_target="tpu_custom_call" | custom-call | tf_op jit(solution)/shard_map/join/pallas_call | solution.py:203
  (3 shorter events, 0.0 us)
Async XLA Ops:
  0.0 14.3 %collective-permute-start.1 = (bf16[32,2048]{1,0:T(8,128)(2,1)}, bf16[32,2048]{1,0:T(8,128)(2,1)S(1)}, u32[]{:S(2)}, u32[]{:S(2)}) collective-permute-start(bf16[32,2048]{1,0:T(8,128)(2,1)} %rest_0_.1), channel_id=1, source_target_pairs={{0,8},{4,12},{8,0},{12,4},{1,9},{5,13},{9,1},{13,5},{2,10},{6,14},... | collective-permute-start | bytes 393224 | tf_op jit(solution)/shard_map/ppermute | solution.py:183
  4.1 10.2 %collective-permute-start = (bf16[32,2048]{1,0:T(8,128)(2,1)}, bf16[32,2048]{1,0:T(8,128)(2,1)S(1)}, u32[]{:S(2)}, u32[]{:S(2)}) collective-permute-start(bf16[32,2048]{1,0:T(8,128)(2,1)} %rest_0_.1), channel_id=1, source_target_pairs={{0,4},{4,8},{8,12},{12,0},{1,5},{5,9},{9,13},{13,1},{2,6},{6,10},{... | collective-permute-start | bytes 393224 | tf_op jit(solution)/shard_map/ppermute | solution.py:183
  5.6 9.3 %collective-permute-start.2 = (bf16[32,2048]{1,0:T(8,128)(2,1)}, bf16[32,2048]{1,0:T(8,128)(2,1)S(1)}, u32[]{:S(2)}, u32[]{:S(2)}) collective-permute-start(bf16[32,2048]{1,0:T(8,128)(2,1)} %rest_0_.1), channel_id=1, source_target_pairs={{0,12},{4,0},{8,4},{12,8},{1,13},{5,1},{9,5},{13,9},{2,14},{6,2},{... | collective-permute-start | bytes 393224 | tf_op jit(solution)/shard_map/ppermute | solution.py:183
  14.3 0.7 %copy-start.3 = (bf16[32,2048]{1,0:T(8,128)(2,1)}, bf16[32,2048]{1,0:T(8,128)(2,1)S(1)}, u32[]{:S(2)}) copy-start(bf16[32,2048]{1,0:T(8,128)(2,1)S(1)} %collective-permute-done.1.rest_2_) | copy-start | bytes 393220
  14.3 0.7 %copy-start.4 = (bf16[32,2048]{1,0:T(8,128)(2,1)}, bf16[32,2048]{1,0:T(8,128)(2,1)S(1)}, u32[]{:S(2)}) copy-start(bf16[32,2048]{1,0:T(8,128)(2,1)S(1)} %collective-permute-done.rest_1_) | copy-start | bytes 393220
  15.0 0.7 %copy-start.5 = (bf16[32,2048]{1,0:T(8,128)(2,1)}, bf16[32,2048]{1,0:T(8,128)(2,1)S(1)}, u32[]{:S(2)}) copy-start(bf16[32,2048]{1,0:T(8,128)(2,1)S(1)} %collective-permute-done.2.rest_3_) | copy-start | bytes 393220
  30.9 6.1 %collective-permute-start.3 = (bf16[528,128]{1,0:T(8,128)(2,1)}, bf16[528,128]{1,0:T(8,128)(2,1)S(1)}, u32[]{:S(2)}, u32[]{:S(2)}) collective-permute-start(bf16[528,128]{1,0:T(8,128)(2,1)} %get-tuple-element.10), channel_id=1, source_target_pairs={{0,12},{4,0},{8,4},{12,8},{1,13},{5,1},{9,5},{13,9},{2,14},{6,2},{... | collective-permute-start | bytes 405512 | tf_op jit(solution)/shard_map/ppermute | solution.py:183
  33.0 14.5 %collective-permute-start.4 = (bf16[528,128]{1,0:T(8,128)(2,1)}, bf16[528,128]{1,0:T(8,128)(2,1)S(1)}, u32[]{:S(2)}, u32[]{:S(2)}) collective-permute-start(bf16[528,128]{1,0:T(8,128)(2,1)} %get-tuple-element.11), channel_id=1, source_target_pairs={{0,8},{4,12},{8,0},{12,4},{1,9},{5,13},{9,1},{13,5},{2,10},{6,14},... | collective-permute-start | bytes 405512 | tf_op jit(solution)/shard_map/ppermute | solution.py:183
  34.8 12.7 %collective-permute-start.5 = (bf16[528,128]{1,0:T(8,128)(2,1)}, bf16[528,128]{1,0:T(8,128)(2,1)S(1)}, u32[]{:S(2)}, u32[]{:S(2)}) collective-permute-start(bf16[528,128]{1,0:T(8,128)(2,1)} %get-tuple-element.12), channel_id=1, source_target_pairs={{0,4},{4,8},{8,12},{12,0},{1,5},{5,9},{9,13},{13,1},{2,6},{6,10},{... | collective-permute-start | bytes 405512 | tf_op jit(solution)/shard_map/ppermute | solution.py:183
  37.0 10.5 %copy-start = (bf16[528,128]{1,0:T(8,128)(2,1)}, bf16[528,128]{1,0:T(8,128)(2,1)S(1)}, u32[]{:S(2)}) copy-start(bf16[528,128]{1,0:T(8,128)(2,1)S(1)} %collective-permute-done.3.refs_1_) | copy-start | bytes 405508
  47.5 0.7 %copy-start.1 = (bf16[528,128]{1,0:T(8,128)(2,1)}, bf16[528,128]{1,0:T(8,128)(2,1)S(1)}, u32[]{:S(2)}) copy-start(bf16[528,128]{1,0:T(8,128)(2,1)S(1)} %collective-permute-done.4.refs_2_) | copy-start | bytes 405508
  47.5 0.7 %copy-start.2 = (bf16[528,128]{1,0:T(8,128)(2,1)}, bf16[528,128]{1,0:T(8,128)(2,1)S(1)}, u32[]{:S(2)}) copy-start(bf16[528,128]{1,0:T(8,128)(2,1)S(1)} %collective-permute-done.5.refs_3_) | copy-start | bytes 405508

commit v2 on v0

v2 whole, which is shorter than its diff:
```python
import functools
import math

import jax
import jax.numpy as jnp
from jax import lax
from jax.experimental import pallas as pl
from jax.experimental.pallas import tpu as pltpu
from jax.sharding import PartitionSpec as P

QHEADS = 64
KVHEADS = 8
HEAD_DIM = 128
GROUP = QHEADS // KVHEADS
LOW = -1.0e30
SCALE = HEAD_DIM ** -0.5 * math.log2(math.e)
TILE = 256
VMEM_BYTES = 20 * 2 ** 20


def dot(a, b, dims=(((1,), (0,)), ((), ()))):
    return lax.dot_general(a, b, dims, preferred_element_type=jnp.float32)


def pieces(x):
    hi = x.astype(jnp.bfloat16)
    rest = x - hi.astype(jnp.float32)
    mid = rest.astype(jnp.bfloat16)
    low = (rest - mid.astype(jnp.float32)).astype(jnp.bfloat16)
    return hi, mid, low


def pipeline(blocks, score_ref):
    query, best = {}, {}

    def tiles(i):
        return [slice(at, at + TILE) for at in range(0, blocks[i][4], TILE)] if i < len(blocks) else []

    def score(i, at):
        if i not in query:
            query[i] = blocks[i][0]()
        s = dot(query[i], blocks[i][1](at), (((1,), (1,)), ((), ())))
        if blocks[i][3] is not None:
            s = s + blocks[i][3](at)
        score_ref[i % 2, :, at] = s
        for part in range(TILE // HEAD_DIM):
            t = s[:, part * HEAD_DIM:(part + 1) * HEAD_DIM]
            best[i] = jnp.maximum(best[i], t) if i in best else t

    for at in tiles(0):
        score(0, at)
    for i, (_, _, values, _, _, finish) in enumerate(blocks):
        peak = jnp.broadcast_to(jnp.max(best[i], axis=1, keepdims=True) * SCALE, best[i].shape)
        wide = jnp.concatenate([peak] * (TILE // HEAD_DIM), axis=1)
        ahead = tiles(i + 1)
        out = None
        for at in tiles(i):
            for later in ahead[:1]:
                score(i + 1, later)
            ahead = ahead[1:]
            w = jnp.exp2(score_ref[i % 2, :, at] * SCALE - wide).astype(jnp.bfloat16)
            part = dot(w, jnp.concatenate([values(at), jnp.ones((TILE, HEAD_DIM), jnp.bfloat16)], axis=1))
            out = part if out is None else out + part
        for later in ahead:
            score(i + 1, later)
        whole = out[:, HEAD_DIM:]
        finish(out[:, :HEAD_DIM] / whole, peak + jnp.log2(whole))


def stack_heads(chunk, first=0):
    return jnp.concatenate([chunk[:, (first + h) * HEAD_DIM:(first + h + 1) * HEAD_DIM] for h in range(GROUP)], axis=0)


def compact(levels):
    rows = next(iter(levels.values())).shape[0] // GROUP
    lane = lax.broadcasted_iota(jnp.int32, (rows, HEAD_DIM), 1)
    result = jnp.zeros((rows, HEAD_DIM), jnp.float32)
    for f, level in levels.items():
        for h in range(GROUP):
            result = jnp.where(lane == f * GROUP + h, level[h * rows:(h + 1) * rows, :], result)
    return result


def spread(stat, h, rows):
    return jnp.broadcast_to(stat[:, h:h + 1], (rows, HEAD_DIM))


def roots(query, rk_ref, rv_ref, heads, finish):
    outputs, levels = {}, {}

    def block(f):
        cut = slice(f * HEAD_DIM, (f + 1) * HEAD_DIM)

        def done(output, level):
            outputs[f], levels[f] = output, level
            if len(levels) == len(heads):
                finish(outputs, compact(levels))

        return (lambda: query(f), lambda at: rk_ref[at, cut], lambda at: rv_ref[at, cut], None, rk_ref.shape[0], done)

    return [block(f) for f in heads]


def store(out_ref, level_ref):
    def finish(outputs, level):
        for f, output in outputs.items():
            out_ref[f] = output
        level_ref[...] = level

    return finish


def own(*rest, kv_local):
    sources, rest = rest[:7], rest[7:]
    rk_ref, rv_ref, bk_ref, bv_ref, pick_ref, bias_ref, out_ref, level_ref, score_ref, id_ref, q_ref, doc_ref, arrived = rest
    loads = [pltpu.make_async_copy(source, target, arrived.at[n]) for n, (source, target) in enumerate(zip(sources, (id_ref, q_ref, rk_ref, doc_ref, rv_ref, bk_ref, bv_ref)))]
    for load in loads[:5]:
        load.start()
    branch_dev, rows, most_rows = pick_ref.shape
    me = lax.axis_index("seq").astype(jnp.int32)
    loads[3].wait()
    slot = lax.broadcasted_iota(jnp.int32, (1, bias_ref.shape[1]), 1)
    for b in range(branch_dev):
        bias_ref[b:b + 1, :] = jnp.where(slot < doc_ref[me * branch_dev + b], 0.0, LOW)
    loads[0].wait()
    ids = id_ref[...]
    before = jnp.where(lax.broadcasted_iota(jnp.int32, (rows, rows), 0) < lax.broadcasted_iota(jnp.int32, (rows, rows), 1), 1.0, 0.0).astype(jnp.bfloat16)
    slot = lax.broadcasted_iota(jnp.int32, (most_rows, rows), 0).astype(jnp.float32)
    unit = jnp.where(lax.broadcasted_iota(jnp.int32, (most_rows, most_rows), 0) == lax.broadcasted_iota(jnp.int32, (most_rows, most_rows), 1), 1.0, 0.0).astype(jnp.bfloat16)
    for b in range(branch_dev):
        named = jnp.broadcast_to(jnp.where(ids == me * branch_dev + b, 1.0, 0.0), (most_rows, rows))
        rank = dot(named.astype(jnp.bfloat16), before)
        chosen = jnp.where((rank == slot) & (named > 0.0), 1.0, 0.0).astype(jnp.bfloat16)
        pick_ref[b] = dot(chosen, unit, (((0,), (0,)), ((), ()))).astype(jnp.bfloat16)
    for load in loads[1:3] + loads[4:5]:
        load.wait()
    for load in loads[5:]:
        load.start()
    pipeline(roots(lambda f: stack_heads(q_ref, f * GROUP), rk_ref, rv_ref, range(kv_local), store(out_ref, level_ref)), score_ref)
    for load in loads[5:]:
        load.wait()


def root(q_ref, rk_ref, rv_ref, out_ref, level_ref, score_ref, *, kv_local):
    pipeline(roots(lambda f: stack_heads(q_ref, f * GROUP), rk_ref, rv_ref, range(kv_local), store(out_ref, level_ref)), score_ref)


def picks(pick_ref, key, row_dev):
    source = lax.axis_index("seq").astype(jnp.int32) ^ key
    at = pl.ds(pl.multiple_of(source * row_dev, row_dev), row_dev)
    return [pick_ref[b, at, :] for b in range(pick_ref.shape[0])]


def merge(share_ref, pick, outputs, level, branch_refs, b_level):
    row_dev = level.shape[0]
    pick = jnp.concatenate(pick, axis=1)
    has = jnp.sum(pick.astype(jnp.float32), axis=1, keepdims=True) > 0.0
    found = dot(pick, b_level)
    b_level = jnp.where(has, found[:, :HEAD_DIM] + found[:, HEAD_DIM:2 * HEAD_DIM] + found[:, 2 * HEAD_DIM:], LOW)
    top = jnp.maximum(level, b_level)
    ours, theirs = jnp.exp2(level - top), jnp.exp2(b_level - top)
    both = ours + theirs
    ours, theirs = ours / both, theirs / both
    for n, (f, output) in enumerate(outputs.items()):
        b_out = dot(pick, branch_refs[f][...])
        for g in range(GROUP):
            h = f * GROUP + g
            at = (n * GROUP + g) * row_dev
            ahead = output[g * row_dev:(g + 1) * row_dev, :] * spread(ours, h, row_dev)
            share_ref[at:at + row_dev, :] = (ahead + b_out[:, g * HEAD_DIM:(g + 1) * HEAD_DIM] * spread(theirs, h, row_dev)).astype(jnp.bfloat16)
    lane = lax.broadcasted_iota(jnp.int32, (row_dev, HEAD_DIM), 1)
    here = functools.reduce(jnp.logical_or, [(lane >= f * GROUP) & (lane < (f + 1) * GROUP) for f in outputs])
    stat = jnp.where(here, top + jnp.log2(both), 0.0)
    heads = len(branch_refs) * GROUP
    stat = stat + pltpu.roll(stat, heads, 1) + pltpu.roll(stat, 2 * heads, 1)
    hi, mid, low = [piece.astype(jnp.float32) for piece in pieces(stat)]
    packed = jnp.where(lane < heads, hi, jnp.where(lane < 2 * heads, mid, low))
    half = row_dev // 2
    share_ref[len(outputs) * GROUP * row_dev:, :] = (packed[:half] + pltpu.roll(packed[half:], HEAD_DIM // 2, 1)).astype(jnp.bfloat16)


def branch_blocks(pick_ref, bias_ref, bk_ref, bv_ref, q_refs, rows_ref, branch_ref, keys, f, finish):
    row_dev = q_refs[0].shape[0]
    branch_dev, _, most_rows = pick_ref.shape
    part = rows_ref.shape[1]
    cut = slice(f * HEAD_DIM, (f + 1) * HEAD_DIM)
    me = lax.axis_index("seq").astype(jnp.int32)
    for k, q_ref in zip(keys, q_refs):
        at = pl.ds(pl.multiple_of((me ^ k) * row_dev, row_dev), row_dev)
        rows_ref[at, :] = q_ref[...] if k == keys[-1] else q_ref[:, f * part:(f + 1) * part]
    named = jnp.concatenate([pick_ref[b] for b in range(branch_dev)], axis=1)
    picked = dot(named, rows_ref[...], (((0,), (0,)), ((), ()))).astype(jnp.bfloat16)
    levels = []

    def block(b):
        def done(output, level):
            for h in range(GROUP):
                branch_ref[b * most_rows:(b + 1) * most_rows, h * HEAD_DIM:(h + 1) * HEAD_DIM] = output[h * most_rows:(h + 1) * most_rows].astype(jnp.bfloat16)
            levels.append(compact({f: level}))
            if len(levels) == branch_dev:
                finish(jnp.concatenate(levels, axis=0))

        return (lambda: stack_heads(picked[b * most_rows:(b + 1) * most_rows]), lambda at: bk_ref[b, at, cut], lambda at: bv_ref[b, at, cut], lambda at: bias_ref[b:b + 1, at], bk_ref.shape[1], done)

    return [block(b) for b in range(branch_dev)]


def branch(pick_ref, bias_ref, bk_ref, bv_ref, out_ref, level_ref, *rest, keys, f, key, kv_local):
    branch_refs, rest = rest[:f], rest[f:]
    total_refs, rest = rest[:min(f, 1)], rest[min(f, 1):]
    q_refs = rest[:len(keys)]
    share_ref, branch_ref, total_ref, score_ref, rows_ref = rest[len(keys):]

    def finish(level):
        total = jnp.concatenate(pieces(level), axis=1)
        for ref in total_refs:
            total = total + ref[...]
        total_ref[...] = total

    pipeline(branch_blocks(pick_ref, bias_ref, bk_ref, bv_ref, q_refs, rows_ref, branch_ref, keys, f, finish), score_ref)
    every = [*branch_refs, branch_ref] + [None] * (kv_local - 1 - f)
    merge(share_ref, picks(pick_ref, key, level_ref.shape[0]), {f: out_ref[f]}, level_ref[...], every, total_ref[...])


def share(pick_ref, b_level_ref, rk_ref, rv_ref, *rest, key, kv_local):
    branch_refs, q_refs, share_ref, score_ref = rest[:kv_local], rest[kv_local:2 * kv_local], rest[-2], rest[-1]

    def finish(outputs, level):
        merge(share_ref, picks(pick_ref, key, level.shape[0]), outputs, level, branch_refs, b_level_ref[...])

    pipeline(roots(lambda f: stack_heads(q_refs[f]), rk_ref, rv_ref, range(kv_local), finish), score_ref)


def given(pick_ref, b_level_ref, out_ref, level_ref, *rest, key):
    branch_refs, share_ref = rest[:-1], rest[-1]
    merge(share_ref, picks(pick_ref, key, level_ref.shape[0]), {f: out_ref[f] for f in range(len(branch_refs))}, level_ref[...], branch_refs, b_level_ref[...])


def join(*refs, heads, counts):
    out_ref = refs[-1]
    row_dev = out_ref.shape[0]
    half = row_dev // 2
    groups, at = [], 0
    for count in counts:
        groups.append(refs[at:at + count])
        at += count
    levels = []
    for group in groups:
        s = sum(ref[heads // len(group) * row_dev:, :].astype(jnp.float32) for ref in group)
        levels.append(s + pltpu.roll(s, HEAD_DIM - heads, 1) + pltpu.roll(s, HEAD_DIM - 2 * heads, 1))
    top = functools.reduce(jnp.maximum, levels)
    parts = [jnp.exp2(x - top) for x in levels]
    whole = functools.reduce(jnp.add, parts)
    parts = [x / whole for x in parts]
    for h in range(heads):
        result = None
        for group, part in zip(groups, parts):
            each = heads // len(group)
            factor = jnp.concatenate([spread(part, h, half), spread(part, HEAD_DIM // 2 + h, half)], axis=0)
            term = group[h // each][h % each * row_dev:(h % each + 1) * row_dev, :].astype(jnp.float32) * factor
            result = term if result is None else result + term
        out_ref[:, h * HEAD_DIM:(h + 1) * HEAD_DIM] = result.astype(jnp.bfloat16)


VMEM = pl.BlockSpec(memory_space=pltpu.VMEM)
SMEM = pl.BlockSpec(memory_space=pltpu.SMEM)
HBM = pl.BlockSpec(memory_space=pltpu.HBM)


def call(kernel, out_shape, in_specs, scratch_shapes=(), **static):
    many = isinstance(out_shape, list)
    return pl.pallas_call(
        functools.partial(kernel, **static),
        out_shape=out_shape,
        in_specs=in_specs,
        out_specs=[VMEM] * len(out_shape) if many else VMEM,
        scratch_shapes=scratch_shapes,
        compiler_params=pltpu.CompilerParams(vmem_limit_bytes=VMEM_BYTES),
    )


def body(queries, root_keys, root_values, branch_keys, branch_values, branch_id, doc_len):
    shares = lax.axis_size("seq")
    row_dev, width = queries.shape
    rows = branch_id.shape[0]
    kv_local = root_keys.shape[1] // HEAD_DIM
    heads = kv_local * GROUP
    part = width // kv_local
    branch_dev, branch_len, _ = branch_keys.shape
    most_rows = 2 * row_dev // branch_dev
    slots = branch_dev * most_rows
    block = GROUP * row_dev
    f32 = functools.partial(jax.ShapeDtypeStruct, dtype=jnp.float32)
    bf16 = functools.partial(jax.ShapeDtypeStruct, dtype=jnp.bfloat16)
    scores = pltpu.VMEM((2, block, max(root_keys.shape[0], branch_len)), jnp.float32)
    some_rows = pltpu.VMEM((rows, part), jnp.bfloat16)
    result = [f32((kv_local, block, HEAD_DIM)), f32((row_dev, HEAD_DIM))]
    payload = bf16((heads * row_dev + row_dev // 2, HEAD_DIM))

    def swap(x, k):
        return lax.ppermute(x, "seq", [(i, i ^ k) for i in range(shares)])

    _, early, last, first, later = plan(shares)
    gathered = {}
    for k in early:
        gathered[k] = swap(queries, k)
    pieces_of_last = []
    for f in range(kv_local):
        piece = queries[:, f * part:(f + 1) * part]
        pieces_of_last.append(swap(piece, last))
    stored = (root_keys, root_values, branch_keys, branch_values)
    rk, rv, bk, bv, pick, bias, *mine = call(
        own,
        [bf16(x.shape) for x in stored] + [bf16((branch_dev, rows, most_rows)), f32((branch_dev, branch_len))] + result,
        [HBM] * 7,
        [scores, pltpu.VMEM((1, rows), jnp.int32), pltpu.VMEM((row_dev, width), jnp.bfloat16), pltpu.SMEM(doc_len.shape, jnp.int32), pltpu.SemaphoreType.DMA((7,))],
        kv_local=kv_local,
    )(*[pltpu.with_memory_space_constraint(x, pltpu.HBM) for x in (branch_id.reshape(1, rows), queries, root_keys, doc_len, *stored[1:])])
    ready = {0: mine}
    for k in early:
        ready[k] = call(root, result, [VMEM] * 3, [scores], kv_local=kv_local)(gathered[k], rk, rv)
    keys = [0] + early + [last]
    chunks = [queries] + [gathered[k] for k in early]
    branch_out, totals, sent = [], [], {first: []}
    for f in range(kv_local):
        partial, out, total = call(
            branch,
            [bf16((block + row_dev // 2, HEAD_DIM)), bf16((slots, part)), bf16((slots, 3 * HEAD_DIM))],
            [VMEM] * (6 + f + len(totals) + shares),
            [scores, some_rows],
            keys=keys,
            f=f,
            key=first,
            kv_local=kv_local,
        )(pick, bias, bk, bv, *ready[first], *branch_out, *totals, *chunks, pieces_of_last[f])
        branch_out.append(out)
        totals = [total]
        sent[first].append(partial)
    for k in later:
        if k in ready:
            partial = call(given, payload, [VMEM] * (4 + kv_local), key=k)(pick, *totals, *ready[k], *branch_out)
        else:
            partial = call(share, payload, [VMEM] * (4 + 2 * kv_local), [scores], key=k, kv_local=kv_local)(pick, *totals, rk, rv, *branch_out, *pieces_of_last)
        sent[k] = [partial]
    received, counts = [*sent[0]], [1]
    for k in [first] + later[:-1]:
        for partial in sent[k]:
            received.append(swap(partial, k))
        counts.append(len(sent[k]))
    return call(join, bf16((row_dev, width)), [VMEM] * len(received), heads=heads, counts=counts)(*received)


def plan(shares):
    order = list(range(1, shares))
    order = [shares // 2] + [k for k in order if k != shares // 2]
    return order, order[:-1], order[-1], order[0], [order[-1]] + order[1:-1] + [0]


def solution(mesh):
    rows = P(("parts", "seq"), "head")
    in_specs = (
        rows,
        rows,
        rows,
        P(("parts", "seq"), None, "head"),
        P(("parts", "seq"), None, "head"),
        P("parts", None),
        P("parts"),
    )

    return jax.shard_map(body, mesh=mesh, in_specs=in_specs, out_specs=rows, check_vma=False)
```

time: 125 us -> 39.9 us (0.32)
  local copies, waits for them, and re-layouts: 37 us -> 0.89 us
  other arithmetic: 18.4 us -> 0 us
  blocking collectives: 17.7 us -> 0 us
  Pallas kernels: 0 us -> 15.4 us
  matrix products: 14 us -> 0 us
  waiting for transfers between devices: 22.1 us -> 9.26 us
    all_to_all x3 -> x0, waiting for transfers between devices: 22.1 us -> none  [the longest x1 18.1 us: body(): lax.all_to_all(local_part[2][None], 'seq', split_axis=1, concat_axis=0, t...]
    all_gather x1 -> x0, blocking collectives: 17.7 us -> none  [body(): gathered = lax.all_gather(queries, 'seq', axis=0, tiled=True)]
    pallas_call x0 -> x9, Pallas kernels: none -> 15.4 us  [the longest x2 4.23 us: body(): call(branch, [bf16((block + row_dev // 2, HEAD_DIM)), bf16((slots, part))...]
    ppermute x0 -> x8, starting transfers between devices: none -> 14.1 us  [swap(): return lax.ppermute(x, 'seq', [(i, i ^ k) for i in range(shares)])]
    dot_general x8 -> x0, matrix products: 14 us -> none  [the longest x4 9.15 us: attend(): jnp.einsum('taoz,zah->taoh', softmax_weights.astype(jnp.bfloat16), value_...]
    all_to_all x3 -> x0, starting transfers between devices: 14 us -> none  [the longest x1 5.38 us: body(): lax.all_to_all(local_part[1][None], 'seq', split_axis=1, concat_axis=0, t...]
    scatter x8 -> x0, local copies, waits for them, and re-layouts: 9.56 us -> none  [the longest x3 3.32 us: body(): branch_part[0].at[target].set(result[0], mode='drop')]
    unnamed x42 -> x2, local copies, waits for them, and re-layouts: 9.32 us -> 0.01 us
  transfers between devices with their start and end apart: 3 -> 8, of which waited for: 2 -> 2; matrix products, arithmetic and copies ran while one was open for 15% -> 2% of each run, Pallas kernels for 0% -> 29%
where the time goes in v2:
time: 39.9 us; the launch traced here: 39.7 us
  Pallas kernels  15.4 us (39%)
  starting transfers between devices  14.1 us (35%)
  waiting for transfers between devices  9.26 us (23%)
  local copies, waits for them, and re-layouts  0.89 us (2%)
    ppermute x8, starting transfers between devices, swap(): return lax.ppermute(x, 'seq', [(i, i ^ k) for i in range(shares)])  14.1 us
    ppermute x8, waiting for transfers between devices, swap(): return lax.ppermute(x, 'seq', [(i, i ^ k) for i in range(shares)])  9.26 us
    pallas_call x2, Pallas kernels, body(): call(branch, [bf16((block + row_dev // 2, HEAD_DIM)), bf16((slots, part))...  4.23 us
    pallas_call x1, Pallas kernels, body(): call(own, [bf16(x.shape) for x in stored] + [bf16((branch_dev, rows, most...  3.92 us
    pallas_call x2, Pallas kernels, body(): call(root, result, [VMEM] * 3, [scores], kv_local=kv_local)  3.02 us
    pallas_call x1, Pallas kernels, body(): call(share, payload, [VMEM] * (4 + 2 * kv_local), [scores], key=k, kv_loc...  1.9 us
    pallas_call x1, Pallas kernels, body(): call(join, bf16((row_dev, width)), [VMEM] * len(received), heads=heads, c...  1.23 us
    pallas_call x2, Pallas kernels, body(): call(given, payload, [VMEM] * (4 + kv_local), key=k)  1.05 us
  transfers between devices with their start and end apart: 8, of which 2 were waited for; matrix products, arithmetic and copies ran while one was open for 2% of the time, Pallas kernels for 29%

profile of v2, /device:TPU:0, one launch (start us, length us, event | category | flops | bytes accessed | tf_op | source)
XLA Modules:
  0.0 39.7 jit_solution(1865411155630386735)
XLA Ops:
  0.0 4.1 %collective-permute-start = (bf16[32,2048]{1,0:T(8,128)(2,1)}, bf16[32,2048]{1,0:T(8,128)(2,1)S(1)}, u32[]{:S(2)}, u32[]{:S(2)}) collective-permute-start(bf16[32,2048]{1,0:T(8,128)(2,1)} %rest_2_.3), channel_id=1, source_target_pairs={{0,8},{4,12},{8,0},{12,4},{1,9},{5,13},{9,1},{13,5},{2,10},{6,14},... | collective-permute-start | bytes 393224 | tf_op jit(solution)/shard_map/ppermute | solution.py:301
  4.1 1.6 %collective-permute-start.1 = (bf16[32,2048]{1,0:T(8,128)(2,1)}, bf16[32,2048]{1,0:T(8,128)(2,1)S(1)}, u32[]{:S(2)}, u32[]{:S(2)}) collective-permute-start(bf16[32,2048]{1,0:T(8,128)(2,1)} %rest_2_.3), channel_id=1, source_target_pairs={{0,4},{4,0},{8,12},{12,8},{1,5},{5,1},{9,13},{13,9},{2,6},{6,2},{1... | collective-permute-start | bytes 393224 | tf_op jit(solution)/shard_map/ppermute | solution.py:301
  5.6 0.9 %fusion = (bf16[32,1024]{1,0:T(8,128)(2,1)S(1)}, bf16[32,1024]{1,0:T(8,128)(2,1)S(1)}) fusion(bf16[32,2048]{1,0:T(8,128)(2,1)} %rest_2_.3), kind=kLoop, calls=%fused_computation | loop fusion | bytes 262144 | tf_op jit(solution)/shard_map/slice | solution.py:309
  6.5 0.1 collective-permute-start.2
  6.6 3.8 %collective-permute-start.3 = (bf16[32,1024]{1,0:T(8,128)(2,1)S(1)}, bf16[32,1024]{1,0:T(8,128)(2,1)S(1)}, u32[]{:S(2)}, u32[]{:S(2)}) collective-permute-start(bf16[32,1024]{1,0:T(8,128)(2,1)S(1)} %get-tuple-element.41), channel_id=1, source_target_pairs={{0,12},{4,8},{8,4},{12,0},{1,13},{5,9},{9,5},{13,1},{2,14},{6,10},... | collective-permute-start | bytes 196616 | tf_op jit(solution)/shard_map/ppermute | solution.py:301
  10.4 3.9 %shard_map.73 = (bf16[2048,256]{1,0:T(8,128)(2,1)S(1)}, bf16[2048,256]{1,0:T(8,128)(2,1)S(1)}, bf16[2,2048,256]{2,1,0:T(8,128)(2,1)S(1)}, bf16[2,2048,256]{2,1,0...) custom-call(s32[1,128]{1,0:T(1,128)} %bitcast.1, ...), custom_call_target="tpu_custom_call" | custom-call | tf_op jit(solution)/shard_map/pallas_call | solution.py:312
  14.4 0.0 copy-start
  14.4 1.5 %shard_map.74 = (f32[2,256,128]{2,1,0:T(8,128)S(1)}, f32[32,128]{1,0:T(8,128)S(1)}) custom-call(bf16[32,2048]{1,0:T(8,128)(2,1)S(1)} %collective-permute-done.q_ref.rest_1_.rest_3_, bf16[2048,256]{1,0:T(8,128)(2,1)S(1)} %get-tuple-element.27.rk_ref, bf16[2048,256]{1,0:T(8,128)(2,1)S(1)} %get-tuple-element.28.rv_ref), custom_call_target="tpu_custom_call" | custom-call | tf_op jit(solution)/shard_map/pallas_call | solution.py:321
  15.9 0.0 collective-permute-done.1.rest_2_.rest_4_.q_ref
  15.9 1.5 %shard_map.79 = (f32[2,256,128]{2,1,0:T(8,128)S(1)}, f32[32,128]{1,0:T(8,128)S(1)}) custom-call(bf16[32,2048]{1,0:T(8,128)(2,1)S(1)} %collective-permute-done.1.rest_2_.rest_4_.q_ref, bf16[2048,256]{1,0:T(8,128)(2,1)S(1)} %get-tuple-element.27.rk_ref, bf16[2048,256]{1,0:T(8,128)(2,1)S(1)} %get-tuple-element.28.rv_ref), custom_call_target="tpu_custom_call" | custom-call | tf_op jit(solution)/shard_map/pallas_call | solution.py:321
  17.4 2.1 %shard_map.75 = (bf16[272,128]{1,0:T(8,128)(2,1)S(1)}, bf16[64,1024]{1,0:T(8,128)(2,1)S(1)}, bf16[64,384]{1,0:T(8,128)(2,1)S(1)}) custom-call(bf16[2,128,32]{2,1,0:T(8,128)(2,1)S(1)} %get-tuple-element.23.pick_ref, f32[2,2048]{1,0:T(2,128)S(1)} %get-tuple-element.24.bias_ref, bf16[2,2048,256]{2,1,0:T(8,128)(2,1)S(1)} %get-tuple-element.25.bk_ref, ...), custom_call_target="tpu_custom_call" | custom-call | tf_op jit(solution)/shard_map/pallas_call | solution.py:326
  19.6 2.1 %shard_map.76 = (bf16[272,128]{1,0:T(8,128)(2,1)S(1)}, bf16[64,1024]{1,0:T(8,128)(2,1)S(1)}, bf16[64,384]{1,0:T(8,128)(2,1)S(1)}) custom-call(bf16[2,128,32]{2,1,0:T(8,128)(2,1)S(1)} %get-tuple-element.23.pick_ref, f32[2,2048]{1,0:T(2,128)S(1)} %get-tuple-element.24.bias_ref, bf16[2,2048,256]{2,1,0:T(8,128)(2,1)S(1)} %get-tuple-element.25.bk_ref, ...), custom_call_target="tpu_custom_call" | custom-call | tf_op jit(solution)/shard_map/pallas_call | solution.py:326
  21.7 0.5 %shard_map.80 = bf16[528,128]{1,0:T(8,128)(2,1)S(1)} custom-call(bf16[2,128,32]{2,1,0:T(8,128)(2,1)S(1)} %get-tuple-element.23.pick_ref, bf16[64,384]{1,0:T(8,128)(2,1)S(1)} %get-tuple-element.33.b_level_ref, f32[2,256,128]{2,1,0:T(8,128)S(1)} %get-tuple-element.39.out_ref, f32[32,128]{1,0:T(8,128)S(1)} %get-tuple-element.40.level_ref, ...), custom_call_target="tpu_custom_call" | custom-call | tf_op jit(solution)/shard_map/pallas_call | solution.py:341
  22.2 0.0 collective-permute-start.7
  22.3 1.9 %shard_map.78 = bf16[528,128]{1,0:T(8,128)(2,1)S(1)} custom-call(bf16[2,128,32]{2,1,0:T(8,128)(2,1)S(1)} %get-tuple-element.23.pick_ref, bf16[64,384]{1,0:T(8,128)(2,1)S(1)} %get-tuple-element.33.b_level_ref, bf16[2048,256]{1,0:T(8,128)(2,1)S(1)} %get-tuple-element.27.rk_ref, bf16[2048,256]{1,0:T(8,128)(2,1)S(1)} %get-tuple-element.28.rv_ref, ...), custom_call_target="tpu_custom_call" | custom-call | tf_op jit(solution)/shard_map/pallas_call | solution.py:343
  24.2 1.6 %collective-permute-start.6 = (bf16[528,128]{1,0:T(8,128)(2,1)S(1)}, bf16[528,128]{1,0:T(8,128)(2,1)S(1)}, u32[]{:S(2)}, u32[]{:S(2)}) collective-permute-start(bf16[528,128]{1,0:T(8,128)(2,1)S(1)} %shard_map.78), channel_id=1, source_target_pairs={{0,12},{4,8},{8,4},{12,0},{1,13},{5,9},{9,5},{13,1},{2,14},{6,10},... | collective-permute-start | bytes 405512 | tf_op jit(solution)/shard_map/ppermute | solution.py:301
  25.7 1.9 %collective-permute-start.5 = (bf16[272,128]{1,0:T(8,128)(2,1)S(1)}, bf16[272,128]{1,0:T(8,128)(2,1)S(1)}, u32[]{:S(2)}, u32[]{:S(2)}) collective-permute-start(bf16[272,128]{1,0:T(8,128)(2,1)S(1)} %get-tuple-element.38), channel_id=1, source_target_pairs={{0,8},{4,12},{8,0},{12,4},{1,9},{5,13},{9,1},{13,5},{2,10},{6,14},... | collective-permute-start | bytes 208904 | tf_op jit(solution)/shard_map/ppermute | solution.py:301
  27.7 1.0 %collective-permute-start.4 = (bf16[272,128]{1,0:T(8,128)(2,1)S(1)}, bf16[272,128]{1,0:T(8,128)(2,1)S(1)}, u32[]{:S(2)}, u32[]{:S(2)}) collective-permute-start(bf16[272,128]{1,0:T(8,128)(2,1)S(1)} %get-tuple-element.37), channel_id=1, source_target_pairs={{0,8},{4,12},{8,0},{12,4},{1,9},{5,13},{9,1},{13,5},{2,10},{6,14},... | collective-permute-start | bytes 208904 | tf_op jit(solution)/shard_map/ppermute | solution.py:301
  28.7 0.5 %shard_map.77.refs_0_ = bf16[528,128]{1,0:T(8,128)(2,1)S(1)} custom-call(bf16[2,128,32]{2,1,0:T(8,128)(2,1)S(1)} %get-tuple-element.23.pick_ref, bf16[64,384]{1,0:T(8,128)(2,1)S(1)} %get-tuple-element.33.b_level_ref, f32[2,256,128]{2,1,0:T(8,128)S(1)} %get-tuple-element.34.out_ref, f32[32,128]{1,0:T(8,128)S(1)} %get-tuple-element.35.level_ref, ...), custom_call_target="tpu_custom_call" | custom-call | tf_op jit(solution)/shard_map/pallas_call | solution.py:341
  29.2 8.5 %collective-permute-done.5.refs_2_ = bf16[272,128]{1,0:T(8,128)(2,1)S(1)} collective-permute-done((bf16[272,128]{1,0:T(8,128)(2,1)S(1)}, bf16[272,128]{1,0:T(8,128)(2,1)S(1)}, u32[]{:S(2)}, u32[]{:S(2)}) %collective-permute-start.5) | collective-permute-done | bytes 69664 | tf_op jit(solution)/shard_map/ppermute | solution.py:301
  37.7 0.8 %collective-permute-done.4.refs_1_ = bf16[272,128]{1,0:T(8,128)(2,1)S(1)} collective-permute-done((bf16[272,128]{1,0:T(8,128)(2,1)S(1)}, bf16[272,128]{1,0:T(8,128)(2,1)S(1)}, u32[]{:S(2)}, u32[]{:S(2)}) %collective-permute-start.4) | collective-permute-done | bytes 69664 | tf_op jit(solution)/shard_map/ppermute | solution.py:301
  38.4 0.0 collective-permute-done.7.refs_4_
  38.4 0.0 collective-permute-done.6.refs_3_
  38.4 1.2 %shard_map.81 = bf16[32,2048]{1,0:T(8,128)(2,1)} custom-call(bf16[528,128]{1,0:T(8,128)(2,1)S(1)} %shard_map.77.refs_0_, bf16[272,128]{1,0:T(8,128)(2,1)S(1)} %collective-permute-done.4.refs_1_, bf16[272,128]{1,0:T(8,128)(2,1)S(1)} %collective-permute-done.5.refs_2_, bf16[528,128]{1,0:T(8,128)(2,1)S(1)} %collective-permute-done.6.refs_3_, ...), custom_call_target="tpu_custom_call" | custom-call | tf_op jit(solution)/shard_map/pallas_call | solution.py:350
  (4 shorter events, 0.0 us)
Async XLA Ops:
  0.0 14.3 %collective-permute-start = (bf16[32,2048]{1,0:T(8,128)(2,1)}, bf16[32,2048]{1,0:T(8,128)(2,1)S(1)}, u32[]{:S(2)}, u32[]{:S(2)}) collective-permute-start(bf16[32,2048]{1,0:T(8,128)(2,1)} %rest_2_.3), channel_id=1, source_target_pairs={{0,8},{4,12},{8,0},{12,4},{1,9},{5,13},{9,1},{13,5},{2,10},{6,14},... | collective-permute-start | bytes 393224 | tf_op jit(solution)/shard_map/ppermute | solution.py:301
  4.1 11.8 %collective-permute-start.1 = (bf16[32,2048]{1,0:T(8,128)(2,1)}, bf16[32,2048]{1,0:T(8,128)(2,1)S(1)}, u32[]{:S(2)}, u32[]{:S(2)}) collective-permute-start(bf16[32,2048]{1,0:T(8,128)(2,1)} %rest_2_.3), channel_id=1, source_target_pairs={{0,4},{4,0},{8,12},{12,8},{1,5},{5,1},{9,13},{13,9},{2,6},{6,2},{1... | collective-permute-start | bytes 393224 | tf_op jit(solution)/shard_map/ppermute | solution.py:301
  6.5 10.9 %collective-permute-start.2 = (bf16[32,1024]{1,0:T(8,128)(2,1)S(1)}, bf16[32,1024]{1,0:T(8,128)(2,1)S(1)}, u32[]{:S(2)}, u32[]{:S(2)}) collective-permute-start(bf16[32,1024]{1,0:T(8,128)(2,1)S(1)} %get-tuple-element.42), channel_id=1, source_target_pairs={{0,12},{4,8},{8,4},{12,0},{1,13},{5,9},{9,5},{13,1},{2,14},{6,10},... | collective-permute-start | bytes 196616 | tf_op jit(solution)/shard_map/ppermute | solution.py:301
  6.6 12.9 %collective-permute-start.3 = (bf16[32,1024]{1,0:T(8,128)(2,1)S(1)}, bf16[32,1024]{1,0:T(8,128)(2,1)S(1)}, u32[]{:S(2)}, u32[]{:S(2)}) collective-permute-start(bf16[32,1024]{1,0:T(8,128)(2,1)S(1)} %get-tuple-element.41), channel_id=1, source_target_pairs={{0,12},{4,8},{8,4},{12,0},{1,13},{5,9},{9,5},{13,1},{2,14},{6,10},... | collective-permute-start | bytes 196616 | tf_op jit(solution)/shard_map/ppermute | solution.py:301
  14.4 3.1 %copy-start = (bf16[32,2048]{1,0:T(8,128)(2,1)S(1)}, bf16[32,2048]{1,0:T(8,128)(2,1)}, u32[]{:S(2)}) copy-start(bf16[32,2048]{1,0:T(8,128)(2,1)} %rest_2_.3) | copy-start | bytes 393220
  22.2 16.2 %collective-permute-start.7 = (bf16[528,128]{1,0:T(8,128)(2,1)S(1)}, bf16[528,128]{1,0:T(8,128)(2,1)S(1)}, u32[]{:S(2)}, u32[]{:S(2)}) collective-permute-start(bf16[528,128]{1,0:T(8,128)(2,1)S(1)} %shard_map.80), channel_id=1, source_target_pairs={{0,4},{4,0},{8,12},{12,8},{1,5},{5,1},{9,13},{13,9},{2,6},{6,2},{1... | collective-permute-start | bytes 405512 | tf_op jit(solution)/shard_map/ppermute | solution.py:301
  24.2 14.3 %collective-permute-start.6 = (bf16[528,128]{1,0:T(8,128)(2,1)S(1)}, bf16[528,128]{1,0:T(8,128)(2,1)S(1)}, u32[]{:S(2)}, u32[]{:S(2)}) collective-permute-start(bf16[528,128]{1,0:T(8,128)(2,1)S(1)} %shard_map.78), channel_id=1, source_target_pairs={{0,12},{4,8},{8,4},{12,0},{1,13},{5,9},{9,5},{13,1},{2,14},{6,10},... | collective-permute-start | bytes 405512 | tf_op jit(solution)/shard_map/ppermute | solution.py:301
  25.7 11.9 %collective-permute-start.5 = (bf16[272,128]{1,0:T(8,128)(2,1)S(1)}, bf16[272,128]{1,0:T(8,128)(2,1)S(1)}, u32[]{:S(2)}, u32[]{:S(2)}) collective-permute-start(bf16[272,128]{1,0:T(8,128)(2,1)S(1)} %get-tuple-element.38), channel_id=1, source_target_pairs={{0,8},{4,12},{8,0},{12,4},{1,9},{5,13},{9,1},{13,5},{2,10},{6,14},... | collective-permute-start | bytes 208904 | tf_op jit(solution)/shard_map/ppermute | solution.py:301
  27.7 10.8 %collective-permute-start.4 = (bf16[272,128]{1,0:T(8,128)(2,1)S(1)}, bf16[272,128]{1,0:T(8,128)(2,1)S(1)}, u32[]{:S(2)}, u32[]{:S(2)}) collective-permute-start(bf16[272,128]{1,0:T(8,128)(2,1)S(1)} %get-tuple-element.37), channel_id=1, source_target_pairs={{0,8},{4,12},{8,0},{12,4},{1,9},{5,13},{9,1},{13,5},{2,10},{6,14},... | collective-permute-start | bytes 208904 | tf_op jit(solution)/shard_map/ppermute | solution.py:301

commit v3 on v2

--- a/solution.py
+++ b/solution.py
@@ -112,17 +112,18 @@
 
 def own(*rest, kv_local):
     sources, rest = rest[:7], rest[7:]
-    rk_ref, rv_ref, bk_ref, bv_ref, pick_ref, bias_ref, out_ref, level_ref, score_ref, id_ref, q_ref, doc_ref, arrived = rest
-    loads = [pltpu.make_async_copy(source, target, arrived.at[n]) for n, (source, target) in enumerate(zip(sources, (id_ref, q_ref, rk_ref, doc_ref, rv_ref, bk_ref, bv_ref)))]
-    for load in loads[:5]:
+    rk_ref, rv_ref, bk_ref, bv_ref, pick_ref, bias_ref, out_ref, level_ref = rest[:8]
+    cut_refs, (score_ref, id_ref, q_ref, doc_ref, arrived) = rest[8:8 + kv_local], rest[8 + kv_local:]
+    loads = [pltpu.make_async_copy(source, target, arrived.at[n]) for n, (source, target) in enumerate(zip(sources, (doc_ref, id_ref, q_ref, rk_ref, rv_ref, bk_ref, bv_ref)))]
+    for load in loads:
         load.start()
     branch_dev, rows, most_rows = pick_ref.shape
     me = lax.axis_index("seq").astype(jnp.int32)
-    loads[3].wait()
+    loads[0].wait()
     slot = lax.broadcasted_iota(jnp.int32, (1, bias_ref.shape[1]), 1)
     for b in range(branch_dev):
         bias_ref[b:b + 1, :] = jnp.where(slot < doc_ref[me * branch_dev + b], 0.0, LOW)
-    loads[0].wait()
+    loads[1].wait()
     ids = id_ref[...]
     before = jnp.where(lax.broadcasted_iota(jnp.int32, (rows, rows), 0) < lax.broadcasted_iota(jnp.int32, (rows, rows), 1), 1.0, 0.0).astype(jnp.bfloat16)
     slot = lax.broadcasted_iota(jnp.int32, (most_rows, rows), 0).astype(jnp.float32)
@@ -132,10 +133,12 @@
         rank = dot(named.astype(jnp.bfloat16), before)
         chosen = jnp.where((rank == slot) & (named > 0.0), 1.0, 0.0).astype(jnp.bfloat16)
         pick_ref[b] = dot(chosen, unit, (((0,), (0,)), ((), ()))).astype(jnp.bfloat16)
-    for load in loads[1:3] + loads[4:5]:
+    loads[2].wait()
+    part = q_ref.shape[1] // kv_local
+    for f in range(kv_local):
+        cut_refs[f][...] = q_ref[:, f * part:(f + 1) * part]
+    for load in loads[3:5]:
         load.wait()
-    for load in loads[5:]:
-        load.start()
     pipeline(roots(lambda f: stack_heads(q_ref, f * GROUP), rk_ref, rv_ref, range(kv_local), store(out_ref, level_ref)), score_ref)
     for load in loads[5:]:
         load.wait()
@@ -145,8 +148,16 @@
     pipeline(roots(lambda f: stack_heads(q_ref, f * GROUP), rk_ref, rv_ref, range(kv_local), store(out_ref, level_ref)), score_ref)
 
 
-def picks(pick_ref, key, row_dev):
-    source = lax.axis_index("seq").astype(jnp.int32) ^ key
+def source_of(sources):
+    me = lax.axis_index("seq").astype(jnp.int32)
+    result = jnp.int32(sources[0])
+    for device in range(1, len(sources)):
+        result = jnp.where(me == device, sources[device], result)
+    return result
+
+
+def picks(pick_ref, sources, row_dev):
+    source = source_of(sources)
     at = pl.ds(pl.multiple_of(source * row_dev, row_dev), row_dev)
     return [pick_ref[b, at, :] for b in range(pick_ref.shape[0])]
 
@@ -184,10 +195,9 @@
     branch_dev, _, most_rows = pick_ref.shape
     part = rows_ref.shape[1]
     cut = slice(f * HEAD_DIM, (f + 1) * HEAD_DIM)
-    me = lax.axis_index("seq").astype(jnp.int32)
-    for k, q_ref in zip(keys, q_refs):
-        at = pl.ds(pl.multiple_of((me ^ k) * row_dev, row_dev), row_dev)
-        rows_ref[at, :] = q_ref[...] if k == keys[-1] else q_ref[:, f * part:(f + 1) * part]
+    for sources, q_ref in zip(keys, q_refs):
+        at = pl.ds(pl.multiple_of(source_of(sources) * row_dev, row_dev), row_dev)
+        rows_ref[at, :] = q_ref[...] if q_ref is q_refs[-1] else q_ref[:, f * part:(f + 1) * part]
     named = jnp.concatenate([pick_ref[b] for b in range(branch_dev)], axis=1)
     picked = dot(named, rows_ref[...], (((0,), (0,)), ((), ()))).astype(jnp.bfloat16)
     levels = []
@@ -205,11 +215,13 @@
     return [block(b) for b in range(branch_dev)]
 
 
-def branch(pick_ref, bias_ref, bk_ref, bv_ref, out_ref, level_ref, *rest, keys, f, key, kv_local):
+def branch(pick_ref, bias_ref, bk_ref, bv_ref, *rest, keys, f, key, kv_local):
+    ends = f == kv_local - 1
     branch_refs, rest = rest[:f], rest[f:]
     total_refs, rest = rest[:min(f, 1)], rest[min(f, 1):]
-    q_refs = rest[:len(keys)]
-    share_ref, branch_ref, total_ref, score_ref, rows_ref = rest[len(keys):]
+    q_refs, rest = rest[:len(keys)], rest[len(keys):]
+    given_refs, rest = (rest[:2], rest[2:]) if ends else ((), rest)
+    branch_ref, total_ref, *share_refs, score_ref, rows_ref = rest
 
     def finish(level):
         total = jnp.concatenate(pieces(level), axis=1)
@@ -218,8 +230,9 @@
         total_ref[...] = total
 
     pipeline(branch_blocks(pick_ref, bias_ref, bk_ref, bv_ref, q_refs, rows_ref, branch_ref, keys, f, finish), score_ref)
-    every = [*branch_refs, branch_ref] + [None] * (kv_local - 1 - f)
-    merge(share_ref, picks(pick_ref, key, level_ref.shape[0]), {f: out_ref[f]}, level_ref[...], every, total_ref[...])
+    if ends:
+        out_ref, level_ref = given_refs
+        merge(share_refs[0], picks(pick_ref, key, level_ref.shape[0]), {g: out_ref[g] for g in range(kv_local)}, level_ref[...], [*branch_refs, branch_ref], total_ref[...])
 
 
 def share(pick_ref, b_level_ref, rk_ref, rv_ref, *rest, key, kv_local):
@@ -236,17 +249,13 @@
     merge(share_ref, picks(pick_ref, key, level_ref.shape[0]), {f: out_ref[f] for f in range(len(branch_refs))}, level_ref[...], branch_refs, b_level_ref[...])
 
 
-def join(*refs, heads, counts):
-    out_ref = refs[-1]
+def join(*refs, heads):
+    share_refs, out_ref = refs[:-1], refs[-1]
     row_dev = out_ref.shape[0]
     half = row_dev // 2
-    groups, at = [], 0
-    for count in counts:
-        groups.append(refs[at:at + count])
-        at += count
     levels = []
-    for group in groups:
-        s = sum(ref[heads // len(group) * row_dev:, :].astype(jnp.float32) for ref in group)
+    for ref in share_refs:
+        s = ref[heads * row_dev:, :].astype(jnp.float32)
         levels.append(s + pltpu.roll(s, HEAD_DIM - heads, 1) + pltpu.roll(s, HEAD_DIM - 2 * heads, 1))
     top = functools.reduce(jnp.maximum, levels)
     parts = [jnp.exp2(x - top) for x in levels]
@@ -254,10 +263,9 @@
     parts = [x / whole for x in parts]
     for h in range(heads):
         result = None
-        for group, part in zip(groups, parts):
-            each = heads // len(group)
+        for ref, part in zip(share_refs, parts):
             factor = jnp.concatenate([spread(part, h, half), spread(part, HEAD_DIM // 2 + h, half)], axis=0)
-            term = group[h // each][h % each * row_dev:(h % each + 1) * row_dev, :].astype(jnp.float32) * factor
+            term = ref[h * row_dev:(h + 1) * row_dev, :].astype(jnp.float32) * factor
             result = term if result is None else result + term
         out_ref[:, h * HEAD_DIM:(h + 1) * HEAD_DIM] = result.astype(jnp.bfloat16)
 
@@ -297,63 +305,63 @@
     result = [f32((kv_local, block, HEAD_DIM)), f32((row_dev, HEAD_DIM))]
     payload = bf16((heads * row_dev + row_dev // 2, HEAD_DIM))
 
-    def swap(x, k):
-        return lax.ppermute(x, "seq", [(i, i ^ k) for i in range(shares)])
-
-    _, early, last, first, later = plan(shares)
-    gathered = {}
-    for k in early:
-        gathered[k] = swap(queries, k)
-    pieces_of_last = []
-    for f in range(kv_local):
-        piece = queries[:, f * part:(f + 1) * part]
-        pieces_of_last.append(swap(piece, last))
+    def move(x, targets):
+        return lax.ppermute(x, "seq", list(enumerate(targets)))
+
+    rounds = plan(shares)
+    back = [inverse(targets) for targets in rounds]
+    early, last = range(len(rounds) - 1), len(rounds) - 1
+    gathered = []
+    for n in early:
+        gathered.append(move(queries, rounds[n]))
     stored = (root_keys, root_values, branch_keys, branch_values)
     rk, rv, bk, bv, pick, bias, *mine = call(
         own,
-        [bf16(x.shape) for x in stored] + [bf16((branch_dev, rows, most_rows)), f32((branch_dev, branch_len))] + result,
+        [bf16(x.shape) for x in stored] + [bf16((branch_dev, rows, most_rows)), f32((branch_dev, branch_len))] + result + [bf16((row_dev, part))] * kv_local,
         [HBM] * 7,
         [scores, pltpu.VMEM((1, rows), jnp.int32), pltpu.VMEM((row_dev, width), jnp.bfloat16), pltpu.SMEM(doc_len.shape, jnp.int32), pltpu.SemaphoreType.DMA((7,))],
         kv_local=kv_local,
-    )(*[pltpu.with_memory_space_constraint(x, pltpu.HBM) for x in (branch_id.reshape(1, rows), queries, root_keys, doc_len, *stored[1:])])
-    ready = {0: mine}
-    for k in early:
-        ready[k] = call(root, result, [VMEM] * 3, [scores], kv_local=kv_local)(gathered[k], rk, rv)
-    keys = [0] + early + [last]
-    chunks = [queries] + [gathered[k] for k in early]
-    branch_out, totals, sent = [], [], {first: []}
+    )(*[pltpu.with_memory_space_constraint(x, pltpu.HBM) for x in (doc_len, branch_id.reshape(1, rows), queries, *stored)])
+    pieces_of_last = []
     for f in range(kv_local):
-        partial, out, total = call(
+        pieces_of_last.append(move(mine[2 + f], rounds[last]))
+    ready = []
+    for n in early:
+        ready.append(call(root, result, [VMEM] * 3, [scores], kv_local=kv_local)(gathered[n], rk, rv))
+    keys = [tuple(range(shares))] + back
+    branch_out, totals, sent = [], [], []
+    for f in range(kv_local):
+        ends = f == kv_local - 1
+        out, total, *partial = call(
             branch,
-            [bf16((block + row_dev // 2, HEAD_DIM)), bf16((slots, part)), bf16((slots, 3 * HEAD_DIM))],
-            [VMEM] * (6 + f + len(totals) + shares),
+            [bf16((slots, part)), bf16((slots, 3 * HEAD_DIM))] + [payload] * ends,
+            [VMEM] * (4 + f + len(totals) + shares + 2 * ends),
             [scores, some_rows],
             keys=keys,
             f=f,
-            key=first,
+            key=back[0],
             kv_local=kv_local,
-        )(pick, bias, bk, bv, *ready[first], *branch_out, *totals, *chunks, pieces_of_last[f])
+        )(pick, bias, bk, bv, *branch_out, *totals, queries, *gathered, pieces_of_last[f], *(ready[0] if ends else ()))
         branch_out.append(out)
         totals = [total]
-        sent[first].append(partial)
-    for k in later:
-        if k in ready:
-            partial = call(given, payload, [VMEM] * (4 + kv_local), key=k)(pick, *totals, *ready[k], *branch_out)
-        else:
-            partial = call(share, payload, [VMEM] * (4 + 2 * kv_local), [scores], key=k, kv_local=kv_local)(pick, *totals, rk, rv, *branch_out, *pieces_of_last)
-        sent[k] = [partial]
-    received, counts = [*sent[0]], [1]
-    for k in [first] + later[:-1]:
-        for partial in sent[k]:
-            received.append(swap(partial, k))
-        counts.append(len(sent[k]))
-    return call(join, bf16((row_dev, width)), [VMEM] * len(received), heads=heads, counts=counts)(*received)
+    sent = partial
+    for n in early[1:]:
+        sent.append(call(given, payload, [VMEM] * (4 + kv_local), key=back[n])(pick, *totals, *ready[n], *branch_out))
+    sent.append(call(share, payload, [VMEM] * (4 + 2 * kv_local), [scores], key=back[last], kv_local=kv_local)(pick, *totals, rk, rv, *branch_out, *pieces_of_last))
+    received = [call(given, payload, [VMEM] * (4 + kv_local), key=keys[0])(pick, *totals, *mine[:2], *branch_out)]
+    for n, partial in enumerate(sent):
+        received.append(move(partial, back[n]))
+    return call(join, bf16((row_dev, width)), [VMEM] * shares, heads=heads)(*received)
+
+
+def inverse(targets):
+    return tuple(targets.index(device) for device in range(len(targets)))
 
 
 def plan(shares):
-    order = list(range(1, shares))
-    order = [shares // 2] + [k for k in order if k != shares // 2]
-    return order, order[:-1], order[-1], order[0], [order[-1]] + order[1:-1] + [0]
+    if shares == 4:
+        return [(2, 0, 3, 1), (1, 3, 0, 2), (3, 2, 1, 0)]
+    return [tuple(device ^ k for device in range(shares)) for k in range(1, shares)]
 
 
 def solution(mesh):

time: 39.9 us -> 35.9 us (0.90)
  starting transfers between devices: 14.1 us -> 11.7 us
  Pallas kernels: 15.4 us -> 14.4 us
  local copies, waits for them, and re-layouts: 0.89 us -> 0.01 us
    ppermute x8 -> x7, starting transfers between devices: 14.1 us -> 11.7 us  [move(): return lax.ppermute(x, 'seq', list(enumerate(targets)))]
    slice x1 -> x0, local copies, waits for them, and re-layouts: 0.88 us -> none  [body(): piece = queries[:, f * part:(f + 1) * part]]
    pallas_call x1, Pallas kernels: 3.92 us -> 3.2 us  [body(): call(own, [bf16(x.shape) for x in stored] + [bf16((branch_dev, rows, most...]
    ppermute x8 -> x7, waiting for transfers between devices: 9.26 us -> 9.55 us  [move(): return lax.ppermute(x, 'seq', list(enumerate(targets)))]
  transfers between devices with their start and end apart: 8 -> 7, of which waited for: 2 -> 6; matrix products, arithmetic and copies ran while one was open for 2% -> 0% of each run, Pallas kernels for 29% -> 25%
where the time goes in v3:
time: 35.9 us; the launch traced here: 35.7 us
  Pallas kernels  14.4 us (40%)
  starting transfers between devices  11.7 us (33%)
  waiting for transfers between devices  9.55 us (27%)
    ppermute x7, starting transfers between devices, move(): return lax.ppermute(x, 'seq', list(enumerate(targets)))  11.7 us
    ppermute x7, waiting for transfers between devices, move(): return lax.ppermute(x, 'seq', list(enumerate(targets)))  9.55 us
    pallas_call x2, Pallas kernels, body(): call(branch, [bf16((slots, part)), bf16((slots, 3 * HEAD_DIM))] + [payloa...  3.97 us
    pallas_call x1, Pallas kernels, body(): call(own, [bf16(x.shape) for x in stored] + [bf16((branch_dev, rows, most...  3.2 us
    pallas_call x2, Pallas kernels, body(): call(root, result, [VMEM] * 3, [scores], kv_local=kv_local)  3.01 us
    pallas_call x1, Pallas kernels, body(): call(share, payload, [VMEM] * (4 + 2 * kv_local), [scores], key=back[last...  1.9 us
    pallas_call x1, Pallas kernels, body(): call(join, bf16((row_dev, width)), [VMEM] * shares, heads=heads)(*received)  1.23 us
  transfers between devices with their start and end apart: 7, of which 6 were waited for; matrix products, arithmetic and copies ran while one was open for 0% of the time, Pallas kernels for 25%

profile of v3, /device:TPU:0, one launch (start us, length us, event | category | flops | bytes accessed | tf_op | source)
XLA Modules:
  0.0 35.7 jit_solution(2684346600530457269)
XLA Ops:
  0.0 4.1 %collective-permute-start = (bf16[32,2048]{1,0:T(8,128)(2,1)}, bf16[32,2048]{1,0:T(8,128)(2,1)S(1)}, u32[]{:S(2)}, u32[]{:S(2)}) collective-permute-start(bf16[32,2048]{1,0:T(8,128)(2,1)} %rest_2_.3), channel_id=1, source_target_pairs={{0,8},{4,0},{8,12},{12,4},{1,9},{5,1},{9,13},{13,5},{2,10},{6,2},{... | collective-permute-start | bytes 393224 | tf_op jit(solution)/shard_map/ppermute | solution.py:309
  4.1 0.0 collective-permute-start.1
  4.1 3.2 %shard_map.73 = (bf16[2048,256]{1,0:T(8,128)(2,1)S(1)}, bf16[2048,256]{1,0:T(8,128)(2,1)S(1)}, bf16[2,2048,256]{2,1,0:T(8,128)(2,1)S(1)}, bf16[2,2048,256]{2,1,0...) custom-call(s32[8]{0:T(128)} %rest_0_.2, ...), custom_call_target="tpu_custom_call" | custom-call | tf_op jit(solution)/shard_map/pallas_call | solution.py:318
  7.3 0.0 copy-start
  7.3 3.1 %collective-permute-start.2 = (bf16[32,1024]{1,0:T(8,128)(2,1)S(1)}, bf16[32,1024]{1,0:T(8,128)(2,1)S(1)}, u32[]{:S(2)}, u32[]{:S(2)}) collective-permute-start(bf16[32,1024]{1,0:T(8,128)(2,1)S(1)} %get-tuple-element.28), channel_id=1, source_target_pairs={{0,12},{4,8},{8,4},{12,0},{1,13},{5,9},{9,5},{13,1},{2,14},{6,10},... | collective-permute-start | bytes 196616 | tf_op jit(solution)/shard_map/ppermute | solution.py:309
  10.4 0.8 %collective-permute-start.3 = (bf16[32,1024]{1,0:T(8,128)(2,1)S(1)}, bf16[32,1024]{1,0:T(8,128)(2,1)S(1)}, u32[]{:S(2)}, u32[]{:S(2)}) collective-permute-start(bf16[32,1024]{1,0:T(8,128)(2,1)S(1)} %get-tuple-element.31), channel_id=1, source_target_pairs={{0,12},{4,8},{8,4},{12,0},{1,13},{5,9},{9,5},{13,1},{2,14},{6,10},... | collective-permute-start | bytes 196616 | tf_op jit(solution)/shard_map/ppermute | solution.py:309
  11.2 0.0 collective-permute-done.rest_1_.q_ref.rest_3_
  11.2 1.5 %shard_map.75 = (f32[2,256,128]{2,1,0:T(8,128)S(1)}, f32[32,128]{1,0:T(8,128)S(1)}) custom-call(bf16[32,2048]{1,0:T(8,128)(2,1)S(1)} %collective-permute-done.rest_1_.q_ref.rest_3_, bf16[2048,256]{1,0:T(8,128)(2,1)S(1)} %get-tuple-element.32.rk_ref, bf16[2048,256]{1,0:T(8,128)(2,1)S(1)} %get-tuple-element.33.rv_ref), custom_call_target="tpu_custom_call" | custom-call | tf_op jit(solution)/shard_map/pallas_call | solution.py:330
  12.7 0.7 %collective-permute-done.2.rest_3_.rest_2_ = bf16[32,1024]{1,0:T(8,128)(2,1)S(1)} collective-permute-done((bf16[32,1024]{1,0:T(8,128)(2,1)S(1)}, bf16[32,1024]{1,0:T(8,128)(2,1)S(1)}, u32[]{:S(2)}, u32[]{:S(2)}) %collective-permute-start.2) | collective-permute-done | bytes 65568 | tf_op jit(solution)/shard_map/ppermute | solution.py:309
  13.4 0.1 collective-permute-done.1.rest_2_.rest_4_.q_ref
  13.6 1.7 %shard_map.74 = (bf16[64,1024]{1,0:T(8,128)(2,1)S(1)}, bf16[64,384]{1,0:T(8,128)(2,1)S(1)}) custom-call(bf16[2,128,32]{2,1,0:T(8,128)(2,1)S(1)} %get-tuple-element.24.pick_ref, f32[2,2048]{1,0:T(2,128)S(1)} %get-tuple-element.25.bias_ref, bf16[2,2048,256]{2,1,0:T(8,128)(2,1)S(1)} %get-tuple-element.26.bk_ref, ...), custom_call_target="tpu_custom_call" | custom-call | tf_op jit(solution)/shard_map/pallas_call | solution.py:335
  15.3 1.2 %collective-permute-done.3.rest_5_.rest_3_ = bf16[32,1024]{1,0:T(8,128)(2,1)S(1)} collective-permute-done((bf16[32,1024]{1,0:T(8,128)(2,1)S(1)}, bf16[32,1024]{1,0:T(8,128)(2,1)S(1)}, u32[]{:S(2)}, u32[]{:S(2)}) %collective-permute-start.3) | collective-permute-done | bytes 65568 | tf_op jit(solution)/shard_map/ppermute | solution.py:309
  16.6 2.2 %shard_map.76 = (bf16[64,1024]{1,0:T(8,128)(2,1)S(1)}, bf16[64,384]{1,0:T(8,128)(2,1)S(1)}, bf16[528,128]{1,0:T(8,128)(2,1)S(1)}) custom-call(bf16[2,128,32]{2,1,0:T(8,128)(2,1)S(1)} %get-tuple-element.24.pick_ref, f32[2,2048]{1,0:T(2,128)S(1)} %get-tuple-element.25.bias_ref, bf16[2,2048,256]{2,1,0:T(8,128)(2,1)S(1)} %get-tuple-element.26.bk_ref, ...), custom_call_target="tpu_custom_call" | custom-call | tf_op jit(solution)/shard_map/pallas_call | solution.py:335
  18.8 1.9 %shard_map.80 = bf16[528,128]{1,0:T(8,128)(2,1)S(1)} custom-call(bf16[2,128,32]{2,1,0:T(8,128)(2,1)S(1)} %get-tuple-element.24.pick_ref, bf16[64,384]{1,0:T(8,128)(2,1)S(1)} %get-tuple-element.36.b_level_ref, bf16[2048,256]{1,0:T(8,128)(2,1)S(1)} %get-tuple-element.32.rk_ref, bf16[2048,256]{1,0:T(8,128)(2,1)S(1)} %get-tuple-element.33.rv_ref, ...), custom_call_target="tpu_custom_call" | custom-call | tf_op jit(solution)/shard_map/pallas_call | solution.py:350
  20.7 1.7 %collective-permute-start.6 = (bf16[528,128]{1,0:T(8,128)(2,1)S(1)}, bf16[528,128]{1,0:T(8,128)(2,1)S(1)}, u32[]{:S(2)}, u32[]{:S(2)}) collective-permute-start(bf16[528,128]{1,0:T(8,128)(2,1)S(1)} %shard_map.80), channel_id=1, source_target_pairs={{0,12},{4,8},{8,4},{12,0},{1,13},{5,9},{9,5},{13,1},{2,14},{6,10},... | collective-permute-start | bytes 405512 | tf_op jit(solution)/shard_map/ppermute | solution.py:309
  22.4 1.5 %shard_map.78 = (f32[2,256,128]{2,1,0:T(8,128)S(1)}, f32[32,128]{1,0:T(8,128)S(1)}) custom-call(bf16[32,2048]{1,0:T(8,128)(2,1)S(1)} %collective-permute-done.1.rest_2_.rest_4_.q_ref, bf16[2048,256]{1,0:T(8,128)(2,1)S(1)} %get-tuple-element.32.rk_ref, bf16[2048,256]{1,0:T(8,128)(2,1)S(1)} %get-tuple-element.33.rv_ref), custom_call_target="tpu_custom_call" | custom-call | tf_op jit(solution)/shard_map/pallas_call | solution.py:330
  23.9 0.5 %shard_map.79 = bf16[528,128]{1,0:T(8,128)(2,1)S(1)} custom-call(bf16[2,128,32]{2,1,0:T(8,128)(2,1)S(1)} %get-tuple-element.24.pick_ref, bf16[64,384]{1,0:T(8,128)(2,1)S(1)} %get-tuple-element.36.b_level_ref, f32[2,256,128]{2,1,0:T(8,128)S(1)} %get-tuple-element.41.out_ref, f32[32,128]{1,0:T(8,128)S(1)} %get-tuple-element.42.level_ref, ...), custom_call_target="tpu_custom_call" | custom-call | tf_op jit(solution)/shard_map/pallas_call | solution.py:349
  24.5 1.3 %collective-permute-start.5 = (bf16[528,128]{1,0:T(8,128)(2,1)S(1)}, bf16[528,128]{1,0:T(8,128)(2,1)S(1)}, u32[]{:S(2)}, u32[]{:S(2)}) collective-permute-start(bf16[528,128]{1,0:T(8,128)(2,1)S(1)} %shard_map.79), channel_id=1, source_target_pairs={{0,8},{4,0},{8,12},{12,4},{1,9},{5,1},{9,13},{13,5},{2,10},{6,2},{... | collective-permute-start | bytes 405512 | tf_op jit(solution)/shard_map/ppermute | solution.py:309
  25.7 0.8 %collective-permute-start.4 = (bf16[528,128]{1,0:T(8,128)(2,1)S(1)}, bf16[528,128]{1,0:T(8,128)(2,1)S(1)}, u32[]{:S(2)}, u32[]{:S(2)}) collective-permute-start(bf16[528,128]{1,0:T(8,128)(2,1)S(1)} %get-tuple-element.40), channel_id=1, source_target_pairs={{0,4},{4,12},{8,0},{12,8},{1,5},{5,13},{9,1},{13,9},{2,6},{6,14},{... | collective-permute-start | bytes 405512 | tf_op jit(solution)/shard_map/ppermute | solution.py:309
  26.5 0.5 %shard_map.77.refs_0_ = bf16[528,128]{1,0:T(8,128)(2,1)S(1)} custom-call(bf16[2,128,32]{2,1,0:T(8,128)(2,1)S(1)} %get-tuple-element.24.pick_ref, bf16[64,384]{1,0:T(8,128)(2,1)S(1)} %get-tuple-element.36.b_level_ref, f32[2,256,128]{2,1,0:T(8,128)S(1)} %get-tuple-element.37.out_ref, f32[32,128]{1,0:T(8,128)S(1)} %get-tuple-element.38.level_ref, ...), custom_call_target="tpu_custom_call" | custom-call | tf_op jit(solution)/shard_map/pallas_call | solution.py:351
  27.0 0.7 %collective-permute-done.6.refs_3_ = bf16[528,128]{1,0:T(8,128)(2,1)S(1)} collective-permute-done((bf16[528,128]{1,0:T(8,128)(2,1)S(1)}, bf16[528,128]{1,0:T(8,128)(2,1)S(1)}, u32[]{:S(2)}, u32[]{:S(2)}) %collective-permute-start.6) | collective-permute-done | bytes 135200 | tf_op jit(solution)/shard_map/ppermute | solution.py:309
  27.8 3.1 %collective-permute-done.5.refs_2_ = bf16[528,128]{1,0:T(8,128)(2,1)S(1)} collective-permute-done((bf16[528,128]{1,0:T(8,128)(2,1)S(1)}, bf16[528,128]{1,0:T(8,128)(2,1)S(1)}, u32[]{:S(2)}, u32[]{:S(2)}) %collective-permute-start.5) | collective-permute-done | bytes 135200 | tf_op jit(solution)/shard_map/ppermute | solution.py:309
  30.9 3.6 %collective-permute-done.4.refs_1_ = bf16[528,128]{1,0:T(8,128)(2,1)S(1)} collective-permute-done((bf16[528,128]{1,0:T(8,128)(2,1)S(1)}, bf16[528,128]{1,0:T(8,128)(2,1)S(1)}, u32[]{:S(2)}, u32[]{:S(2)}) %collective-permute-start.4) | collective-permute-done | bytes 135200 | tf_op jit(solution)/shard_map/ppermute | solution.py:309
  34.5 1.2 %shard_map.81 = bf16[32,2048]{1,0:T(8,128)(2,1)} custom-call(bf16[528,128]{1,0:T(8,128)(2,1)S(1)} %shard_map.77.refs_0_, bf16[528,128]{1,0:T(8,128)(2,1)S(1)} %collective-permute-done.4.refs_1_, bf16[528,128]{1,0:T(8,128)(2,1)S(1)} %collective-permute-done.5.refs_2_, bf16[528,128]{1,0:T(8,128)(2,1)S(1)} %collective-permute-done.6.refs_3_), custom_call_target="tpu_custom_call" | custom-call | tf_op jit(solution)/shard_map/pallas_call | solution.py:354
  (1 shorter events, 0.0 us)
Async XLA Ops:
  0.0 11.2 %collective-permute-start = (bf16[32,2048]{1,0:T(8,128)(2,1)}, bf16[32,2048]{1,0:T(8,128)(2,1)S(1)}, u32[]{:S(2)}, u32[]{:S(2)}) collective-permute-start(bf16[32,2048]{1,0:T(8,128)(2,1)} %rest_2_.3), channel_id=1, source_target_pairs={{0,8},{4,0},{8,12},{12,4},{1,9},{5,1},{9,13},{13,5},{2,10},{6,2},{... | collective-permute-start | bytes 393224 | tf_op jit(solution)/shard_map/ppermute | solution.py:309
  4.1 9.5 %collective-permute-start.1 = (bf16[32,2048]{1,0:T(8,128)(2,1)}, bf16[32,2048]{1,0:T(8,128)(2,1)S(1)}, u32[]{:S(2)}, u32[]{:S(2)}) collective-permute-start(bf16[32,2048]{1,0:T(8,128)(2,1)} %rest_2_.3), channel_id=1, source_target_pairs={{0,4},{4,12},{8,0},{12,8},{1,5},{5,13},{9,1},{13,9},{2,6},{6,14},{... | collective-permute-start | bytes 393224 | tf_op jit(solution)/shard_map/ppermute | solution.py:309
  7.3 6.3 %copy-start = (bf16[32,2048]{1,0:T(8,128)(2,1)S(1)}, bf16[32,2048]{1,0:T(8,128)(2,1)}, u32[]{:S(2)}) copy-start(bf16[32,2048]{1,0:T(8,128)(2,1)} %rest_2_.3) | copy-start | bytes 393220
  7.3 6.1 %collective-permute-start.2 = (bf16[32,1024]{1,0:T(8,128)(2,1)S(1)}, bf16[32,1024]{1,0:T(8,128)(2,1)S(1)}, u32[]{:S(2)}, u32[]{:S(2)}) collective-permute-start(bf16[32,1024]{1,0:T(8,128)(2,1)S(1)} %get-tuple-element.28), channel_id=1, source_target_pairs={{0,12},{4,8},{8,4},{12,0},{1,13},{5,9},{9,5},{13,1},{2,14},{6,10},... | collective-permute-start | bytes 196616 | tf_op jit(solution)/shard_map/ppermute | solution.py:309
  10.4 6.2 %collective-permute-start.3 = (bf16[32,1024]{1,0:T(8,128)(2,1)S(1)}, bf16[32,1024]{1,0:T(8,128)(2,1)S(1)}, u32[]{:S(2)}, u32[]{:S(2)}) collective-permute-start(bf16[32,1024]{1,0:T(8,128)(2,1)S(1)} %get-tuple-element.31), channel_id=1, source_target_pairs={{0,12},{4,8},{8,4},{12,0},{1,13},{5,9},{9,5},{13,1},{2,14},{6,10},... | collective-permute-start | bytes 196616 | tf_op jit(solution)/shard_map/ppermute | solution.py:309
  20.7 7.1 %collective-permute-start.6 = (bf16[528,128]{1,0:T(8,128)(2,1)S(1)}, bf16[528,128]{1,0:T(8,128)(2,1)S(1)}, u32[]{:S(2)}, u32[]{:S(2)}) collective-permute-start(bf16[528,128]{1,0:T(8,128)(2,1)S(1)} %shard_map.80), channel_id=1, source_target_pairs={{0,12},{4,8},{8,4},{12,0},{1,13},{5,9},{9,5},{13,1},{2,14},{6,10},... | collective-permute-start | bytes 405512 | tf_op jit(solution)/shard_map/ppermute | solution.py:309
  24.5 6.4 %collective-permute-start.5 = (bf16[528,128]{1,0:T(8,128)(2,1)S(1)}, bf16[528,128]{1,0:T(8,128)(2,1)S(1)}, u32[]{:S(2)}, u32[]{:S(2)}) collective-permute-start(bf16[528,128]{1,0:T(8,128)(2,1)S(1)} %shard_map.79), channel_id=1, source_target_pairs={{0,8},{4,0},{8,12},{12,4},{1,9},{5,1},{9,13},{13,5},{2,10},{6,2},{... | collective-permute-start | bytes 405512 | tf_op jit(solution)/shard_map/ppermute | solution.py:309
  25.7 8.7 %collective-permute-start.4 = (bf16[528,128]{1,0:T(8,128)(2,1)S(1)}, bf16[528,128]{1,0:T(8,128)(2,1)S(1)}, u32[]{:S(2)}, u32[]{:S(2)}) collective-permute-start(bf16[528,128]{1,0:T(8,128)(2,1)S(1)} %get-tuple-element.40), channel_id=1, source_target_pairs={{0,4},{4,12},{8,0},{12,8},{1,5},{5,13},{9,1},{13,9},{2,6},{6,14},{... | collective-permute-start | bytes 405512 | tf_op jit(solution)/shard_map/ppermute | solution.py:309

commit v4 on v3

--- a/solution.py
+++ b/solution.py
@@ -110,11 +110,8 @@
     return finish
 
 
-def own(*rest, kv_local):
-    sources, rest = rest[:7], rest[7:]
-    rk_ref, rv_ref, bk_ref, bv_ref, pick_ref, bias_ref, out_ref, level_ref = rest[:8]
-    cut_refs, (score_ref, id_ref, q_ref, doc_ref, arrived) = rest[8:8 + kv_local], rest[8 + kv_local:]
-    loads = [pltpu.make_async_copy(source, target, arrived.at[n]) for n, (source, target) in enumerate(zip(sources, (doc_ref, id_ref, q_ref, rk_ref, rv_ref, bk_ref, bv_ref)))]
+def own(doc_hbm, id_hbm, rk_hbm, rv_hbm, bk_hbm, rk_ref, rv_ref, bk_ref, pick_ref, bias_ref, id_ref, doc_ref, arrived):
+    loads = [pltpu.make_async_copy(source, target, arrived.at[n]) for n, (source, target) in enumerate(zip((doc_hbm, id_hbm, rk_hbm, rv_hbm, bk_hbm), (doc_ref, id_ref, rk_ref, rv_ref, bk_ref)))]
     for load in loads:
         load.start()
     branch_dev, rows, most_rows = pick_ref.shape
@@ -133,15 +130,15 @@
         rank = dot(named.astype(jnp.bfloat16), before)
         chosen = jnp.where((rank == slot) & (named > 0.0), 1.0, 0.0).astype(jnp.bfloat16)
         pick_ref[b] = dot(chosen, unit, (((0,), (0,)), ((), ()))).astype(jnp.bfloat16)
-    loads[2].wait()
-    part = q_ref.shape[1] // kv_local
-    for f in range(kv_local):
-        cut_refs[f][...] = q_ref[:, f * part:(f + 1) * part]
-    for load in loads[3:5]:
+    for load in loads[2:]:
         load.wait()
-    pipeline(roots(lambda f: stack_heads(q_ref, f * GROUP), rk_ref, rv_ref, range(kv_local), store(out_ref, level_ref)), score_ref)
-    for load in loads[5:]:
-        load.wait()
+
+
+def root_load(q_ref, rk_ref, rv_ref, bv_hbm, out_ref, level_ref, bv_ref, score_ref, arrived, *, kv_local):
+    load = pltpu.make_async_copy(bv_hbm, bv_ref, arrived)
+    load.start()
+    root(q_ref, rk_ref, rv_ref, out_ref, level_ref, score_ref, kv_local=kv_local)
+    load.wait()
 
 
 def root(q_ref, rk_ref, rv_ref, out_ref, level_ref, score_ref, *, kv_local):
@@ -162,8 +159,9 @@
     return [pick_ref[b, at, :] for b in range(pick_ref.shape[0])]
 
 
-def merge(share_ref, pick, outputs, level, branch_refs, b_level):
+def merge(share_ref, pick, outputs, level, branch_ref, b_level):
     row_dev = level.shape[0]
+    heads = len(outputs) * GROUP
     pick = jnp.concatenate(pick, axis=1)
     has = jnp.sum(pick.astype(jnp.float32), axis=1, keepdims=True) > 0.0
     found = dot(pick, b_level)
@@ -172,81 +170,68 @@
     ours, theirs = jnp.exp2(level - top), jnp.exp2(b_level - top)
     both = ours + theirs
     ours, theirs = ours / both, theirs / both
-    for n, (f, output) in enumerate(outputs.items()):
-        b_out = dot(pick, branch_refs[f][...])
+    b_out = dot(pick, branch_ref[...])
+    for f, output in enumerate(outputs):
         for g in range(GROUP):
             h = f * GROUP + g
-            at = (n * GROUP + g) * row_dev
             ahead = output[g * row_dev:(g + 1) * row_dev, :] * spread(ours, h, row_dev)
-            share_ref[at:at + row_dev, :] = (ahead + b_out[:, g * HEAD_DIM:(g + 1) * HEAD_DIM] * spread(theirs, h, row_dev)).astype(jnp.bfloat16)
+            share_ref[h * row_dev:(h + 1) * row_dev, :] = (ahead + b_out[:, h * HEAD_DIM:(h + 1) * HEAD_DIM] * spread(theirs, h, row_dev)).astype(jnp.bfloat16)
+    write_level(share_ref, top + jnp.log2(both), heads)
+
+
+def write_level(share_ref, level, heads):
+    row_dev = level.shape[0]
     lane = lax.broadcasted_iota(jnp.int32, (row_dev, HEAD_DIM), 1)
-    here = functools.reduce(jnp.logical_or, [(lane >= f * GROUP) & (lane < (f + 1) * GROUP) for f in outputs])
-    stat = jnp.where(here, top + jnp.log2(both), 0.0)
-    heads = len(branch_refs) * GROUP
+    stat = jnp.where(lane < heads, level, 0.0)
     stat = stat + pltpu.roll(stat, heads, 1) + pltpu.roll(stat, 2 * heads, 1)
     hi, mid, low = [piece.astype(jnp.float32) for piece in pieces(stat)]
     packed = jnp.where(lane < heads, hi, jnp.where(lane < 2 * heads, mid, low))
     half = row_dev // 2
-    share_ref[len(outputs) * GROUP * row_dev:, :] = (packed[:half] + pltpu.roll(packed[half:], HEAD_DIM // 2, 1)).astype(jnp.bfloat16)
-
-
-def branch_blocks(pick_ref, bias_ref, bk_ref, bv_ref, q_refs, rows_ref, branch_ref, keys, f, finish):
-    row_dev = q_refs[0].shape[0]
+    share_ref[heads * row_dev:, :] = (packed[:half] + pltpu.roll(packed[half:], HEAD_DIM // 2, 1)).astype(jnp.bfloat16)
+
+
+def branch(pick_ref, bias_ref, bk_ref, bv_ref, out_ref, level_ref, *rest, keys, direct, kv_local):
+    q_refs, last_refs, rest = rest[:len(keys) - 1], rest[len(keys) - 1:-6], rest[-6:]
+    share_ref, branch_ref, total_ref, last_ref, score_ref, rows_ref = rest
+    row_dev, width = q_refs[0].shape
     branch_dev, _, most_rows = pick_ref.shape
-    part = rows_ref.shape[1]
-    cut = slice(f * HEAD_DIM, (f + 1) * HEAD_DIM)
-    for sources, q_ref in zip(keys, q_refs):
+    part = width // kv_local
+    last = last_refs[0][...]
+    if len(last_refs) > 1:
+        last = jnp.where(source_of(direct) == 1, last, last_refs[1][...])
+    last_ref[...] = last
+    for sources, q_ref in zip(keys, [*q_refs, last_ref]):
         at = pl.ds(pl.multiple_of(source_of(sources) * row_dev, row_dev), row_dev)
-        rows_ref[at, :] = q_ref[...] if q_ref is q_refs[-1] else q_ref[:, f * part:(f + 1) * part]
+        rows_ref[at, :] = q_ref[...]
     named = jnp.concatenate([pick_ref[b] for b in range(branch_dev)], axis=1)
     picked = dot(named, rows_ref[...], (((0,), (0,)), ((), ()))).astype(jnp.bfloat16)
-    levels = []
-
-    def block(b):
+    levels = [{} for _ in range(branch_dev)]
+
+    def block(b, f):
+        cut = slice(f * HEAD_DIM, (f + 1) * HEAD_DIM)
+
         def done(output, level):
             for h in range(GROUP):
-                branch_ref[b * most_rows:(b + 1) * most_rows, h * HEAD_DIM:(h + 1) * HEAD_DIM] = output[h * most_rows:(h + 1) * most_rows].astype(jnp.bfloat16)
-            levels.append(compact({f: level}))
-            if len(levels) == branch_dev:
-                finish(jnp.concatenate(levels, axis=0))
-
-        return (lambda: stack_heads(picked[b * most_rows:(b + 1) * most_rows]), lambda at: bk_ref[b, at, cut], lambda at: bv_ref[b, at, cut], lambda at: bias_ref[b:b + 1, at], bk_ref.shape[1], done)
-
-    return [block(b) for b in range(branch_dev)]
-
-
-def branch(pick_ref, bias_ref, bk_ref, bv_ref, *rest, keys, f, key, kv_local):
-    ends = f == kv_local - 1
-    branch_refs, rest = rest[:f], rest[f:]
-    total_refs, rest = rest[:min(f, 1)], rest[min(f, 1):]
-    q_refs, rest = rest[:len(keys)], rest[len(keys):]
-    given_refs, rest = (rest[:2], rest[2:]) if ends else ((), rest)
-    branch_ref, total_ref, *share_refs, score_ref, rows_ref = rest
-
-    def finish(level):
-        total = jnp.concatenate(pieces(level), axis=1)
-        for ref in total_refs:
-            total = total + ref[...]
-        total_ref[...] = total
-
-    pipeline(branch_blocks(pick_ref, bias_ref, bk_ref, bv_ref, q_refs, rows_ref, branch_ref, keys, f, finish), score_ref)
-    if ends:
-        out_ref, level_ref = given_refs
-        merge(share_refs[0], picks(pick_ref, key, level_ref.shape[0]), {g: out_ref[g] for g in range(kv_local)}, level_ref[...], [*branch_refs, branch_ref], total_ref[...])
-
-
-def share(pick_ref, b_level_ref, rk_ref, rv_ref, *rest, key, kv_local):
-    branch_refs, q_refs, share_ref, score_ref = rest[:kv_local], rest[kv_local:2 * kv_local], rest[-2], rest[-1]
-
+                at = slice(f * part + h * HEAD_DIM, f * part + (h + 1) * HEAD_DIM)
+                branch_ref[b * most_rows:(b + 1) * most_rows, at] = output[h * most_rows:(h + 1) * most_rows].astype(jnp.bfloat16)
+            levels[b][f] = level
+
+        return (lambda: stack_heads(picked[b * most_rows:(b + 1) * most_rows], f * GROUP), lambda at: bk_ref[b, at, cut], lambda at: bv_ref[b, at, cut], lambda at: bias_ref[b:b + 1, at], bk_ref.shape[1], done)
+
+    pipeline([block(b, f) for b in range(branch_dev) for f in range(kv_local)], score_ref)
+    total_ref[...] = jnp.concatenate(pieces(jnp.concatenate([compact(level) for level in levels], axis=0)), axis=1)
+    merge(share_ref, picks(pick_ref, keys[1], row_dev), [out_ref[f] for f in range(kv_local)], level_ref[...], branch_ref, total_ref[...])
+
+
+def share(pick_ref, b_level_ref, rk_ref, rv_ref, branch_ref, q_ref, share_ref, score_ref, *, key, kv_local):
     def finish(outputs, level):
-        merge(share_ref, picks(pick_ref, key, level.shape[0]), outputs, level, branch_refs, b_level_ref[...])
-
-    pipeline(roots(lambda f: stack_heads(q_refs[f]), rk_ref, rv_ref, range(kv_local), finish), score_ref)
-
-
-def given(pick_ref, b_level_ref, out_ref, level_ref, *rest, key):
-    branch_refs, share_ref = rest[:-1], rest[-1]
-    merge(share_ref, picks(pick_ref, key, level_ref.shape[0]), {f: out_ref[f] for f in range(len(branch_refs))}, level_ref[...], branch_refs, b_level_ref[...])
+        merge(share_ref, picks(pick_ref, key, level.shape[0]), list(outputs.values()), level, branch_ref, b_level_ref[...])
+
+    pipeline(roots(lambda f: stack_heads(q_ref, f * GROUP), rk_ref, rv_ref, range(kv_local), finish), score_ref)
+
+
+def given(pick_ref, b_level_ref, out_ref, level_ref, branch_ref, share_ref, *, key):
+    merge(share_ref, picks(pick_ref, key, level_ref.shape[0]), [out_ref[f] for f in range(out_ref.shape[0])], level_ref[...], branch_ref, b_level_ref[...])
 
 
 def join(*refs, heads):
@@ -306,62 +291,61 @@
     payload = bf16((heads * row_dev + row_dev // 2, HEAD_DIM))
 
     def move(x, targets):
-        return lax.ppermute(x, "seq", list(enumerate(targets)))
-
-    rounds = plan(shares)
+        return lax.ppermute(x, "seq", [(i, target) for i, target in enumerate(targets) if target is not None])
+
+    rounds, relay = plan(shares)
     back = [inverse(targets) for targets in rounds]
     early, last = range(len(rounds) - 1), len(rounds) - 1
     gathered = []
     for n in early:
         gathered.append(move(queries, rounds[n]))
-    stored = (root_keys, root_values, branch_keys, branch_values)
-    rk, rv, bk, bv, pick, bias, *mine = call(
+    at_last = [move(queries, relay[0] if relay else rounds[last])]
+    if relay:
+        at_last.append(move(gathered[0], relay[1]))
+    in_hbm = [pltpu.with_memory_space_constraint(x, pltpu.HBM) for x in (doc_len, branch_id.reshape(1, rows), root_keys, root_values, branch_keys, branch_values)]
+    rk, rv, bk, pick, bias = call(
         own,
-        [bf16(x.shape) for x in stored] + [bf16((branch_dev, rows, most_rows)), f32((branch_dev, branch_len))] + result + [bf16((row_dev, part))] * kv_local,
-        [HBM] * 7,
-        [scores, pltpu.VMEM((1, rows), jnp.int32), pltpu.VMEM((row_dev, width), jnp.bfloat16), pltpu.SMEM(doc_len.shape, jnp.int32), pltpu.SemaphoreType.DMA((7,))],
-        kv_local=kv_local,
-    )(*[pltpu.with_memory_space_constraint(x, pltpu.HBM) for x in (doc_len, branch_id.reshape(1, rows), queries, *stored)])
-    pieces_of_last = []
-    for f in range(kv_local):
-        pieces_of_last.append(move(mine[2 + f], rounds[last]))
+        [bf16(x.shape) for x in (root_keys, root_values, branch_keys)] + [bf16((branch_dev, rows, most_rows)), f32((branch_dev, branch_len))],
+        [HBM] * 5,
+        [pltpu.VMEM((1, rows), jnp.int32), pltpu.SMEM(doc_len.shape, jnp.int32), pltpu.SemaphoreType.DMA((5,))],
+    )(*in_hbm[:5])
     ready = []
     for n in early:
-        ready.append(call(root, result, [VMEM] * 3, [scores], kv_local=kv_local)(gathered[n], rk, rv))
+        if n == 0:
+            *first, bv = call(
+                root_load, result + [bf16(branch_values.shape)], [VMEM] * 3 + [HBM], [scores, pltpu.SemaphoreType.DMA(())], kv_local=kv_local
+            )(gathered[n], rk, rv, in_hbm[5])
+            ready.append(first)
+        else:
+            ready.append(call(root, result, [VMEM] * 3, [scores], kv_local=kv_local)(gathered[n], rk, rv))
     keys = [tuple(range(shares))] + back
-    branch_out, totals, sent = [], [], []
-    for f in range(kv_local):
-        ends = f == kv_local - 1
-        out, total, *partial = call(
-            branch,
-            [bf16((slots, part)), bf16((slots, 3 * HEAD_DIM))] + [payload] * ends,
-            [VMEM] * (4 + f + len(totals) + shares + 2 * ends),
-            [scores, some_rows],
-            keys=keys,
-            f=f,
-            key=back[0],
-            kv_local=kv_local,
-        )(pick, bias, bk, bv, *branch_out, *totals, queries, *gathered, pieces_of_last[f], *(ready[0] if ends else ()))
-        branch_out.append(out)
-        totals = [total]
-    sent = partial
+    partial, out, total, rest = call(
+        branch,
+        [payload, bf16((slots, width)), bf16((slots, 3 * HEAD_DIM)), bf16((row_dev, width))],
+        [VMEM] * (5 + shares + len(at_last)),
+        [scores, pltpu.VMEM((rows, width), jnp.bfloat16)],
+        keys=keys,
+        direct=tuple(int(a == b) for a, b in zip(inverse(relay[0]), back[last])) if relay else None,
+        kv_local=kv_local,
+    )(pick, bias, bk, bv, *ready[0], queries, *gathered, *at_last)
+    sent = [partial]
     for n in early[1:]:
-        sent.append(call(given, payload, [VMEM] * (4 + kv_local), key=back[n])(pick, *totals, *ready[n], *branch_out))
-    sent.append(call(share, payload, [VMEM] * (4 + 2 * kv_local), [scores], key=back[last], kv_local=kv_local)(pick, *totals, rk, rv, *branch_out, *pieces_of_last))
-    received = [call(given, payload, [VMEM] * (4 + kv_local), key=keys[0])(pick, *totals, *mine[:2], *branch_out)]
+        sent.append(call(given, payload, [VMEM] * 5, key=back[n])(pick, total, *ready[n], out))
+    sent.append(call(share, payload, [VMEM] * 6, [scores], key=back[last], kv_local=kv_local)(pick, total, rk, rv, out, rest))
+    received = [call(share, payload, [VMEM] * 6, [scores], key=keys[0], kv_local=kv_local)(pick, total, rk, rv, out, queries)]
     for n, partial in enumerate(sent):
         received.append(move(partial, back[n]))
     return call(join, bf16((row_dev, width)), [VMEM] * shares, heads=heads)(*received)
 
 
 def inverse(targets):
-    return tuple(targets.index(device) for device in range(len(targets)))
+    return tuple(targets.index(device) if device in targets else None for device in range(len(targets)))
 
 
 def plan(shares):
     if shares == 4:
-        return [(2, 0, 3, 1), (1, 3, 0, 2), (3, 2, 1, 0)]
-    return [tuple(device ^ k for device in range(shares)) for k in range(1, shares)]
+        return [(2, 0, 3, 1), (1, 3, 0, 2), (3, 2, 1, 0)], [(0, 2, 1, 3), (1, 0, 3, 2)]
+    return [tuple(device ^ k for device in range(shares)) for k in range(1, shares)], None
 
 
 def solution(mesh):

time: 35.9 us -> 35.5 us (0.989)
  waiting for transfers between devices: 9.55 us -> 8.14 us
  starting transfers between devices: 11.7 us -> 12.4 us
    pallas_call x6, Pallas kernels: 10.1 us -> 11.9 us  [the longest x1 3.63 us: body(): call(branch, [payload, bf16((slots, width)), bf16((slots, 3 * HEAD_DIM)),...]
    pallas_call x2 -> x1, Pallas kernels: 3.01 us -> 1.54 us  [body(): call(root, result, [VMEM] * 3, [scores], kv_local=kv_local)]
    ppermute x7, waiting for transfers between devices: 9.55 us -> 8.14 us  [move(): lax.ppermute(x, 'seq', [(i, target) for i, target in enumerate(targets) i...]
    ppermute x7, starting transfers between devices: 11.7 us -> 12.4 us  [move(): lax.ppermute(x, 'seq', [(i, target) for i, target in enumerate(targets) i...]
  transfers between devices with their start and end apart: 7 -> 7, of which waited for: 6 -> 4; matrix products, arithmetic and copies ran while one was open for 0% -> 0% of each run, Pallas kernels for 25% -> 22%
where the time goes in v4:
time: 35.5 us; the launch traced here: 35.4 us
  Pallas kernels  14.7 us (41%)
  starting transfers between devices  12.4 us (35%)
  waiting for transfers between devices  8.14 us (23%)
    ppermute x7, starting transfers between devices, move(): lax.ppermute(x, 'seq', [(i, target) for i, target in enumerate(targets) i...  12.4 us
    ppermute x7, waiting for transfers between devices, move(): lax.ppermute(x, 'seq', [(i, target) for i, target in enumerate(targets) i...  8.14 us
    pallas_call x1, Pallas kernels, body(): call(branch, [payload, bf16((slots, width)), bf16((slots, 3 * HEAD_DIM)),...  3.63 us
    pallas_call x1, Pallas kernels, body(): call(own, [bf16(x.shape) for x in (root_keys, root_values, branch_keys)]...  2.29 us
    pallas_call x1, Pallas kernels, body(): call(share, payload, [VMEM] * 6, [scores], key=back[last], kv_local=kv_lo...  1.94 us
    pallas_call x1, Pallas kernels, body(): call(share, payload, [VMEM] * 6, [scores], key=keys[0], kv_local=kv_local)  1.94 us
    pallas_call x1, Pallas kernels, body(): call(root_load, result + [bf16(branch_values.shape)], [VMEM] * 3 + [HBM],...  1.62 us
    pallas_call x1, Pallas kernels, body(): call(root, result, [VMEM] * 3, [scores], kv_local=kv_local)  1.54 us
  transfers between devices with their start and end apart: 7, of which 4 were waited for; matrix products, arithmetic and copies ran while one was open for 0% of the time, Pallas kernels for 22%

profile of v4, /device:TPU:0, one launch (start us, length us, event | category | flops | bytes accessed | tf_op | source)
XLA Modules:
  0.0 35.4 jit_solution(2852363075514104245)
XLA Ops:
  0.0 4.1 %collective-permute-start = (bf16[32,2048]{1,0:T(8,128)(2,1)}, bf16[32,2048]{1,0:T(8,128)(2,1)S(1)}, u32[]{:S(2)}, u32[]{:S(2)}) collective-permute-start(bf16[32,2048]{1,0:T(8,128)(2,1)} %q_ref.1), channel_id=1, source_target_pairs={{0,8},{4,0},{8,12},{12,4},{1,9},{5,1},{9,13},{13,5},{2,10},{6,2},{... | collective-permute-start | bytes 393224 | tf_op jit(solution)/shard_map/ppermute | solution.py:294
  4.1 0.0 collective-permute-start.1
  4.1 1.6 %collective-permute-start.2 = (bf16[32,2048]{1,0:T(8,128)(2,1)}, bf16[32,2048]{1,0:T(8,128)(2,1)S(1)}, u32[]{:S(2)}, u32[]{:S(2)}) collective-permute-start(bf16[32,2048]{1,0:T(8,128)(2,1)} %q_ref.1), channel_id=1, source_target_pairs={{0,0},{4,8},{8,4},{12,12},{1,1},{5,9},{9,5},{13,13},{2,2},{6,10},{... | collective-permute-start | bytes 393224 | tf_op jit(solution)/shard_map/ppermute | solution.py:294
  5.6 2.6 %collective-permute-done.q_ref.rest_1_ = bf16[32,2048]{1,0:T(8,128)(2,1)S(1)} collective-permute-done((bf16[32,2048]{1,0:T(8,128)(2,1)}, bf16[32,2048]{1,0:T(8,128)(2,1)S(1)}, u32[]{:S(2)}, u32[]{:S(2)}) %collective-permute-start) | collective-permute-done | bytes 131104 | tf_op jit(solution)/shard_map/ppermute | solution.py:294
  8.3 2.3 %collective-permute-start.3 = (bf16[32,2048]{1,0:T(8,128)(2,1)S(1)}, bf16[32,2048]{1,0:T(8,128)(2,1)S(1)}, u32[]{:S(2)}, u32[]{:S(2)}) collective-permute-start(bf16[32,2048]{1,0:T(8,128)(2,1)S(1)} %collective-permute-done.q_ref.rest_1_), channel_id=1, source_target_pairs={{0,4},{4,0},{8,12},{12,8},{1,5},{5,1},{9,13},{13,9},{2,6},{6,2},{1... | collective-permute-start | bytes 393224 | tf_op jit(solution)/shard_map/ppermute | solution.py:294
  10.5 2.3 %shard_map.73 = (bf16[2048,256]{1,0:T(8,128)(2,1)S(1)}, bf16[2048,256]{1,0:T(8,128)(2,1)S(1)}, bf16[2,2048,256]{2,1,0:T(8,128)(2,1)S(1)}, bf16[2,128,32]{2,1,0:T(8,128)(2,1)S(1)}, f32[2,2048]{1,0:T(2,128)S(1)}) custom-call(s32[8]{0:T(128)} %doc_hbm.1, s32[1,128]{1,0:T(1,128)} %bitcast.1, bf16[2048,256]{1,0:T(8,128)(2,1)} %rk_hbm.1, ...), custom_call_target="tpu_custom_call" | custom-call | tf_op jit(solution)/shard_map/pallas_call | solution.py:306
  12.8 1.6 %shard_map.74 = (f32[2,256,128]{2,1,0:T(8,128)S(1)}, f32[32,128]{1,0:T(8,128)S(1)}, bf16[2,2048,256]{2,1,0:T(8,128)(2,1)S(1)}) custom-call(bf16[32,2048]{1,0:T(8,128)(2,1)S(1)} %collective-permute-done.q_ref.rest_1_, bf16[2048,256]{1,0:T(8,128)(2,1)S(1)} %get-tuple-element.22.rk_ref, bf16[2048,256]{1,0:T(8,128)(2,1)S(1)} %get-tuple-element.23.rv_ref, ...), custom_call_target="tpu_custom_call" | custom-call | tf_op jit(solution)/shard_map/pallas_call | solution.py:315
  14.5 0.0 copy-start
  14.5 0.0 collective-permute-done.1.rest_2_.q_ref
  14.5 1.5 %shard_map.77 = (f32[2,256,128]{2,1,0:T(8,128)S(1)}, f32[32,128]{1,0:T(8,128)S(1)}) custom-call(bf16[32,2048]{1,0:T(8,128)(2,1)S(1)} %collective-permute-done.1.rest_2_.q_ref, bf16[2048,256]{1,0:T(8,128)(2,1)S(1)} %get-tuple-element.22.rk_ref, bf16[2048,256]{1,0:T(8,128)(2,1)S(1)} %get-tuple-element.23.rv_ref), custom_call_target="tpu_custom_call" | custom-call | tf_op jit(solution)/shard_map/pallas_call | solution.py:320
  16.0 0.0 collective-permute-done.2.rest_3_
  16.0 0.0 collective-permute-done.3.rest_4_
  16.0 0.0 copy-done
  16.1 3.6 %shard_map.75 = (bf16[528,128]{1,0:T(8,128)(2,1)S(1)}, bf16[64,2048]{1,0:T(8,128)(2,1)S(1)}, bf16[64,384]{1,0:T(8,128)(2,1)S(1)}, bf16[32,2048]{1,0:T(8,128)(2,1)S(1)}) custom-call(bf16[2,128,32]{2,1,0:T(8,128)(2,1)S(1)} %get-tuple-element.19.pick_ref, f32[2,2048]{1,0:T(2,128)S(1)} %get-tuple-element.20.bias_ref, ...), custom_call_target="tpu_custom_call" | custom-call | tf_op jit(solution)/shard_map/pallas_call | solution.py:322
  19.7 1.9 %shard_map.79 = bf16[528,128]{1,0:T(8,128)(2,1)S(1)} custom-call(bf16[2,128,32]{2,1,0:T(8,128)(2,1)S(1)} %get-tuple-element.19.pick_ref, bf16[64,384]{1,0:T(8,128)(2,1)S(1)} %get-tuple-element.27.b_level_ref, bf16[2048,256]{1,0:T(8,128)(2,1)S(1)} %get-tuple-element.22.rk_ref, bf16[2048,256]{1,0:T(8,128)(2,1)S(1)} %get-tuple-element.23.rv_ref, ...), custom_call_target="tpu_custom_call" | custom-call | tf_op jit(solution)/shard_map/pallas_call | solution.py:334
  21.6 2.5 %collective-permute-start.6 = (bf16[528,128]{1,0:T(8,128)(2,1)S(1)}, bf16[528,128]{1,0:T(8,128)(2,1)S(1)}, u32[]{:S(2)}, u32[]{:S(2)}) collective-permute-start(bf16[528,128]{1,0:T(8,128)(2,1)S(1)} %shard_map.79), channel_id=1, source_target_pairs={{0,12},{4,8},{8,4},{12,0},{1,13},{5,9},{9,5},{13,1},{2,14},{6,10},... | collective-permute-start | bytes 405512 | tf_op jit(solution)/shard_map/ppermute | solution.py:294
  24.1 0.5 %shard_map.78 = bf16[528,128]{1,0:T(8,128)(2,1)S(1)} custom-call(bf16[2,128,32]{2,1,0:T(8,128)(2,1)S(1)} %get-tuple-element.19.pick_ref, bf16[64,384]{1,0:T(8,128)(2,1)S(1)} %get-tuple-element.27.b_level_ref, f32[2,256,128]{2,1,0:T(8,128)S(1)} %get-tuple-element.30.out_ref, f32[32,128]{1,0:T(8,128)S(1)} %get-tuple-element.31.level_ref, ...), custom_call_target="tpu_custom_call" | custom-call | tf_op jit(solution)/shard_map/pallas_call | solution.py:333
  24.7 0.0 collective-permute-start.5
  24.7 2.0 %collective-permute-start.4 = (bf16[528,128]{1,0:T(8,128)(2,1)S(1)}, bf16[528,128]{1,0:T(8,128)(2,1)S(1)}, u32[]{:S(2)}, u32[]{:S(2)}) collective-permute-start(bf16[528,128]{1,0:T(8,128)(2,1)S(1)} %get-tuple-element.29), channel_id=1, source_target_pairs={{0,4},{4,12},{8,0},{12,8},{1,5},{5,13},{9,1},{13,9},{2,6},{6,14},{... | collective-permute-start | bytes 405512 | tf_op jit(solution)/shard_map/ppermute | solution.py:294
  26.7 1.9 %shard_map.76.refs_0_ = bf16[528,128]{1,0:T(8,128)(2,1)S(1)} custom-call(bf16[2,128,32]{2,1,0:T(8,128)(2,1)S(1)} %get-tuple-element.19.pick_ref, bf16[64,384]{1,0:T(8,128)(2,1)S(1)} %get-tuple-element.27.b_level_ref, bf16[2048,256]{1,0:T(8,128)(2,1)S(1)} %get-tuple-element.22.rk_ref, bf16[2048,256]{1,0:T(8,128)(2,1)S(1)} %get-tuple-element.23.rv_ref, ...), custom_call_target="tpu_custom_call" | custom-call | tf_op jit(solution)/shard_map/pallas_call | solution.py:335
  28.7 1.2 %collective-permute-done.6.refs_3_ = bf16[528,128]{1,0:T(8,128)(2,1)S(1)} collective-permute-done((bf16[528,128]{1,0:T(8,128)(2,1)S(1)}, bf16[528,128]{1,0:T(8,128)(2,1)S(1)}, u32[]{:S(2)}, u32[]{:S(2)}) %collective-permute-start.6) | collective-permute-done | bytes 135200 | tf_op jit(solution)/shard_map/ppermute | solution.py:294
  29.8 1.1 %collective-permute-done.5.refs_2_ = bf16[528,128]{1,0:T(8,128)(2,1)S(1)} collective-permute-done((bf16[528,128]{1,0:T(8,128)(2,1)S(1)}, bf16[528,128]{1,0:T(8,128)(2,1)S(1)}, u32[]{:S(2)}, u32[]{:S(2)}) %collective-permute-start.5) | collective-permute-done | bytes 135200 | tf_op jit(solution)/shard_map/ppermute | solution.py:294
  30.9 3.2 %collective-permute-done.4.refs_1_ = bf16[528,128]{1,0:T(8,128)(2,1)S(1)} collective-permute-done((bf16[528,128]{1,0:T(8,128)(2,1)S(1)}, bf16[528,128]{1,0:T(8,128)(2,1)S(1)}, u32[]{:S(2)}, u32[]{:S(2)}) %collective-permute-start.4) | collective-permute-done | bytes 135200 | tf_op jit(solution)/shard_map/ppermute | solution.py:294
  34.1 1.2 %shard_map.80 = bf16[32,2048]{1,0:T(8,128)(2,1)} custom-call(bf16[528,128]{1,0:T(8,128)(2,1)S(1)} %shard_map.76.refs_0_, bf16[528,128]{1,0:T(8,128)(2,1)S(1)} %collective-permute-done.4.refs_1_, bf16[528,128]{1,0:T(8,128)(2,1)S(1)} %collective-permute-done.5.refs_2_, bf16[528,128]{1,0:T(8,128)(2,1)S(1)} %collective-permute-done.6.refs_3_), custom_call_target="tpu_custom_call" | custom-call | tf_op jit(solution)/shard_map/pallas_call | solution.py:338
Async XLA Ops:
  0.0 8.3 %collective-permute-start = (bf16[32,2048]{1,0:T(8,128)(2,1)}, bf16[32,2048]{1,0:T(8,128)(2,1)S(1)}, u32[]{:S(2)}, u32[]{:S(2)}) collective-permute-start(bf16[32,2048]{1,0:T(8,128)(2,1)} %q_ref.1), channel_id=1, source_target_pairs={{0,8},{4,0},{8,12},{12,4},{1,9},{5,1},{9,13},{13,5},{2,10},{6,2},{... | collective-permute-start | bytes 393224 | tf_op jit(solution)/shard_map/ppermute | solution.py:294
  4.1 10.4 %collective-permute-start.1 = (bf16[32,2048]{1,0:T(8,128)(2,1)}, bf16[32,2048]{1,0:T(8,128)(2,1)S(1)}, u32[]{:S(2)}, u32[]{:S(2)}) collective-permute-start(bf16[32,2048]{1,0:T(8,128)(2,1)} %q_ref.1), channel_id=1, source_target_pairs={{0,4},{4,12},{8,0},{12,8},{1,5},{5,13},{9,1},{13,9},{2,6},{6,14},{... | collective-permute-start | bytes 393224 | tf_op jit(solution)/shard_map/ppermute | solution.py:294
  4.1 12.0 %collective-permute-start.2 = (bf16[32,2048]{1,0:T(8,128)(2,1)}, bf16[32,2048]{1,0:T(8,128)(2,1)S(1)}, u32[]{:S(2)}, u32[]{:S(2)}) collective-permute-start(bf16[32,2048]{1,0:T(8,128)(2,1)} %q_ref.1), channel_id=1, source_target_pairs={{0,0},{4,8},{8,4},{12,12},{1,1},{5,9},{9,5},{13,13},{2,2},{6,10},{... | collective-permute-start | bytes 393224 | tf_op jit(solution)/shard_map/ppermute | solution.py:294
  8.3 7.8 %collective-permute-start.3 = (bf16[32,2048]{1,0:T(8,128)(2,1)S(1)}, bf16[32,2048]{1,0:T(8,128)(2,1)S(1)}, u32[]{:S(2)}, u32[]{:S(2)}) collective-permute-start(bf16[32,2048]{1,0:T(8,128)(2,1)S(1)} %collective-permute-done.q_ref.rest_1_), channel_id=1, source_target_pairs={{0,4},{4,0},{8,12},{12,8},{1,5},{5,1},{9,13},{13,9},{2,6},{6,2},{1... | collective-permute-start | bytes 393224 | tf_op jit(solution)/shard_map/ppermute | solution.py:294
  14.5 1.6 %copy-start = (bf16[32,2048]{1,0:T(8,128)(2,1)S(1)}, bf16[32,2048]{1,0:T(8,128)(2,1)}, u32[]{:S(2)}) copy-start(bf16[32,2048]{1,0:T(8,128)(2,1)} %q_ref.1) | copy-start | bytes 393220
  21.6 8.2 %collective-permute-start.6 = (bf16[528,128]{1,0:T(8,128)(2,1)S(1)}, bf16[528,128]{1,0:T(8,128)(2,1)S(1)}, u32[]{:S(2)}, u32[]{:S(2)}) collective-permute-start(bf16[528,128]{1,0:T(8,128)(2,1)S(1)} %shard_map.79), channel_id=1, source_target_pairs={{0,12},{4,8},{8,4},{12,0},{1,13},{5,9},{9,5},{13,1},{2,14},{6,10},... | collective-permute-start | bytes 405512 | tf_op jit(solution)/shard_map/ppermute | solution.py:294
  24.7 6.2 %collective-permute-start.5 = (bf16[528,128]{1,0:T(8,128)(2,1)S(1)}, bf16[528,128]{1,0:T(8,128)(2,1)S(1)}, u32[]{:S(2)}, u32[]{:S(2)}) collective-permute-start(bf16[528,128]{1,0:T(8,128)(2,1)S(1)} %shard_map.78), channel_id=1, source_target_pairs={{0,8},{4,0},{8,12},{12,4},{1,9},{5,1},{9,13},{13,5},{2,10},{6,2},{... | collective-permute-start | bytes 405512 | tf_op jit(solution)/shard_map/ppermute | solution.py:294
  24.7 9.4 %collective-permute-start.4 = (bf16[528,128]{1,0:T(8,128)(2,1)S(1)}, bf16[528,128]{1,0:T(8,128)(2,1)S(1)}, u32[]{:S(2)}, u32[]{:S(2)}) collective-permute-start(bf16[528,128]{1,0:T(8,128)(2,1)S(1)} %get-tuple-element.29), channel_id=1, source_target_pairs={{0,4},{4,12},{8,0},{12,8},{1,5},{5,13},{9,1},{13,9},{2,6},{6,14},{... | collective-permute-start | bytes 405512 | tf_op jit(solution)/shard_map/ppermute | solution.py:294

commit v5 on v4

--- a/solution.py
+++ b/solution.py
@@ -14,7 +14,7 @@
 GROUP = QHEADS // KVHEADS
 LOW = -1.0e30
 SCALE = HEAD_DIM ** -0.5 * math.log2(math.e)
-TILE = 256
+TILE = 512
 VMEM_BYTES = 20 * 2 ** 20
 
 
@@ -110,8 +110,8 @@
     return finish
 
 
-def own(doc_hbm, id_hbm, rk_hbm, rv_hbm, bk_hbm, rk_ref, rv_ref, bk_ref, pick_ref, bias_ref, id_ref, doc_ref, arrived):
-    loads = [pltpu.make_async_copy(source, target, arrived.at[n]) for n, (source, target) in enumerate(zip((doc_hbm, id_hbm, rk_hbm, rv_hbm, bk_hbm), (doc_ref, id_ref, rk_ref, rv_ref, bk_ref)))]
+def own(doc_hbm, id_hbm, rk_hbm, rv_hbm, rk_ref, rv_ref, pick_ref, bias_ref, id_ref, doc_ref, arrived):
+    loads = [pltpu.make_async_copy(source, target, arrived.at[n]) for n, (source, target) in enumerate(zip((doc_hbm, id_hbm, rk_hbm, rv_hbm), (doc_ref, id_ref, rk_ref, rv_ref)))]
     for load in loads:
         load.start()
     branch_dev, rows, most_rows = pick_ref.shape
@@ -134,8 +134,8 @@
         load.wait()
 
 
-def root_load(q_ref, rk_ref, rv_ref, bv_hbm, out_ref, level_ref, bv_ref, score_ref, arrived, *, kv_local):
-    load = pltpu.make_async_copy(bv_hbm, bv_ref, arrived)
+def root_load(q_ref, rk_ref, rv_ref, stored_hbm, out_ref, level_ref, stored_ref, score_ref, arrived, *, kv_local):
+    load = pltpu.make_async_copy(stored_hbm, stored_ref, arrived)
     load.start()
     root(q_ref, rk_ref, rv_ref, out_ref, level_ref, score_ref, kv_local=kv_local)
     load.wait()
@@ -303,21 +303,23 @@
     if relay:
         at_last.append(move(gathered[0], relay[1]))
     in_hbm = [pltpu.with_memory_space_constraint(x, pltpu.HBM) for x in (doc_len, branch_id.reshape(1, rows), root_keys, root_values, branch_keys, branch_values)]
-    rk, rv, bk, pick, bias = call(
+    rk, rv, pick, bias = call(
         own,
-        [bf16(x.shape) for x in (root_keys, root_values, branch_keys)] + [bf16((branch_dev, rows, most_rows)), f32((branch_dev, branch_len))],
-        [HBM] * 5,
-        [pltpu.VMEM((1, rows), jnp.int32), pltpu.SMEM(doc_len.shape, jnp.int32), pltpu.SemaphoreType.DMA((5,))],
-    )(*in_hbm[:5])
-    ready = []
+        [bf16(x.shape) for x in (root_keys, root_values)] + [bf16((branch_dev, rows, most_rows)), f32((branch_dev, branch_len))],
+        [HBM] * 4,
+        [pltpu.VMEM((1, rows), jnp.int32), pltpu.SMEM(doc_len.shape, jnp.int32), pltpu.SemaphoreType.DMA((4,))],
+    )(*in_hbm[:4])
+    ready, branch_stored = [], []
     for n in early:
-        if n == 0:
-            *first, bv = call(
-                root_load, result + [bf16(branch_values.shape)], [VMEM] * 3 + [HBM], [scores, pltpu.SemaphoreType.DMA(())], kv_local=kv_local
-            )(gathered[n], rk, rv, in_hbm[5])
+        if n < 2:
+            *first, loaded = call(
+                root_load, result + [bf16(branch_keys.shape)], [VMEM] * 3 + [HBM], [scores, pltpu.SemaphoreType.DMA(())], kv_local=kv_local
+            )(gathered[n], rk, rv, in_hbm[4 + n])
             ready.append(first)
+            branch_stored.append(loaded)
         else:
             ready.append(call(root, result, [VMEM] * 3, [scores], kv_local=kv_local)(gathered[n], rk, rv))
+    bk, bv = branch_stored
     keys = [tuple(range(shares))] + back
     partial, out, total, rest = call(
         branch,

time: 35.5 us -> 35.6 us (level)
  starting transfers between devices: 12.4 us -> 13.4 us
  Pallas kernels: 14.7 us -> 14.1 us
    ppermute x7, starting transfers between devices: 12.4 us -> 13.4 us  [move(): lax.ppermute(x, 'seq', [(i, target) for i, target in enumerate(targets) i...]
    pallas_call x3, Pallas kernels: 5.45 us -> 4.84 us  [the longest x2 3.25 us: body(): call(root_load, result + [bf16(branch_keys.shape)], [VMEM] * 3 + [HBM], [...]
  transfers between devices with their start and end apart: 7 -> 7, of which waited for: 4 -> 3; matrix products, arithmetic and copies ran while one was open for 0% -> 0% of each run, Pallas kernels for 22% -> 21%
where the time goes in v5:
time: 35.6 us; the launch traced here: 35.4 us
  Pallas kernels  14.1 us (40%)
  starting transfers between devices  13.4 us (38%)
  waiting for transfers between devices  7.85 us (22%)
    ppermute x7, starting transfers between devices, move(): lax.ppermute(x, 'seq', [(i, target) for i, target in enumerate(targets) i...  13.4 us
    ppermute x7, waiting for transfers between devices, move(): lax.ppermute(x, 'seq', [(i, target) for i, target in enumerate(targets) i...  7.85 us
    pallas_call x1, Pallas kernels, body(): call(branch, [payload, bf16((slots, width)), bf16((slots, 3 * HEAD_DIM)),...  3.65 us
    pallas_call x2, Pallas kernels, body(): call(root_load, result + [bf16(branch_keys.shape)], [VMEM] * 3 + [HBM], [...  3.25 us
    pallas_call x1, Pallas kernels, body(): call(share, payload, [VMEM] * 6, [scores], key=back[last], kv_local=kv_lo...  1.94 us
    pallas_call x1, Pallas kernels, body(): call(share, payload, [VMEM] * 6, [scores], key=keys[0], kv_local=kv_local)  1.94 us
    pallas_call x1, Pallas kernels, body(): call(own, [bf16(x.shape) for x in (root_keys, root_values)] + [bf16((bran...  1.59 us
    pallas_call x1, Pallas kernels, body(): call(join, bf16((row_dev, width)), [VMEM] * shares, heads=heads)(*received)  1.23 us
  transfers between devices with their start and end apart: 7, of which 3 were waited for; matrix products, arithmetic and copies ran while one was open for 0% of the time, Pallas kernels for 21%

profile of v5, /device:TPU:0, one launch (start us, length us, event | category | flops | bytes accessed | tf_op | source)
XLA Modules:
  0.0 35.4 jit_solution(17078580367631607778)
XLA Ops:
  0.0 4.1 %collective-permute-start = (bf16[32,2048]{1,0:T(8,128)(2,1)}, bf16[32,2048]{1,0:T(8,128)(2,1)S(1)}, u32[]{:S(2)}, u32[]{:S(2)}) collective-permute-start(bf16[32,2048]{1,0:T(8,128)(2,1)} %q_ref.1), channel_id=1, source_target_pairs={{0,8},{4,0},{8,12},{12,4},{1,9},{5,1},{9,13},{13,5},{2,10},{6,2},{... | collective-permute-start | bytes 393224 | tf_op jit(solution)/shard_map/ppermute | solution.py:294
  4.1 0.0 collective-permute-start.1
  4.1 1.6 %collective-permute-start.2 = (bf16[32,2048]{1,0:T(8,128)(2,1)}, bf16[32,2048]{1,0:T(8,128)(2,1)S(1)}, u32[]{:S(2)}, u32[]{:S(2)}) collective-permute-start(bf16[32,2048]{1,0:T(8,128)(2,1)} %q_ref.1), channel_id=1, source_target_pairs={{0,0},{4,8},{8,4},{12,12},{1,1},{5,9},{9,5},{13,13},{2,2},{6,10},{... | collective-permute-start | bytes 393224 | tf_op jit(solution)/shard_map/ppermute | solution.py:294
  5.6 2.6 %collective-permute-done.q_ref.rest_1_ = bf16[32,2048]{1,0:T(8,128)(2,1)S(1)} collective-permute-done((bf16[32,2048]{1,0:T(8,128)(2,1)}, bf16[32,2048]{1,0:T(8,128)(2,1)S(1)}, u32[]{:S(2)}, u32[]{:S(2)}) %collective-permute-start) | collective-permute-done | bytes 131104 | tf_op jit(solution)/shard_map/ppermute | solution.py:294
  8.3 2.3 %collective-permute-start.3 = (bf16[32,2048]{1,0:T(8,128)(2,1)S(1)}, bf16[32,2048]{1,0:T(8,128)(2,1)S(1)}, u32[]{:S(2)}, u32[]{:S(2)}) collective-permute-start(bf16[32,2048]{1,0:T(8,128)(2,1)S(1)} %collective-permute-done.q_ref.rest_1_), channel_id=1, source_target_pairs={{0,4},{4,0},{8,12},{12,8},{1,5},{5,1},{9,13},{13,9},{2,6},{6,2},{1... | collective-permute-start | bytes 393224 | tf_op jit(solution)/shard_map/ppermute | solution.py:294
  10.5 1.6 %shard_map.73 = (bf16[2048,256]{1,0:T(8,128)(2,1)S(1)}, bf16[2048,256]{1,0:T(8,128)(2,1)S(1)}, bf16[2,128,32]{2,1,0:T(8,128)(2,1)S(1)}, f32[2,2048]{1,0:T(2,128)S(1)}) custom-call(s32[8]{0:T(128)} %doc_hbm.1, s32[1,128]{1,0:T(1,128)} %bitcast.1, bf16[2048,256]{1,0:T(8,128)(2,1)} %rk_hbm.1, bf16[2048,256]{1,0:T(8,128)(2,1)} %rv_hbm.1), custom_call_target="tpu_custom_call" | custom-call | tf_op jit(solution)/shard_map/pallas_call | solution.py:306
  12.1 1.6 %shard_map.74 = (f32[2,256,128]{2,1,0:T(8,128)S(1)}, f32[32,128]{1,0:T(8,128)S(1)}, bf16[2,2048,256]{2,1,0:T(8,128)(2,1)S(1)}) custom-call(bf16[32,2048]{1,0:T(8,128)(2,1)S(1)} %collective-permute-done.q_ref.rest_1_, bf16[2048,256]{1,0:T(8,128)(2,1)S(1)} %get-tuple-element.21.rk_ref, bf16[2048,256]{1,0:T(8,128)(2,1)S(1)} %get-tuple-element.22.rv_ref, ...), custom_call_target="tpu_custom_call" | custom-call | tf_op jit(solution)/shard_map/pallas_call | solution.py:315
  13.7 0.0 copy-start
  13.8 0.0 collective-permute-done.1.q_ref.rest_2_
  13.8 1.6 %shard_map.75 = (f32[2,256,128]{2,1,0:T(8,128)S(1)}, f32[32,128]{1,0:T(8,128)S(1)}, bf16[2,2048,256]{2,1,0:T(8,128)(2,1)S(1)}) custom-call(bf16[32,2048]{1,0:T(8,128)(2,1)S(1)} %collective-permute-done.1.q_ref.rest_2_, bf16[2048,256]{1,0:T(8,128)(2,1)S(1)} %get-tuple-element.21.rk_ref, bf16[2048,256]{1,0:T(8,128)(2,1)S(1)} %get-tuple-element.22.rv_ref, ...), custom_call_target="tpu_custom_call" | custom-call | tf_op jit(solution)/shard_map/pallas_call | solution.py:315
  15.4 0.0 collective-permute-done.2.rest_3_
  15.4 0.0 collective-permute-done.3.rest_4_
  15.4 0.0 copy-done
  15.4 3.6 %shard_map.76 = (bf16[528,128]{1,0:T(8,128)(2,1)S(1)}, bf16[64,2048]{1,0:T(8,128)(2,1)S(1)}, bf16[64,384]{1,0:T(8,128)(2,1)S(1)}, bf16[32,2048]{1,0:T(8,128)(2,1)S(1)}) custom-call(bf16[2,128,32]{2,1,0:T(8,128)(2,1)S(1)} %get-tuple-element.19.pick_ref, f32[2,2048]{1,0:T(2,128)S(1)} %get-tuple-element.20.bias_ref, ...), custom_call_target="tpu_custom_call" | custom-call | tf_op jit(solution)/shard_map/pallas_call | solution.py:324
  19.1 1.9 %shard_map.79 = bf16[528,128]{1,0:T(8,128)(2,1)S(1)} custom-call(bf16[2,128,32]{2,1,0:T(8,128)(2,1)S(1)} %get-tuple-element.19.pick_ref, bf16[64,384]{1,0:T(8,128)(2,1)S(1)} %get-tuple-element.27.b_level_ref, bf16[2048,256]{1,0:T(8,128)(2,1)S(1)} %get-tuple-element.21.rk_ref, bf16[2048,256]{1,0:T(8,128)(2,1)S(1)} %get-tuple-element.22.rv_ref, ...), custom_call_target="tpu_custom_call" | custom-call | tf_op jit(solution)/shard_map/pallas_call | solution.py:336
  21.0 2.5 %collective-permute-start.6 = (bf16[528,128]{1,0:T(8,128)(2,1)S(1)}, bf16[528,128]{1,0:T(8,128)(2,1)S(1)}, u32[]{:S(2)}, u32[]{:S(2)}) collective-permute-start(bf16[528,128]{1,0:T(8,128)(2,1)S(1)} %shard_map.79), channel_id=1, source_target_pairs={{0,12},{4,8},{8,4},{12,0},{1,13},{5,9},{9,5},{13,1},{2,14},{6,10},... | collective-permute-start | bytes 405512 | tf_op jit(solution)/shard_map/ppermute | solution.py:294
  23.6 0.0 collective-permute-start.4
  23.6 0.5 %shard_map.78 = bf16[528,128]{1,0:T(8,128)(2,1)S(1)} custom-call(bf16[2,128,32]{2,1,0:T(8,128)(2,1)S(1)} %get-tuple-element.19.pick_ref, bf16[64,384]{1,0:T(8,128)(2,1)S(1)} %get-tuple-element.27.b_level_ref, f32[2,256,128]{2,1,0:T(8,128)S(1)} %get-tuple-element.30.out_ref, f32[32,128]{1,0:T(8,128)S(1)} %get-tuple-element.31.level_ref, ...), custom_call_target="tpu_custom_call" | custom-call | tf_op jit(solution)/shard_map/pallas_call | solution.py:335
  24.1 2.9 %collective-permute-start.5 = (bf16[528,128]{1,0:T(8,128)(2,1)S(1)}, bf16[528,128]{1,0:T(8,128)(2,1)S(1)}, u32[]{:S(2)}, u32[]{:S(2)}) collective-permute-start(bf16[528,128]{1,0:T(8,128)(2,1)S(1)} %shard_map.78), channel_id=1, source_target_pairs={{0,8},{4,0},{8,12},{12,4},{1,9},{5,1},{9,13},{13,5},{2,10},{6,2},{... | collective-permute-start | bytes 405512 | tf_op jit(solution)/shard_map/ppermute | solution.py:294
  27.0 1.9 %shard_map.77.refs_0_ = bf16[528,128]{1,0:T(8,128)(2,1)S(1)} custom-call(bf16[2,128,32]{2,1,0:T(8,128)(2,1)S(1)} %get-tuple-element.19.pick_ref, bf16[64,384]{1,0:T(8,128)(2,1)S(1)} %get-tuple-element.27.b_level_ref, bf16[2048,256]{1,0:T(8,128)(2,1)S(1)} %get-tuple-element.21.rk_ref, bf16[2048,256]{1,0:T(8,128)(2,1)S(1)} %get-tuple-element.22.rv_ref, ...), custom_call_target="tpu_custom_call" | custom-call | tf_op jit(solution)/shard_map/pallas_call | solution.py:337
  29.0 0.5 %collective-permute-done.6.refs_3_ = bf16[528,128]{1,0:T(8,128)(2,1)S(1)} collective-permute-done((bf16[528,128]{1,0:T(8,128)(2,1)S(1)}, bf16[528,128]{1,0:T(8,128)(2,1)S(1)}, u32[]{:S(2)}, u32[]{:S(2)}) %collective-permute-start.6) | collective-permute-done | bytes 135200 | tf_op jit(solution)/shard_map/ppermute | solution.py:294
  29.4 4.7 %collective-permute-done.4.refs_1_ = bf16[528,128]{1,0:T(8,128)(2,1)S(1)} collective-permute-done((bf16[528,128]{1,0:T(8,128)(2,1)S(1)}, bf16[528,128]{1,0:T(8,128)(2,1)S(1)}, u32[]{:S(2)}, u32[]{:S(2)}) %collective-permute-start.4) | collective-permute-done | bytes 135200 | tf_op jit(solution)/shard_map/ppermute | solution.py:294
  34.2 0.0 collective-permute-done.5.refs_2_
  34.2 1.2 %shard_map.80 = bf16[32,2048]{1,0:T(8,128)(2,1)} custom-call(bf16[528,128]{1,0:T(8,128)(2,1)S(1)} %shard_map.77.refs_0_, bf16[528,128]{1,0:T(8,128)(2,1)S(1)} %collective-permute-done.4.refs_1_, bf16[528,128]{1,0:T(8,128)(2,1)S(1)} %collective-permute-done.5.refs_2_, bf16[528,128]{1,0:T(8,128)(2,1)S(1)} %collective-permute-done.6.refs_3_), custom_call_target="tpu_custom_call" | custom-call | tf_op jit(solution)/shard_map/pallas_call | solution.py:340
Async XLA Ops:
  0.0 8.3 %collective-permute-start = (bf16[32,2048]{1,0:T(8,128)(2,1)}, bf16[32,2048]{1,0:T(8,128)(2,1)S(1)}, u32[]{:S(2)}, u32[]{:S(2)}) collective-permute-start(bf16[32,2048]{1,0:T(8,128)(2,1)} %q_ref.1), channel_id=1, source_target_pairs={{0,8},{4,0},{8,12},{12,4},{1,9},{5,1},{9,13},{13,5},{2,10},{6,2},{... | collective-permute-start | bytes 393224 | tf_op jit(solution)/shard_map/ppermute | solution.py:294
  4.1 9.7 %collective-permute-start.1 = (bf16[32,2048]{1,0:T(8,128)(2,1)}, bf16[32,2048]{1,0:T(8,128)(2,1)S(1)}, u32[]{:S(2)}, u32[]{:S(2)}) collective-permute-start(bf16[32,2048]{1,0:T(8,128)(2,1)} %q_ref.1), channel_id=1, source_target_pairs={{0,4},{4,12},{8,0},{12,8},{1,5},{5,13},{9,1},{13,9},{2,6},{6,14},{... | collective-permute-start | bytes 393224 | tf_op jit(solution)/shard_map/ppermute | solution.py:294
  4.1 11.3 %collective-permute-start.2 = (bf16[32,2048]{1,0:T(8,128)(2,1)}, bf16[32,2048]{1,0:T(8,128)(2,1)S(1)}, u32[]{:S(2)}, u32[]{:S(2)}) collective-permute-start(bf16[32,2048]{1,0:T(8,128)(2,1)} %q_ref.1), channel_id=1, source_target_pairs={{0,0},{4,8},{8,4},{12,12},{1,1},{5,9},{9,5},{13,13},{2,2},{6,10},{... | collective-permute-start | bytes 393224 | tf_op jit(solution)/shard_map/ppermute | solution.py:294
  8.3 7.2 %collective-permute-start.3 = (bf16[32,2048]{1,0:T(8,128)(2,1)S(1)}, bf16[32,2048]{1,0:T(8,128)(2,1)S(1)}, u32[]{:S(2)}, u32[]{:S(2)}) collective-permute-start(bf16[32,2048]{1,0:T(8,128)(2,1)S(1)} %collective-permute-done.q_ref.rest_1_), channel_id=1, source_target_pairs={{0,4},{4,0},{8,12},{12,8},{1,5},{5,1},{9,13},{13,9},{2,6},{6,2},{1... | collective-permute-start | bytes 393224 | tf_op jit(solution)/shard_map/ppermute | solution.py:294
  13.7 1.7 %copy-start = (bf16[32,2048]{1,0:T(8,128)(2,1)S(1)}, bf16[32,2048]{1,0:T(8,128)(2,1)}, u32[]{:S(2)}) copy-start(bf16[32,2048]{1,0:T(8,128)(2,1)} %q_ref.1) | copy-start | bytes 393220
  21.0 8.4 %collective-permute-start.6 = (bf16[528,128]{1,0:T(8,128)(2,1)S(1)}, bf16[528,128]{1,0:T(8,128)(2,1)S(1)}, u32[]{:S(2)}, u32[]{:S(2)}) collective-permute-start(bf16[528,128]{1,0:T(8,128)(2,1)S(1)} %shard_map.79), channel_id=1, source_target_pairs={{0,12},{4,8},{8,4},{12,0},{1,13},{5,9},{9,5},{13,1},{2,14},{6,10},... | collective-permute-start | bytes 405512 | tf_op jit(solution)/shard_map/ppermute | solution.py:294
  23.6 10.6 %collective-permute-start.4 = (bf16[528,128]{1,0:T(8,128)(2,1)S(1)}, bf16[528,128]{1,0:T(8,128)(2,1)S(1)}, u32[]{:S(2)}, u32[]{:S(2)}) collective-permute-start(bf16[528,128]{1,0:T(8,128)(2,1)S(1)} %get-tuple-element.29), channel_id=1, source_target_pairs={{0,4},{4,12},{8,0},{12,8},{1,5},{5,13},{9,1},{13,9},{2,6},{6,14},{... | collective-permute-start | bytes 405512 | tf_op jit(solution)/shard_map/ppermute | solution.py:294
  24.1 10.1 %collective-permute-start.5 = (bf16[528,128]{1,0:T(8,128)(2,1)S(1)}, bf16[528,128]{1,0:T(8,128)(2,1)S(1)}, u32[]{:S(2)}, u32[]{:S(2)}) collective-permute-start(bf16[528,128]{1,0:T(8,128)(2,1)S(1)} %shard_map.78), channel_id=1, source_target_pairs={{0,8},{4,0},{8,12},{12,4},{1,9},{5,1},{9,13},{13,5},{2,10},{6,2},{... | collective-permute-start | bytes 405512 | tf_op jit(solution)/shard_map/ppermute | solution.py:294

commit v6 on v5

--- a/solution.py
+++ b/solution.py
@@ -234,25 +234,43 @@
     merge(share_ref, picks(pick_ref, key, level_ref.shape[0]), [out_ref[f] for f in range(out_ref.shape[0])], level_ref[...], branch_ref, b_level_ref[...])
 
 
-def join(*refs, heads):
-    share_refs, out_ref = refs[:-1], refs[-1]
-    row_dev = out_ref.shape[0]
+def level_of(share_ref, heads, row_dev):
+    s = share_ref[heads * row_dev:, :].astype(jnp.float32)
+    return s + pltpu.roll(s, HEAD_DIM - heads, 1) + pltpu.roll(s, HEAD_DIM - 2 * heads, 1)
+
+
+def combine(levels, refs, heads, row_dev, write):
     half = row_dev // 2
-    levels = []
-    for ref in share_refs:
-        s = ref[heads * row_dev:, :].astype(jnp.float32)
-        levels.append(s + pltpu.roll(s, HEAD_DIM - heads, 1) + pltpu.roll(s, HEAD_DIM - 2 * heads, 1))
     top = functools.reduce(jnp.maximum, levels)
     parts = [jnp.exp2(x - top) for x in levels]
     whole = functools.reduce(jnp.add, parts)
     parts = [x / whole for x in parts]
     for h in range(heads):
         result = None
-        for ref, part in zip(share_refs, parts):
+        for ref, part in zip(refs, parts):
             factor = jnp.concatenate([spread(part, h, half), spread(part, HEAD_DIM // 2 + h, half)], axis=0)
             term = ref[h * row_dev:(h + 1) * row_dev, :].astype(jnp.float32) * factor
             result = term if result is None else result + term
+        write(h, result)
+    return top + jnp.log2(whole)
+
+
+def gather_up(*refs, heads, row_dev):
+    share_refs, (sum_ref, level_ref) = refs[:-2], refs[-2:]
+
+    def write(h, result):
+        sum_ref[h * row_dev:(h + 1) * row_dev, :] = result
+
+    level_ref[...] = combine([level_of(ref, heads, row_dev) for ref in share_refs], share_refs, heads, row_dev, write)
+
+
+def join(sum_ref, level_ref, share_ref, out_ref, *, heads):
+    row_dev = out_ref.shape[0]
+
+    def write(h, result):
         out_ref[:, h * HEAD_DIM:(h + 1) * HEAD_DIM] = result.astype(jnp.bfloat16)
+
+    combine([level_ref[...], level_of(share_ref, heads, row_dev)], [sum_ref, share_ref], heads, row_dev, write)
 
 
 VMEM = pl.BlockSpec(memory_space=pltpu.VMEM)
@@ -337,7 +355,8 @@
     received = [call(share, payload, [VMEM] * 6, [scores], key=keys[0], kv_local=kv_local)(pick, total, rk, rv, out, queries)]
     for n, partial in enumerate(sent):
         received.append(move(partial, back[n]))
-    return call(join, bf16((row_dev, width)), [VMEM] * shares, heads=heads)(*received)
+    added = call(gather_up, [f32((heads * row_dev, HEAD_DIM)), f32((row_dev // 2, HEAD_DIM))], [VMEM] * (shares - 1), heads=heads, row_dev=row_dev)(*received[:-1])
+    return call(join, bf16((row_dev, width)), [VMEM] * 3, heads=heads)(*added, received[-1])
 
 
 def inverse(targets):

time: 35.6 us -> 33.3 us (0.935)
  waiting for transfers between devices: 7.85 us -> 5.17 us
    ppermute x7, waiting for transfers between devices: 7.85 us -> 5.17 us  [move(): lax.ppermute(x, 'seq', [(i, target) for i, target in enumerate(targets) i...]
    pallas_call x1 -> x2, Pallas kernels: 1.23 us -> 1.49 us  [the longest x1 1.02 us: body(): call(join, bf16((row_dev, width)), [VMEM] * 3, heads=heads)]
  transfers between devices with their start and end apart: 7 -> 7, of which waited for: 3 -> 2; matrix products, arithmetic and copies ran while one was open for 0% -> 0% of each run, Pallas kernels for 21% -> 29%
where the time goes in v6:
time: 33.3 us; the launch traced here: 33 us
  Pallas kernels  14.4 us (43%)
  starting transfers between devices  13.4 us (40%)
  waiting for transfers between devices  5.17 us (16%)
    ppermute x7, starting transfers between devices, move(): lax.ppermute(x, 'seq', [(i, target) for i, target in enumerate(targets) i...  13.4 us
    ppermute x7, waiting for transfers between devices, move(): lax.ppermute(x, 'seq', [(i, target) for i, target in enumerate(targets) i...  5.17 us
    pallas_call x1, Pallas kernels, body(): call(branch, [payload, bf16((slots, width)), bf16((slots, 3 * HEAD_DIM)),...  3.65 us
    pallas_call x2, Pallas kernels, body(): call(root_load, result + [bf16(branch_keys.shape)], [VMEM] * 3 + [HBM], [...  3.25 us
    pallas_call x1, Pallas kernels, body(): call(share, payload, [VMEM] * 6, [scores], key=keys[0], kv_local=kv_local)  1.94 us
    pallas_call x1, Pallas kernels, body(): call(share, payload, [VMEM] * 6, [scores], key=back[last], kv_local=kv_lo...  1.94 us
    pallas_call x1, Pallas kernels, body(): call(own, [bf16(x.shape) for x in (root_keys, root_values)] + [bf16((bran...  1.59 us
    pallas_call x1, Pallas kernels, body(): call(join, bf16((row_dev, width)), [VMEM] * 3, heads=heads)  1.02 us
  transfers between devices with their start and end apart: 7, of which 2 were waited for; matrix products, arithmetic and copies ran while one was open for 0% of the time, Pallas kernels for 29%

profile of v6, /device:TPU:0, one launch (start us, length us, event | category | flops | bytes accessed | tf_op | source)
XLA Modules:
  0.0 33.0 jit_solution(547155087483273224)
XLA Ops:
  0.0 4.1 %collective-permute-start = (bf16[32,2048]{1,0:T(8,128)(2,1)}, bf16[32,2048]{1,0:T(8,128)(2,1)S(1)}, u32[]{:S(2)}, u32[]{:S(2)}) collective-permute-start(bf16[32,2048]{1,0:T(8,128)(2,1)} %q_ref.1), channel_id=1, source_target_pairs={{0,8},{4,0},{8,12},{12,4},{1,9},{5,1},{9,13},{13,5},{2,10},{6,2},{... | collective-permute-start | bytes 393224 | tf_op jit(solution)/shard_map/ppermute | solution.py:312
  4.1 0.0 collective-permute-start.1
  4.1 1.6 %collective-permute-start.2 = (bf16[32,2048]{1,0:T(8,128)(2,1)}, bf16[32,2048]{1,0:T(8,128)(2,1)S(1)}, u32[]{:S(2)}, u32[]{:S(2)}) collective-permute-start(bf16[32,2048]{1,0:T(8,128)(2,1)} %q_ref.1), channel_id=1, source_target_pairs={{0,0},{4,8},{8,4},{12,12},{1,1},{5,9},{9,5},{13,13},{2,2},{6,10},{... | collective-permute-start | bytes 393224 | tf_op jit(solution)/shard_map/ppermute | solution.py:312
  5.6 2.6 %collective-permute-done.q_ref.rest_1_ = bf16[32,2048]{1,0:T(8,128)(2,1)S(1)} collective-permute-done((bf16[32,2048]{1,0:T(8,128)(2,1)}, bf16[32,2048]{1,0:T(8,128)(2,1)S(1)}, u32[]{:S(2)}, u32[]{:S(2)}) %collective-permute-start) | collective-permute-done | bytes 131104 | tf_op jit(solution)/shard_map/ppermute | solution.py:312
  8.3 2.3 %collective-permute-start.3 = (bf16[32,2048]{1,0:T(8,128)(2,1)S(1)}, bf16[32,2048]{1,0:T(8,128)(2,1)S(1)}, u32[]{:S(2)}, u32[]{:S(2)}) collective-permute-start(bf16[32,2048]{1,0:T(8,128)(2,1)S(1)} %collective-permute-done.q_ref.rest_1_), channel_id=1, source_target_pairs={{0,4},{4,0},{8,12},{12,8},{1,5},{5,1},{9,13},{13,9},{2,6},{6,2},{1... | collective-permute-start | bytes 393224 | tf_op jit(solution)/shard_map/ppermute | solution.py:312
  10.5 1.6 %shard_map.73 = (bf16[2048,256]{1,0:T(8,128)(2,1)S(1)}, bf16[2048,256]{1,0:T(8,128)(2,1)S(1)}, bf16[2,128,32]{2,1,0:T(8,128)(2,1)S(1)}, f32[2,2048]{1,0:T(2,128)S(1)}) custom-call(s32[8]{0:T(128)} %doc_hbm.1, s32[1,128]{1,0:T(1,128)} %bitcast.1, bf16[2048,256]{1,0:T(8,128)(2,1)} %rk_hbm.1, bf16[2048,256]{1,0:T(8,128)(2,1)} %rv_hbm.1), custom_call_target="tpu_custom_call" | custom-call | tf_op jit(solution)/shard_map/pallas_call | solution.py:324
  12.1 1.6 %shard_map.74 = (f32[2,256,128]{2,1,0:T(8,128)S(1)}, f32[32,128]{1,0:T(8,128)S(1)}, bf16[2,2048,256]{2,1,0:T(8,128)(2,1)S(1)}) custom-call(bf16[32,2048]{1,0:T(8,128)(2,1)S(1)} %collective-permute-done.q_ref.rest_1_, bf16[2048,256]{1,0:T(8,128)(2,1)S(1)} %get-tuple-element.23.rk_ref, bf16[2048,256]{1,0:T(8,128)(2,1)S(1)} %get-tuple-element.24.rv_ref, ...), custom_call_target="tpu_custom_call" | custom-call | tf_op jit(solution)/shard_map/pallas_call | solution.py:333
  13.7 0.0 copy-start
  13.8 0.0 collective-permute-done.1.q_ref.rest_2_
  13.8 1.6 %shard_map.75 = (f32[2,256,128]{2,1,0:T(8,128)S(1)}, f32[32,128]{1,0:T(8,128)S(1)}, bf16[2,2048,256]{2,1,0:T(8,128)(2,1)S(1)}) custom-call(bf16[32,2048]{1,0:T(8,128)(2,1)S(1)} %collective-permute-done.1.q_ref.rest_2_, bf16[2048,256]{1,0:T(8,128)(2,1)S(1)} %get-tuple-element.23.rk_ref, bf16[2048,256]{1,0:T(8,128)(2,1)S(1)} %get-tuple-element.24.rv_ref, ...), custom_call_target="tpu_custom_call" | custom-call | tf_op jit(solution)/shard_map/pallas_call | solution.py:333
  15.4 0.0 collective-permute-done.2.rest_3_
  15.4 0.0 collective-permute-done.3.rest_4_
  15.4 3.6 %shard_map.76 = (bf16[528,128]{1,0:T(8,128)(2,1)S(1)}, bf16[64,2048]{1,0:T(8,128)(2,1)S(1)}, bf16[64,384]{1,0:T(8,128)(2,1)S(1)}, bf16[32,2048]{1,0:T(8,128)(2,1)S(1)}) custom-call(bf16[2,128,32]{2,1,0:T(8,128)(2,1)S(1)} %get-tuple-element.21.pick_ref, f32[2,2048]{1,0:T(2,128)S(1)} %get-tuple-element.22.bias_ref, ...), custom_call_target="tpu_custom_call" | custom-call | tf_op jit(solution)/shard_map/pallas_call | solution.py:342
  19.1 0.1 collective-permute-start.4
  19.2 0.5 %shard_map.78 = bf16[528,128]{1,0:T(8,128)(2,1)S(1)} custom-call(bf16[2,128,32]{2,1,0:T(8,128)(2,1)S(1)} %get-tuple-element.21.pick_ref, bf16[64,384]{1,0:T(8,128)(2,1)S(1)} %get-tuple-element.29.b_level_ref, f32[2,256,128]{2,1,0:T(8,128)S(1)} %get-tuple-element.32.out_ref, f32[32,128]{1,0:T(8,128)S(1)} %get-tuple-element.33.level_ref, ...), custom_call_target="tpu_custom_call" | custom-call | tf_op jit(solution)/shard_map/pallas_call | solution.py:353
  19.7 2.9 %collective-permute-start.5 = (bf16[528,128]{1,0:T(8,128)(2,1)S(1)}, bf16[528,128]{1,0:T(8,128)(2,1)S(1)}, u32[]{:S(2)}, u32[]{:S(2)}) collective-permute-start(bf16[528,128]{1,0:T(8,128)(2,1)S(1)} %shard_map.78), channel_id=1, source_target_pairs={{0,8},{4,0},{8,12},{12,4},{1,9},{5,1},{9,13},{13,5},{2,10},{6,2},{... | collective-permute-start | bytes 405512 | tf_op jit(solution)/shard_map/ppermute | solution.py:312
  22.6 1.9 %shard_map.80 = bf16[528,128]{1,0:T(8,128)(2,1)S(1)} custom-call(bf16[2,128,32]{2,1,0:T(8,128)(2,1)S(1)} %get-tuple-element.21.pick_ref, bf16[64,384]{1,0:T(8,128)(2,1)S(1)} %get-tuple-element.29.b_level_ref, bf16[2048,256]{1,0:T(8,128)(2,1)S(1)} %get-tuple-element.23.rk_ref, bf16[2048,256]{1,0:T(8,128)(2,1)S(1)} %get-tuple-element.24.rv_ref, ...), custom_call_target="tpu_custom_call" | custom-call | tf_op jit(solution)/shard_map/pallas_call | solution.py:354
  24.6 2.5 %collective-permute-start.6 = (bf16[528,128]{1,0:T(8,128)(2,1)S(1)}, bf16[528,128]{1,0:T(8,128)(2,1)S(1)}, u32[]{:S(2)}, u32[]{:S(2)}) collective-permute-start(bf16[528,128]{1,0:T(8,128)(2,1)S(1)} %shard_map.80), channel_id=1, source_target_pairs={{0,12},{4,8},{8,4},{12,0},{1,13},{5,9},{9,5},{13,1},{2,14},{6,10},... | collective-permute-start | bytes 405512 | tf_op jit(solution)/shard_map/ppermute | solution.py:312
  27.1 1.9 %shard_map.77.refs_0_ = bf16[528,128]{1,0:T(8,128)(2,1)S(1)} custom-call(bf16[2,128,32]{2,1,0:T(8,128)(2,1)S(1)} %get-tuple-element.21.pick_ref, bf16[64,384]{1,0:T(8,128)(2,1)S(1)} %get-tuple-element.29.b_level_ref, bf16[2048,256]{1,0:T(8,128)(2,1)S(1)} %get-tuple-element.23.rk_ref, bf16[2048,256]{1,0:T(8,128)(2,1)S(1)} %get-tuple-element.24.rv_ref, ...), custom_call_target="tpu_custom_call" | custom-call | tf_op jit(solution)/shard_map/pallas_call | solution.py:355
  29.0 2.5 %collective-permute-done.4.refs_1_ = bf16[528,128]{1,0:T(8,128)(2,1)S(1)} collective-permute-done((bf16[528,128]{1,0:T(8,128)(2,1)S(1)}, bf16[528,128]{1,0:T(8,128)(2,1)S(1)}, u32[]{:S(2)}, u32[]{:S(2)}) %collective-permute-start.4) | collective-permute-done | bytes 135200 | tf_op jit(solution)/shard_map/ppermute | solution.py:312
  31.5 0.0 collective-permute-done.5.refs_2_
  31.5 0.5 %shard_map.79 = (f32[512,128]{1,0:T(8,128)S(1)}, f32[16,128]{1,0:T(8,128)S(1)}) custom-call(bf16[528,128]{1,0:T(8,128)(2,1)S(1)} %shard_map.77.refs_0_, bf16[528,128]{1,0:T(8,128)(2,1)S(1)} %collective-permute-done.4.refs_1_, bf16[528,128]{1,0:T(8,128)(2,1)S(1)} %collective-permute-done.5.refs_2_), custom_call_target="tpu_custom_call" | custom-call | tf_op jit(solution)/shard_map/pallas_call | solution.py:358
  32.0 0.0 collective-permute-done.6.share_ref
  32.0 1.0 %shard_map.81 = bf16[32,2048]{1,0:T(8,128)(2,1)} custom-call(f32[512,128]{1,0:T(8,128)S(1)} %get-tuple-element.34.sum_ref, f32[16,128]{1,0:T(8,128)S(1)} %get-tuple-element.35.level_ref, bf16[528,128]{1,0:T(8,128)(2,1)S(1)} %collective-permute-done.6.share_ref), custom_call_target="tpu_custom_call" | custom-call | tf_op jit(solution)/shard_map/pallas_call | solution.py:359
  (1 shorter events, 0.0 us)
Async XLA Ops:
  0.0 8.3 %collective-permute-start = (bf16[32,2048]{1,0:T(8,128)(2,1)}, bf16[32,2048]{1,0:T(8,128)(2,1)S(1)}, u32[]{:S(2)}, u32[]{:S(2)}) collective-permute-start(bf16[32,2048]{1,0:T(8,128)(2,1)} %q_ref.1), channel_id=1, source_target_pairs={{0,8},{4,0},{8,12},{12,4},{1,9},{5,1},{9,13},{13,5},{2,10},{6,2},{... | collective-permute-start | bytes 393224 | tf_op jit(solution)/shard_map/ppermute | solution.py:312
  4.1 9.7 %collective-permute-start.1 = (bf16[32,2048]{1,0:T(8,128)(2,1)}, bf16[32,2048]{1,0:T(8,128)(2,1)S(1)}, u32[]{:S(2)}, u32[]{:S(2)}) collective-permute-start(bf16[32,2048]{1,0:T(8,128)(2,1)} %q_ref.1), channel_id=1, source_target_pairs={{0,4},{4,12},{8,0},{12,8},{1,5},{5,13},{9,1},{13,9},{2,6},{6,14},{... | collective-permute-start | bytes 393224 | tf_op jit(solution)/shard_map/ppermute | solution.py:312
  4.1 11.3 %collective-permute-start.2 = (bf16[32,2048]{1,0:T(8,128)(2,1)}, bf16[32,2048]{1,0:T(8,128)(2,1)S(1)}, u32[]{:S(2)}, u32[]{:S(2)}) collective-permute-start(bf16[32,2048]{1,0:T(8,128)(2,1)} %q_ref.1), channel_id=1, source_target_pairs={{0,0},{4,8},{8,4},{12,12},{1,1},{5,9},{9,5},{13,13},{2,2},{6,10},{... | collective-permute-start | bytes 393224 | tf_op jit(solution)/shard_map/ppermute | solution.py:312
  8.3 7.2 %collective-permute-start.3 = (bf16[32,2048]{1,0:T(8,128)(2,1)S(1)}, bf16[32,2048]{1,0:T(8,128)(2,1)S(1)}, u32[]{:S(2)}, u32[]{:S(2)}) collective-permute-start(bf16[32,2048]{1,0:T(8,128)(2,1)S(1)} %collective-permute-done.q_ref.rest_1_), channel_id=1, source_target_pairs={{0,4},{4,0},{8,12},{12,8},{1,5},{5,1},{9,13},{13,9},{2,6},{6,2},{1... | collective-permute-start | bytes 393224 | tf_op jit(solution)/shard_map/ppermute | solution.py:312
  13.7 1.7 %copy-start = (bf16[32,2048]{1,0:T(8,128)(2,1)S(1)}, bf16[32,2048]{1,0:T(8,128)(2,1)}, u32[]{:S(2)}) copy-start(bf16[32,2048]{1,0:T(8,128)(2,1)} %q_ref.1) | copy-start | bytes 393220
  19.1 12.4 %collective-permute-start.4 = (bf16[528,128]{1,0:T(8,128)(2,1)S(1)}, bf16[528,128]{1,0:T(8,128)(2,1)S(1)}, u32[]{:S(2)}, u32[]{:S(2)}) collective-permute-start(bf16[528,128]{1,0:T(8,128)(2,1)S(1)} %get-tuple-element.31), channel_id=1, source_target_pairs={{0,4},{4,12},{8,0},{12,8},{1,5},{5,13},{9,1},{13,9},{2,6},{6,14},{... | collective-permute-start | bytes 405512 | tf_op jit(solution)/shard_map/ppermute | solution.py:312
  19.7 11.8 %collective-permute-start.5 = (bf16[528,128]{1,0:T(8,128)(2,1)S(1)}, bf16[528,128]{1,0:T(8,128)(2,1)S(1)}, u32[]{:S(2)}, u32[]{:S(2)}) collective-permute-start(bf16[528,128]{1,0:T(8,128)(2,1)S(1)} %shard_map.78), channel_id=1, source_target_pairs={{0,8},{4,0},{8,12},{12,4},{1,9},{5,1},{9,13},{13,5},{2,10},{6,2},{... | collective-permute-start | bytes 405512 | tf_op jit(solution)/shard_map/ppermute | solution.py:312
  24.6 7.4 %collective-permute-start.6 = (bf16[528,128]{1,0:T(8,128)(2,1)S(1)}, bf16[528,128]{1,0:T(8,128)(2,1)S(1)}, u32[]{:S(2)}, u32[]{:S(2)}) collective-permute-start(bf16[528,128]{1,0:T(8,128)(2,1)S(1)} %shard_map.80), channel_id=1, source_target_pairs={{0,12},{4,8},{8,4},{12,0},{1,13},{5,9},{9,5},{13,1},{2,14},{6,10},... | collective-permute-start | bytes 405512 | tf_op jit(solution)/shard_map/ppermute | solution.py:312

commit v7 on v6

--- a/solution.py
+++ b/solution.py
@@ -159,24 +159,38 @@
     return [pick_ref[b, at, :] for b in range(pick_ref.shape[0])]
 
 
-def merge(share_ref, pick, outputs, level, branch_ref, b_level):
+def merge_head(share_ref, pick, has, f, output, level, branch_ref, b_level):
     row_dev = level.shape[0]
-    heads = len(outputs) * GROUP
-    pick = jnp.concatenate(pick, axis=1)
-    has = jnp.sum(pick.astype(jnp.float32), axis=1, keepdims=True) > 0.0
     found = dot(pick, b_level)
     b_level = jnp.where(has, found[:, :HEAD_DIM] + found[:, HEAD_DIM:2 * HEAD_DIM] + found[:, 2 * HEAD_DIM:], LOW)
     top = jnp.maximum(level, b_level)
     ours, theirs = jnp.exp2(level - top), jnp.exp2(b_level - top)
     both = ours + theirs
     ours, theirs = ours / both, theirs / both
-    b_out = dot(pick, branch_ref[...])
-    for f, output in enumerate(outputs):
-        for g in range(GROUP):
-            h = f * GROUP + g
-            ahead = output[g * row_dev:(g + 1) * row_dev, :] * spread(ours, h, row_dev)
-            share_ref[h * row_dev:(h + 1) * row_dev, :] = (ahead + b_out[:, h * HEAD_DIM:(h + 1) * HEAD_DIM] * spread(theirs, h, row_dev)).astype(jnp.bfloat16)
-    write_level(share_ref, top + jnp.log2(both), heads)
+    b_out = dot(pick, branch_ref[:, f * GROUP * HEAD_DIM:(f + 1) * GROUP * HEAD_DIM])
+    for g in range(GROUP):
+        h = f * GROUP + g
+        ahead = output[g * row_dev:(g + 1) * row_dev, :] * spread(ours, h, row_dev)
+        share_ref[h * row_dev:(h + 1) * row_dev, :] = (ahead + b_out[:, g * HEAD_DIM:(g + 1) * HEAD_DIM] * spread(theirs, h, row_dev)).astype(jnp.bfloat16)
+    return top + jnp.log2(both)
+
+
+def named_rows(pick):
+    pick = jnp.concatenate(pick, axis=1)
+    return pick, jnp.sum(pick.astype(jnp.float32), axis=1, keepdims=True) > 0.0
+
+
+def write_levels(share_ref, levels):
+    lane = lax.broadcasted_iota(jnp.int32, levels[0].shape, 1)
+    level = levels[0]
+    for f in range(1, len(levels)):
+        level = jnp.where(lane >= f * GROUP, levels[f], level)
+    write_level(share_ref, level, len(levels) * GROUP)
+
+
+def merge(share_ref, pick, outputs, level, branch_ref, b_level):
+    pick, has = named_rows(pick)
+    write_levels(share_ref, [merge_head(share_ref, pick, has, f, output, level, branch_ref, b_level) for f, output in enumerate(outputs)])
 
 
 def write_level(share_ref, level, heads):
@@ -224,10 +238,16 @@
 
 
 def share(pick_ref, b_level_ref, rk_ref, rv_ref, branch_ref, q_ref, share_ref, score_ref, *, key, kv_local):
+    pick, has = named_rows(picks(pick_ref, key, q_ref.shape[0]))
+    joined = []
+
     def finish(outputs, level):
-        merge(share_ref, picks(pick_ref, key, level.shape[0]), list(outputs.values()), level, branch_ref, b_level_ref[...])
-
-    pipeline(roots(lambda f: stack_heads(q_ref, f * GROUP), rk_ref, rv_ref, range(kv_local), finish), score_ref)
+        for f, output in outputs.items():
+            joined.append(merge_head(share_ref, pick, has, f, output, level, branch_ref, b_level_ref[...]))
+
+    blocks = [roots(lambda f: stack_heads(q_ref, f * GROUP), rk_ref, rv_ref, [f], finish)[0] for f in range(kv_local)]
+    pipeline(blocks, score_ref)
+    write_levels(share_ref, joined)
 
 
 def given(pick_ref, b_level_ref, out_ref, level_ref, branch_ref, share_ref, *, key):

time: 33.3 us -> 33.3 us (level)
  no operation moved by 1% of the time
where the time goes in v7:
time: 33.3 us; the launch traced here: 33.1 us
  Pallas kernels  14.3 us (43%)
  starting transfers between devices  13.4 us (40%)
  waiting for transfers between devices  5.23 us (16%)
    ppermute x7, starting transfers between devices, move(): lax.ppermute(x, 'seq', [(i, target) for i, target in enumerate(targets) i...  13.4 us
    ppermute x7, waiting for transfers between devices, move(): lax.ppermute(x, 'seq', [(i, target) for i, target in enumerate(targets) i...  5.23 us
    pallas_call x1, Pallas kernels, body(): call(branch, [payload, bf16((slots, width)), bf16((slots, 3 * HEAD_DIM)),...  3.65 us
    pallas_call x2, Pallas kernels, body(): call(root_load, result + [bf16(branch_keys.shape)], [VMEM] * 3 + [HBM], [...  3.25 us
    pallas_call x1, Pallas kernels, body(): call(share, payload, [VMEM] * 6, [scores], key=keys[0], kv_local=kv_local)  1.92 us
    pallas_call x1, Pallas kernels, body(): call(share, payload, [VMEM] * 6, [scores], key=back[last], kv_local=kv_lo...  1.92 us
    pallas_call x1, Pallas kernels, body(): call(own, [bf16(x.shape) for x in (root_keys, root_values)] + [bf16((bran...  1.59 us
    pallas_call x1, Pallas kernels, body(): call(join, bf16((row_dev, width)), [VMEM] * 3, heads=heads)  1.02 us
  transfers between devices with their start and end apart: 7, of which 2 were waited for; matrix products, arithmetic and copies ran while one was open for 0% of the time, Pallas kernels for 29%

profile of v7, /device:TPU:0, one launch (start us, length us, event | category | flops | bytes accessed | tf_op | source)
XLA Modules:
  0.0 33.1 jit_solution(7059078708858480475)
XLA Ops:
  0.0 4.1 %collective-permute-start = (bf16[32,2048]{1,0:T(8,128)(2,1)}, bf16[32,2048]{1,0:T(8,128)(2,1)S(1)}, u32[]{:S(2)}, u32[]{:S(2)}) collective-permute-start(bf16[32,2048]{1,0:T(8,128)(2,1)} %q_ref.1), channel_id=1, source_target_pairs={{0,8},{4,0},{8,12},{12,4},{1,9},{5,1},{9,13},{13,5},{2,10},{6,2},{... | collective-permute-start | bytes 393224 | tf_op jit(solution)/shard_map/ppermute | solution.py:332
  4.1 0.0 collective-permute-start.1
  4.1 1.6 %collective-permute-start.2 = (bf16[32,2048]{1,0:T(8,128)(2,1)}, bf16[32,2048]{1,0:T(8,128)(2,1)S(1)}, u32[]{:S(2)}, u32[]{:S(2)}) collective-permute-start(bf16[32,2048]{1,0:T(8,128)(2,1)} %q_ref.1), channel_id=1, source_target_pairs={{0,0},{4,8},{8,4},{12,12},{1,1},{5,9},{9,5},{13,13},{2,2},{6,10},{... | collective-permute-start | bytes 393224 | tf_op jit(solution)/shard_map/ppermute | solution.py:332
  5.6 2.6 %collective-permute-done.q_ref.rest_1_ = bf16[32,2048]{1,0:T(8,128)(2,1)S(1)} collective-permute-done((bf16[32,2048]{1,0:T(8,128)(2,1)}, bf16[32,2048]{1,0:T(8,128)(2,1)S(1)}, u32[]{:S(2)}, u32[]{:S(2)}) %collective-permute-start) | collective-permute-done | bytes 131104 | tf_op jit(solution)/shard_map/ppermute | solution.py:332
  8.3 2.3 %collective-permute-start.3 = (bf16[32,2048]{1,0:T(8,128)(2,1)S(1)}, bf16[32,2048]{1,0:T(8,128)(2,1)S(1)}, u32[]{:S(2)}, u32[]{:S(2)}) collective-permute-start(bf16[32,2048]{1,0:T(8,128)(2,1)S(1)} %collective-permute-done.q_ref.rest_1_), channel_id=1, source_target_pairs={{0,4},{4,0},{8,12},{12,8},{1,5},{5,1},{9,13},{13,9},{2,6},{6,2},{1... | collective-permute-start | bytes 393224 | tf_op jit(solution)/shard_map/ppermute | solution.py:332
  10.5 1.6 %shard_map.73 = (bf16[2048,256]{1,0:T(8,128)(2,1)S(1)}, bf16[2048,256]{1,0:T(8,128)(2,1)S(1)}, bf16[2,128,32]{2,1,0:T(8,128)(2,1)S(1)}, f32[2,2048]{1,0:T(2,128)S(1)}) custom-call(s32[8]{0:T(128)} %doc_hbm.1, s32[1,128]{1,0:T(1,128)} %bitcast.1, bf16[2048,256]{1,0:T(8,128)(2,1)} %rk_hbm.1, bf16[2048,256]{1,0:T(8,128)(2,1)} %rv_hbm.1), custom_call_target="tpu_custom_call" | custom-call | tf_op jit(solution)/shard_map/pallas_call | solution.py:344
  12.1 1.6 %shard_map.74 = (f32[2,256,128]{2,1,0:T(8,128)S(1)}, f32[32,128]{1,0:T(8,128)S(1)}, bf16[2,2048,256]{2,1,0:T(8,128)(2,1)S(1)}) custom-call(bf16[32,2048]{1,0:T(8,128)(2,1)S(1)} %collective-permute-done.q_ref.rest_1_, bf16[2048,256]{1,0:T(8,128)(2,1)S(1)} %get-tuple-element.23.rk_ref, bf16[2048,256]{1,0:T(8,128)(2,1)S(1)} %get-tuple-element.24.rv_ref, ...), custom_call_target="tpu_custom_call" | custom-call | tf_op jit(solution)/shard_map/pallas_call | solution.py:353
  13.7 0.0 copy-start
  13.8 0.0 collective-permute-done.1.q_ref.rest_2_
  13.8 1.6 %shard_map.75 = (f32[2,256,128]{2,1,0:T(8,128)S(1)}, f32[32,128]{1,0:T(8,128)S(1)}, bf16[2,2048,256]{2,1,0:T(8,128)(2,1)S(1)}) custom-call(bf16[32,2048]{1,0:T(8,128)(2,1)S(1)} %collective-permute-done.1.q_ref.rest_2_, bf16[2048,256]{1,0:T(8,128)(2,1)S(1)} %get-tuple-element.23.rk_ref, bf16[2048,256]{1,0:T(8,128)(2,1)S(1)} %get-tuple-element.24.rv_ref, ...), custom_call_target="tpu_custom_call" | custom-call | tf_op jit(solution)/shard_map/pallas_call | solution.py:353
  15.4 0.0 collective-permute-done.2.rest_3_
  15.4 0.0 collective-permute-done.3.rest_4_
  15.4 3.6 %shard_map.76 = (bf16[528,128]{1,0:T(8,128)(2,1)S(1)}, bf16[64,2048]{1,0:T(8,128)(2,1)S(1)}, bf16[64,384]{1,0:T(8,128)(2,1)S(1)}, bf16[32,2048]{1,0:T(8,128)(2,1)S(1)}) custom-call(bf16[2,128,32]{2,1,0:T(8,128)(2,1)S(1)} %get-tuple-element.21.pick_ref, f32[2,2048]{1,0:T(2,128)S(1)} %get-tuple-element.22.bias_ref, ...), custom_call_target="tpu_custom_call" | custom-call | tf_op jit(solution)/shard_map/pallas_call | solution.py:362
  19.1 0.1 collective-permute-start.4
  19.2 0.5 %shard_map.78 = bf16[528,128]{1,0:T(8,128)(2,1)S(1)} custom-call(bf16[2,128,32]{2,1,0:T(8,128)(2,1)S(1)} %get-tuple-element.21.pick_ref, bf16[64,384]{1,0:T(8,128)(2,1)S(1)} %get-tuple-element.29.b_level_ref, f32[2,256,128]{2,1,0:T(8,128)S(1)} %get-tuple-element.32.out_ref, f32[32,128]{1,0:T(8,128)S(1)} %get-tuple-element.33.level_ref, ...), custom_call_target="tpu_custom_call" | custom-call | tf_op jit(solution)/shard_map/pallas_call | solution.py:373
  19.7 2.9 %collective-permute-start.5 = (bf16[528,128]{1,0:T(8,128)(2,1)S(1)}, bf16[528,128]{1,0:T(8,128)(2,1)S(1)}, u32[]{:S(2)}, u32[]{:S(2)}) collective-permute-start(bf16[528,128]{1,0:T(8,128)(2,1)S(1)} %shard_map.78), channel_id=1, source_target_pairs={{0,8},{4,0},{8,12},{12,4},{1,9},{5,1},{9,13},{13,5},{2,10},{6,2},{... | collective-permute-start | bytes 405512 | tf_op jit(solution)/shard_map/ppermute | solution.py:332
  22.6 1.9 %shard_map.80 = bf16[528,128]{1,0:T(8,128)(2,1)S(1)} custom-call(bf16[2,128,32]{2,1,0:T(8,128)(2,1)S(1)} %get-tuple-element.21.pick_ref, bf16[64,384]{1,0:T(8,128)(2,1)S(1)} %get-tuple-element.29.b_level_ref, bf16[2048,256]{1,0:T(8,128)(2,1)S(1)} %get-tuple-element.23.rk_ref, bf16[2048,256]{1,0:T(8,128)(2,1)S(1)} %get-tuple-element.24.rv_ref, ...), custom_call_target="tpu_custom_call" | custom-call | tf_op jit(solution)/shard_map/pallas_call | solution.py:374
  24.5 2.5 %collective-permute-start.6 = (bf16[528,128]{1,0:T(8,128)(2,1)S(1)}, bf16[528,128]{1,0:T(8,128)(2,1)S(1)}, u32[]{:S(2)}, u32[]{:S(2)}) collective-permute-start(bf16[528,128]{1,0:T(8,128)(2,1)S(1)} %shard_map.80), channel_id=1, source_target_pairs={{0,12},{4,8},{8,4},{12,0},{1,13},{5,9},{9,5},{13,1},{2,14},{6,10},... | collective-permute-start | bytes 405512 | tf_op jit(solution)/shard_map/ppermute | solution.py:332
  27.1 1.9 %shard_map.77.refs_0_ = bf16[528,128]{1,0:T(8,128)(2,1)S(1)} custom-call(bf16[2,128,32]{2,1,0:T(8,128)(2,1)S(1)} %get-tuple-element.21.pick_ref, bf16[64,384]{1,0:T(8,128)(2,1)S(1)} %get-tuple-element.29.b_level_ref, bf16[2048,256]{1,0:T(8,128)(2,1)S(1)} %get-tuple-element.23.rk_ref, bf16[2048,256]{1,0:T(8,128)(2,1)S(1)} %get-tuple-element.24.rv_ref, ...), custom_call_target="tpu_custom_call" | custom-call | tf_op jit(solution)/shard_map/pallas_call | solution.py:375
  29.0 2.6 %collective-permute-done.4.refs_1_ = bf16[528,128]{1,0:T(8,128)(2,1)S(1)} collective-permute-done((bf16[528,128]{1,0:T(8,128)(2,1)S(1)}, bf16[528,128]{1,0:T(8,128)(2,1)S(1)}, u32[]{:S(2)}, u32[]{:S(2)}) %collective-permute-start.4) | collective-permute-done | bytes 135200 | tf_op jit(solution)/shard_map/ppermute | solution.py:332
  31.6 0.0 collective-permute-done.5.refs_2_
  31.6 0.5 %shard_map.79 = (f32[512,128]{1,0:T(8,128)S(1)}, f32[16,128]{1,0:T(8,128)S(1)}) custom-call(bf16[528,128]{1,0:T(8,128)(2,1)S(1)} %shard_map.77.refs_0_, bf16[528,128]{1,0:T(8,128)(2,1)S(1)} %collective-permute-done.4.refs_1_, bf16[528,128]{1,0:T(8,128)(2,1)S(1)} %collective-permute-done.5.refs_2_), custom_call_target="tpu_custom_call" | custom-call | tf_op jit(solution)/shard_map/pallas_call | solution.py:378
  32.0 0.0 collective-permute-done.6.share_ref
  32.0 1.0 %shard_map.81 = bf16[32,2048]{1,0:T(8,128)(2,1)} custom-call(f32[512,128]{1,0:T(8,128)S(1)} %get-tuple-element.34.sum_ref, f32[16,128]{1,0:T(8,128)S(1)} %get-tuple-element.35.level_ref, bf16[528,128]{1,0:T(8,128)(2,1)S(1)} %collective-permute-done.6.share_ref), custom_call_target="tpu_custom_call" | custom-call | tf_op jit(solution)/shard_map/pallas_call | solution.py:379
  (1 shorter events, 0.0 us)
Async XLA Ops:
  0.0 8.3 %collective-permute-start = (bf16[32,2048]{1,0:T(8,128)(2,1)}, bf16[32,2048]{1,0:T(8,128)(2,1)S(1)}, u32[]{:S(2)}, u32[]{:S(2)}) collective-permute-start(bf16[32,2048]{1,0:T(8,128)(2,1)} %q_ref.1), channel_id=1, source_target_pairs={{0,8},{4,0},{8,12},{12,4},{1,9},{5,1},{9,13},{13,5},{2,10},{6,2},{... | collective-permute-start | bytes 393224 | tf_op jit(solution)/shard_map/ppermute | solution.py:332
  4.1 9.7 %collective-permute-start.1 = (bf16[32,2048]{1,0:T(8,128)(2,1)}, bf16[32,2048]{1,0:T(8,128)(2,1)S(1)}, u32[]{:S(2)}, u32[]{:S(2)}) collective-permute-start(bf16[32,2048]{1,0:T(8,128)(2,1)} %q_ref.1), channel_id=1, source_target_pairs={{0,4},{4,12},{8,0},{12,8},{1,5},{5,13},{9,1},{13,9},{2,6},{6,14},{... | collective-permute-start | bytes 393224 | tf_op jit(solution)/shard_map/ppermute | solution.py:332
  4.1 11.3 %collective-permute-start.2 = (bf16[32,2048]{1,0:T(8,128)(2,1)}, bf16[32,2048]{1,0:T(8,128)(2,1)S(1)}, u32[]{:S(2)}, u32[]{:S(2)}) collective-permute-start(bf16[32,2048]{1,0:T(8,128)(2,1)} %q_ref.1), channel_id=1, source_target_pairs={{0,0},{4,8},{8,4},{12,12},{1,1},{5,9},{9,5},{13,13},{2,2},{6,10},{... | collective-permute-start | bytes 393224 | tf_op jit(solution)/shard_map/ppermute | solution.py:332
  8.3 7.2 %collective-permute-start.3 = (bf16[32,2048]{1,0:T(8,128)(2,1)S(1)}, bf16[32,2048]{1,0:T(8,128)(2,1)S(1)}, u32[]{:S(2)}, u32[]{:S(2)}) collective-permute-start(bf16[32,2048]{1,0:T(8,128)(2,1)S(1)} %collective-permute-done.q_ref.rest_1_), channel_id=1, source_target_pairs={{0,4},{4,0},{8,12},{12,8},{1,5},{5,1},{9,13},{13,9},{2,6},{6,2},{1... | collective-permute-start | bytes 393224 | tf_op jit(solution)/shard_map/ppermute | solution.py:332
  13.7 1.7 %copy-start = (bf16[32,2048]{1,0:T(8,128)(2,1)S(1)}, bf16[32,2048]{1,0:T(8,128)(2,1)}, u32[]{:S(2)}) copy-start(bf16[32,2048]{1,0:T(8,128)(2,1)} %q_ref.1) | copy-start | bytes 393220
  19.1 12.5 %collective-permute-start.4 = (bf16[528,128]{1,0:T(8,128)(2,1)S(1)}, bf16[528,128]{1,0:T(8,128)(2,1)S(1)}, u32[]{:S(2)}, u32[]{:S(2)}) collective-permute-start(bf16[528,128]{1,0:T(8,128)(2,1)S(1)} %get-tuple-element.31), channel_id=1, source_target_pairs={{0,4},{4,12},{8,0},{12,8},{1,5},{5,13},{9,1},{13,9},{2,6},{6,14},{... | collective-permute-start | bytes 405512 | tf_op jit(solution)/shard_map/ppermute | solution.py:332
  19.7 11.8 %collective-permute-start.5 = (bf16[528,128]{1,0:T(8,128)(2,1)S(1)}, bf16[528,128]{1,0:T(8,128)(2,1)S(1)}, u32[]{:S(2)}, u32[]{:S(2)}) collective-permute-start(bf16[528,128]{1,0:T(8,128)(2,1)S(1)} %shard_map.78), channel_id=1, source_target_pairs={{0,8},{4,0},{8,12},{12,4},{1,9},{5,1},{9,13},{13,5},{2,10},{6,2},{... | collective-permute-start | bytes 405512 | tf_op jit(solution)/shard_map/ppermute | solution.py:332
  24.5 7.5 %collective-permute-start.6 = (bf16[528,128]{1,0:T(8,128)(2,1)S(1)}, bf16[528,128]{1,0:T(8,128)(2,1)S(1)}, u32[]{:S(2)}, u32[]{:S(2)}) collective-permute-start(bf16[528,128]{1,0:T(8,128)(2,1)S(1)} %shard_map.80), channel_id=1, source_target_pairs={{0,12},{4,8},{8,4},{12,0},{1,13},{5,9},{9,5},{13,1},{2,14},{6,10},... | collective-permute-start | bytes 405512 | tf_op jit(solution)/shard_map/ppermute | solution.py:332
